TPU v7x, 32 devices: a whole 2x2x4 slice. The times are simulated.
32 devices in a mesh: gz: 4 (over x, core), gy: 8 (over z, y).
Axes of the slice: x: 2, y: 2, z: 4, core: 2. Of those that a mesh axis runs over, the one named last changes fastest.
Arguments:
- zone_ids: int32 [32, 256, 512], P('gz', 'gy'), may hold values from 0 to 7
- fixed_cells: int32 [32, 256, 512], P('gz', 'gy'), may hold values 0 or 1
- pressure_old: float32 [32, 256, 512], P('gz', 'gy'), may hold values from -6 to 6
- pressure_iter: float32 [32, 256, 512], P('gz', 'gy'), may hold values from -6 to 6
- strain_change: float32 [32, 256, 512], P('gz', 'gy'), may hold values from -3 to 3
- source: float32 [32, 256, 512], P('gz', 'gy'), may hold values from -40 to 40
- zone_perm: float32 [8], replicated, may hold values from 0.2 to 5
- zone_storage: float32 [8], replicated, may hold values from 0.1 to 1
- zone_biot: float32 [8], replicated, may hold values from 0.5 to 1
- zone_bulk: float32 [8], replicated, may hold values from 0.5 to 2
Outputs:
- pressure: float32 [32, 256, 512], P('gz', 'gy')
- strain_next: float32 [32, 256, 512], P('gz', 'gy')
- outer_norms: float32 [2], replicated
All inputs are finite; a program needn't handle non-finite values. No bound on the sum of `fixed_cells` on one device may be relied on, other than what follows from the above.
Results may differ from a plain program's by a relative error of at most 0.00016.
Values sent between devices are 32-bit elements; how exact they have to be, the bound alone decides.
No kernel may reach another device: no remote copies, remote signals or barrier semaphores. Data moves between devices by JAX's collectives and lax.ppermute only.
A program may use at most 64 MiB of HBM per device.

v0:
```python
import jax
import jax.numpy as jnp
from jax import lax
from jax.sharding import PartitionSpec as P

ITERS = 3


def with_halo(cells, sides, width):
    for axis, dim in sides:
        count = lax.axis_size(axis)
        ends = count - 1
        head = lax.slice_in_dim(cells, 0, width, axis=dim)
        tail = lax.slice_in_dim(cells, cells.shape[dim] - width, cells.shape[dim], axis=dim)
        cells = jnp.concatenate(
            [
                lax.ppermute(tail, axis, [(i, (i + 1) % count) for i in range(ends)]),
                cells,
                lax.ppermute(head, axis, [((i + 1) % count, i) for i in range(ends)]),
            ],
            axis=dim,
        )
    return cells


def lookup(zone_ids, zone_table):
    result = jnp.zeros(zone_ids.shape, jnp.float32)
    for zone_index in range(zone_table.shape[0]):
        result = jnp.where(zone_ids == zone_index, zone_table[zone_index], result)
    return result


def harmonic(lower_side, upper_side):
    return 2.0 * lower_side * upper_side / (lower_side + upper_side)


def neighbour_views(values, padded):
    x_padded = jnp.pad(values, ((0, 0), (0, 0), (1, 1)))
    return (
        padded[:-2, 1:-1],
        padded[2:, 1:-1],
        padded[1:-1, :-2],
        padded[1:-1, 2:],
        x_padded[:, :, :-2],
        x_padded[:, :, 2:],
    )


def paired_totals(residual, precond, applied):
    return lax.psum((jnp.sum(residual * precond), jnp.sum(precond * applied)), ("gz", "gy"))


def per_device(
    zone_ids,
    fixed_cells,
    pressure_old,
    pressure_iter,
    strain_change,
    source,
    zone_perm,
    zone_storage,
    zone_biot,
    zone_bulk,
):
    storage = lookup(zone_ids, zone_storage)
    biot_coeff = lookup(zone_ids, zone_biot)
    bulk_modulus = lookup(zone_ids, zone_bulk)
    permeability = lookup(zone_ids, zone_perm)
    coupling = biot_coeff * biot_coeff / bulk_modulus
    perm_padded = with_halo(permeability, (("gz", 0), ("gy", 1)), 1)
    face_terms = tuple(
        (harmonic(permeability, view) for view in neighbour_views(permeability, perm_padded))
    )
    diagonal = storage + coupling
    for face in face_terms:
        diagonal = diagonal + face
    free_cells = 1.0 - fixed_cells.astype(jnp.float32)
    cell_count = zone_ids.size * lax.axis_size("gz") * lax.axis_size("gy")

    def operator(values):
        padded = with_halo(values, (("gz", 0), ("gy", 1)), 1)
        views = neighbour_views(values, padded)
        neighbours = face_terms[0] * views[0]
        for number in range(1, 6):
            neighbours = neighbours + face_terms[number] * views[number]
        return diagonal * values - neighbours

    right_side = (
        storage * pressure_old + coupling * pressure_iter - biot_coeff * strain_change + source
    )
    pressure = pressure_iter
    residual = free_cells * (right_side - operator(pressure_iter))
    precond = residual / diagonal
    applied = free_cells * operator(precond)
    inner_now, curvature = paired_totals(residual, precond, applied)
    step_size = inner_now / curvature
    direction = precond
    direction_image = applied
    for step_index in range(ITERS):
        pressure = pressure + step_size * direction
        residual = residual - step_size * direction_image
        if step_index + 1 < ITERS:
            precond = residual / diagonal
            applied = free_cells * operator(precond)
            inner_next, curvature = paired_totals(residual, precond, applied)
            growth = inner_next / inner_now
            step_size = inner_next / (curvature - growth * inner_next / step_size)
            direction = precond + growth * direction
            direction_image = applied + growth * direction_image
            inner_now = inner_next
    change = biot_coeff / bulk_modulus * (pressure - pressure_iter)
    strain_next = strain_change + change
    closing = free_cells * (right_side - operator(pressure))
    totals = lax.psum((jnp.sum(closing * closing), jnp.sum(change * change)), ("gz", "gy"))
    outer_norms = jnp.sqrt(jnp.stack([totals[0], totals[1]]) / cell_count)
    return (pressure, strain_next, outer_norms)


def solution(mesh):
    return jax.shard_map(
        per_device,
        mesh=mesh,
        in_specs=(
            P("gz", "gy", None),
            P("gz", "gy", None),
            P("gz", "gy", None),
            P("gz", "gy", None),
            P("gz", "gy", None),
            P("gz", "gy", None),
            P(),
            P(),
            P(),
            P(),
        ),
        out_specs=(P("gz", "gy", None), P("gz", "gy", None), P()),
        check_vma=False,
    )
```

profile of v0, /device:TPU:0, one launch (start us, length us, event | category | flops | bytes accessed | tf_op | source)
XLA Modules:
  0.0 324.6 jit_solution(3830446485278654280)
XLA Ops:
  0.6 0.9 fusion.89
  1.5 1.3 collective-permute-start.5
  2.8 3.0 collective-permute-start.4
  6.5 6.7 %select_select_fusion = (f32[8,32,512]{2,1,0:T(8,128)S(1)}, pred[8,32,512]{2,1,0:T(8,128)(4,1)S(1)}, pred[8,32,512]{2,1,0:T(8,128)(4,1)S(1)}, pred[8,32,512]{2,1...) fusion(f32[]{:T(128)} %bitcast.31, f32[]{:T(128)} %bitcast.30, ...), kind=kLoop, calls=%fused_computation.147 | loop fusion | flops 2097152 | bytes 2097184 | tf_op jit(solution)/shard_map/jit(_where)/select_n | solution.py:29
  13.4 4.6 %collective-permute-start = (f32[1,32,512]{2,1,0:T(8,128)S(1)}, f32[1,32,512]{2,1,0:T(8,128)S(1)}, u32[]{:S(2)}, u32[]{:S(2)}) collective-permute-start(f32[1,32,512]{2,1,0:T(8,128)S(1)} %get-tuple-element.57), channel_id=1, source_target_pairs={{0,8},{8,16},{16,24},{1,9},{9,17},{17,25},{2,10},{10,18},{18,26},{... | collective-permute-start | bytes 196616 | tf_op jit(solution)/shard_map/ppermute | solution.py:17
  18.0 1.3 collective-permute-start.1
  20.9 3.6 %collective-permute-start.6 = (f32[10,1,512]{2,1,0:T(1,128)S(1)}, f32[10,1,512]{2,1,0:T(1,128)S(1)}, u32[]{:S(2)}, u32[]{:S(2)}) collective-permute-start(f32[10,1,512]{2,1,0:T(1,128)S(1)} %get-tuple-element.47), channel_id=1, source_target_pairs={{0,1},{1,2},{2,3},{3,4},{4,5},{5,6},{6,7},{8,9},{9,10},{10,11},{11... | collective-permute-start | bytes 61448 | tf_op jit(solution)/shard_map/ppermute | solution.py:17
  24.5 1.3 collective-permute-start.7
  25.8 4.5 %collective-permute-start.2 = (f32[10,1,512]{2,1,0:T(1,128)S(1)}, f32[10,1,512]{2,1,0:T(1,128)S(1)}, u32[]{:S(2)}, u32[]{:S(2)}) collective-permute-start(f32[10,1,512]{2,1,0:T(1,128)S(1)} %get-tuple-element.45), channel_id=1, source_target_pairs={{0,1},{1,2},{2,3},{3,4},{4,5},{5,6},{6,7},{8,9},{9,10},{10,11},{11... | collective-permute-start | bytes 61448 | tf_op jit(solution)/shard_map/ppermute | solution.py:17
  30.4 1.3 collective-permute-start.3
  32.4 4.1 %collective-permute-done.3 = f32[10,1,512]{2,1,0:T(1,128)S(1)} collective-permute-done((f32[10,1,512]{2,1,0:T(1,128)S(1)}, f32[10,1,512]{2,1,0:T(1,128)S(1)}, u32[]{:S(2)}, u32[]{:S(2)}) %collective-permute-start.3) | collective-permute-done | bytes 20512 | tf_op jit(solution)/shard_map/ppermute | solution.py:19
  36.5 18.7 %fusion.81 = (f32[8,32,512]{2,1,0:T(8,128)S(1)}, f32[8,32,512]{2,1,0:T(8,128)S(1)}, f32[8,32,512]{2,1,0:T(8,128)}, f32[8,32,512]{2,1,0:T(8,128)S(1)}, f32[8,32,512]{2,1,0:T(8,128)S(1)}, /*index=5*/f32[8,32,512]{2,1,0:T(8,128)S(1)}) fusion(f32[8,32,512]{2,1,0:T(8,128)S(1)} %copy-done.6, f32[10,1,512]{2,1,0:T(1,128)S(1)} %collective-permute-done.7, ...), kind=kLoop, calls=%fused_computation.184 | loop fusion | flops 11534336 | bytes 8339552 | tf_op jit(solution)/shard_map/div | solution.py:93
  55.3 1.3 collective-permute-start.8
  56.6 1.3 collective-permute-start.9
  57.9 4.8 %collective-permute-done.9 = f32[1,32,512]{2,1,0:T(8,128)S(1)} collective-permute-done((f32[1,32,512]{2,1,0:T(8,128)S(1)}, f32[1,32,512]{2,1,0:T(8,128)S(1)}, u32[]{:S(2)}, u32[]{:S(2)}) %collective-permute-start.9) | collective-permute-done | bytes 65568 | tf_op jit(solution)/shard_map/ppermute | solution.py:19
  62.7 4.8 %collective-permute-start.10 = (f32[10,1,512]{2,1,0:T(1,128)S(1)}, f32[10,1,512]{2,1,0:T(1,128)S(1)}, u32[]{:S(2)}, u32[]{:S(2)}) collective-permute-start(f32[10,1,512]{2,1,0:T(1,128)S(1)} %get-tuple-element.43), channel_id=1, source_target_pairs={{0,1},{1,2},{2,3},{3,4},{4,5},{5,6},{6,7},{8,9},{9,10},{10,11},{11... | collective-permute-start | bytes 61448 | tf_op jit(solution)/shard_map/ppermute | solution.py:17
  67.6 1.3 collective-permute-start.11
  69.0 4.2 %collective-permute-done.11 = f32[10,1,512]{2,1,0:T(1,128)S(1)} collective-permute-done((f32[10,1,512]{2,1,0:T(1,128)S(1)}, f32[10,1,512]{2,1,0:T(1,128)S(1)}, u32[]{:S(2)}, u32[]{:S(2)}) %collective-permute-start.11) | collective-permute-done | bytes 20512 | tf_op jit(solution)/shard_map/ppermute | solution.py:19
  73.2 2.4 multiply_reduce_fusion.4
  75.6 41.3 %all-reduce.9 = (f32[]{:T(128)}, f32[]{:T(128)}) all-reduce(f32[]{:T(128)} %get-tuple-element.6, f32[]{:T(128)} %get-tuple-element.5), channel_id=1, replica_groups=mesh['gz'=4,'gy'=8] {'gz','gy'}, use_global_device_ids=true, to_apply=%region_1.2 | all-reduce | flops 2 | bytes 16 | tf_op jit(solution)/shard_map/psum | solution.py:50
  118.4 1.2 fusion.77
  119.7 1.4 collective-permute-start.12
  121.1 1.4 collective-permute-start.13
  122.5 4.3 %collective-permute-done.13 = f32[1,32,512]{2,1,0:T(8,128)S(1)} collective-permute-done((f32[1,32,512]{2,1,0:T(8,128)S(1)}, f32[1,32,512]{2,1,0:T(8,128)S(1)}, u32[]{:S(2)}, u32[]{:S(2)}) %collective-permute-start.13) | collective-permute-done | bytes 65568 | tf_op jit(solution)/shard_map/ppermute | solution.py:19
  126.9 3.3 %collective-permute-start.14 = (f32[10,1,512]{2,1,0:T(1,128)S(1)}, f32[10,1,512]{2,1,0:T(1,128)S(1)}, u32[]{:S(2)}, u32[]{:S(2)}) collective-permute-start(f32[10,1,512]{2,1,0:T(1,128)S(1)} %get-tuple-element.41), channel_id=1, source_target_pairs={{0,1},{1,2},{2,3},{3,4},{4,5},{5,6},{6,7},{8,9},{9,10},{10,11},{11... | collective-permute-start | bytes 61448 | tf_op jit(solution)/shard_map/ppermute | solution.py:17
  130.3 1.3 collective-permute-start.15
  131.7 4.2 %collective-permute-done.15 = f32[10,1,512]{2,1,0:T(1,128)S(1)} collective-permute-done((f32[10,1,512]{2,1,0:T(1,128)S(1)}, f32[10,1,512]{2,1,0:T(1,128)S(1)}, u32[]{:S(2)}, u32[]{:S(2)}) %collective-permute-start.15) | collective-permute-done | bytes 20512 | tf_op jit(solution)/shard_map/ppermute | solution.py:19
  136.0 2.5 multiply_reduce_fusion.2
  138.5 41.6 %all-reduce.8 = (f32[]{:T(128)}, f32[]{:T(128)}) all-reduce(f32[]{:T(128)} %get-tuple-element.4, f32[]{:T(128)} %get-tuple-element.3), channel_id=1, replica_groups=mesh['gz'=4,'gy'=8] {'gz','gy'}, use_global_device_ids=true, to_apply=%region_5.6 | all-reduce | flops 2 | bytes 16 | tf_op jit(solution)/shard_map/psum | solution.py:50
  184.7 2.1 multiply_reduce_fusion.1
  186.8 1.3 collective-permute-start.16
  188.1 1.4 collective-permute-start.17
  189.6 4.3 %collective-permute-done.17 = f32[1,32,512]{2,1,0:T(8,128)S(1)} collective-permute-done((f32[1,32,512]{2,1,0:T(8,128)S(1)}, f32[1,32,512]{2,1,0:T(8,128)S(1)}, u32[]{:S(2)}, u32[]{:S(2)}) %collective-permute-start.17) | collective-permute-done | bytes 65568 | tf_op jit(solution)/shard_map/ppermute | solution.py:19
  193.9 2.2 collective-permute-start.18
  196.1 1.4 collective-permute-start.19
  197.6 4.4 %collective-permute-done.19 = f32[10,1,512]{2,1,0:T(1,128)S(1)} collective-permute-done((f32[10,1,512]{2,1,0:T(1,128)S(1)}, f32[10,1,512]{2,1,0:T(1,128)S(1)}, u32[]{:S(2)}, u32[]{:S(2)}) %collective-permute-start.19) | collective-permute-done | bytes 20512 | tf_op jit(solution)/shard_map/ppermute | solution.py:19
  202.0 1.6 fusion.25
  203.5 42.8 %all-reduce.7 = (f32[]{:T(128)}, f32[]{:T(128)}) all-reduce(f32[]{:T(128)} %get-tuple-element.18, f32[]{:T(128)} %fusion.25), channel_id=1, replica_groups=mesh['gz'=4,'gy'=8] {'gz','gy'}, use_global_device_ids=true, to_apply=%region_9.10 | all-reduce | flops 2 | bytes 16 | tf_op jit(solution)/shard_map/psum | solution.py:50
  250.4 13.0 %multiply_reduce_fusion = (f32[]{:T(128)}, f32[8,32,512]{2,1,0:T(8,128)S(1)}, f32[8,32,512]{2,1,0:T(8,128)S(1)}) fusion(f32[8,32,512]{2,1,0:T(8,128)} %param.13, pred[8,32,512]{2,1,0:T(8,128)(4,1)} %copy-done.16, pred[8,32,512]{2,1,0:T(8,128)(4,1)} %copy-done.15, pred[8,32,512]{2,1,0:T(8,128)(4,1)} %copy-done.14, pred[8,32,512]{2,1,0:T(8,128)(4,1)} %copy-done.13, ...), kind=kLoop, calls=%fused_computation.132 | loop fusion | flops 4063231 | bytes 4194392 | tf_op jit(solution)/shard_map/reduce_sum | solution.py:114
  263.4 1.4 collective-permute-start.20
  264.9 1.3 collective-permute-start.21
  266.2 4.3 %collective-permute-done.21 = f32[1,32,512]{2,1,0:T(8,128)S(1)} collective-permute-done((f32[1,32,512]{2,1,0:T(8,128)S(1)}, f32[1,32,512]{2,1,0:T(8,128)S(1)}, u32[]{:S(2)}, u32[]{:S(2)}) %collective-permute-start.21) | collective-permute-done | bytes 65568 | tf_op jit(solution)/shard_map/ppermute | solution.py:19
  270.5 2.2 collective-permute-start.22
  272.8 1.3 collective-permute-start.23
  275.0 3.5 %collective-permute-done.23 = f32[10,1,512]{2,1,0:T(1,128)S(1)} collective-permute-done((f32[10,1,512]{2,1,0:T(1,128)S(1)}, f32[10,1,512]{2,1,0:T(1,128)S(1)}, u32[]{:S(2)}, u32[]{:S(2)}) %collective-permute-start.23) | collective-permute-done | bytes 20512 | tf_op jit(solution)/shard_map/ppermute | solution.py:19
  278.5 1.6 fusion.76
  280.1 42.7 %all-reduce.6 = (f32[1]{0:T(128)}, f32[1]{0:T(128)}) all-reduce(f32[1]{0:T(128)} %bitcast.33, f32[1]{0:T(128)} %bitcast.32), channel_id=1, replica_groups=mesh['gz'=4,'gy'=8] {'gz','gy'}, use_global_device_ids=true, to_apply=%region_15.16 | all-reduce | flops 2 | bytes 16 | tf_op jit(solution)/shard_map/psum | solution.py:114
  322.8 1.8 fusion.78
  (96 shorter events, 4.4 us)
Async XLA Ops:
  1.5 19.3 %collective-permute-start.5 = (f32[1,32,512]{2,1,0:T(8,128)S(1)}, f32[1,32,512]{2,1,0:T(8,128)S(1)}, u32[]{:S(2)}, u32[]{:S(2)}) collective-permute-start(f32[1,32,512]{2,1,0:T(8,128)S(1)} %get-tuple-element.59), channel_id=1, source_target_pairs={{8,0},{16,8},{24,16},{9,1},{17,9},{25,17},{10,2},{18,10},{26,18},{... | collective-permute-start | bytes 196616 | tf_op jit(solution)/shard_map/ppermute | solution.py:19
  2.8 17.9 %collective-permute-start.4 = (f32[1,32,512]{2,1,0:T(8,128)S(1)}, f32[1,32,512]{2,1,0:T(8,128)S(1)}, u32[]{:S(2)}, u32[]{:S(2)}) collective-permute-start(f32[1,32,512]{2,1,0:T(8,128)S(1)} %get-tuple-element.60), channel_id=1, source_target_pairs={{0,8},{8,16},{16,24},{1,9},{9,17},{17,25},{2,10},{10,18},{18,26},{... | collective-permute-start | bytes 196616 | tf_op jit(solution)/shard_map/ppermute | solution.py:17
  6.5 14.2 %copy-start.6 = (f32[8,32,512]{2,1,0:T(8,128)S(1)}, f32[8,32,512]{2,1,0:T(8,128)}, u32[]{:S(2)}) copy-start(f32[8,32,512]{2,1,0:T(8,128)} %param.13) | copy-start | bytes 1572868
  13.3 23.2 %copy-start.11 = (pred[8,32,512]{2,1,0:T(8,128)(4,1)}, pred[8,32,512]{2,1,0:T(8,128)(4,1)S(1)}, u32[]{:S(2)}) copy-start(pred[8,32,512]{2,1,0:T(8,128)(4,1)S(1)} %get-tuple-element.31) | copy-start | bytes 393220
  13.3 23.2 %copy-start.12 = (pred[8,32,512]{2,1,0:T(8,128)(4,1)}, pred[8,32,512]{2,1,0:T(8,128)(4,1)S(1)}, u32[]{:S(2)}) copy-start(pred[8,32,512]{2,1,0:T(8,128)(4,1)S(1)} %get-tuple-element.32) | copy-start | bytes 393220
  13.3 23.1 %copy-start.13 = (pred[8,32,512]{2,1,0:T(8,128)(4,1)}, pred[8,32,512]{2,1,0:T(8,128)(4,1)S(1)}, u32[]{:S(2)}) copy-start(pred[8,32,512]{2,1,0:T(8,128)(4,1)S(1)} %get-tuple-element.33) | copy-start | bytes 393220
  13.3 23.1 %copy-start.14 = (pred[8,32,512]{2,1,0:T(8,128)(4,1)}, pred[8,32,512]{2,1,0:T(8,128)(4,1)S(1)}, u32[]{:S(2)}) copy-start(pred[8,32,512]{2,1,0:T(8,128)(4,1)S(1)} %get-tuple-element.34) | copy-start | bytes 393220
  13.3 23.1 %copy-start.15 = (pred[8,32,512]{2,1,0:T(8,128)(4,1)}, pred[8,32,512]{2,1,0:T(8,128)(4,1)S(1)}, u32[]{:S(2)}) copy-start(pred[8,32,512]{2,1,0:T(8,128)(4,1)S(1)} %get-tuple-element.35) | copy-start | bytes 393220
  13.4 23.1 %copy-start.16 = (pred[8,32,512]{2,1,0:T(8,128)(4,1)}, pred[8,32,512]{2,1,0:T(8,128)(4,1)S(1)}, u32[]{:S(2)}) copy-start(pred[8,32,512]{2,1,0:T(8,128)(4,1)S(1)} %get-tuple-element.36) | copy-start | bytes 393220
  13.4 12.4 %collective-permute-start = (f32[1,32,512]{2,1,0:T(8,128)S(1)}, f32[1,32,512]{2,1,0:T(8,128)S(1)}, u32[]{:S(2)}, u32[]{:S(2)}) collective-permute-start(f32[1,32,512]{2,1,0:T(8,128)S(1)} %get-tuple-element.57), channel_id=1, source_target_pairs={{0,8},{8,16},{16,24},{1,9},{9,17},{17,25},{2,10},{10,18},{18,26},{... | collective-permute-start | bytes 196616 | tf_op jit(solution)/shard_map/ppermute | solution.py:17
  18.0 7.7 %collective-permute-start.1 = (f32[1,32,512]{2,1,0:T(8,128)S(1)}, f32[1,32,512]{2,1,0:T(8,128)S(1)}, u32[]{:S(2)}, u32[]{:S(2)}) collective-permute-start(f32[1,32,512]{2,1,0:T(8,128)S(1)} %get-tuple-element.58), channel_id=1, source_target_pairs={{8,0},{16,8},{24,16},{9,1},{17,9},{25,17},{10,2},{18,10},{26,18},{... | collective-permute-start | bytes 196616 | tf_op jit(solution)/shard_map/ppermute | solution.py:19
  20.7 15.8 %copy-start.18 = (f32[8,32,512]{2,1,0:T(8,128)S(1)}, f32[8,32,512]{2,1,0:T(8,128)}, u32[]{:S(2)}) copy-start(f32[8,32,512]{2,1,0:T(8,128)} %param.12) | copy-start | bytes 1572868
  20.7 10.9 %copy-start.30 = (f32[8]{0:T(128)S(1)}, f32[8]{0:T(128)}, u32[]{:S(2)}) copy-start(f32[8]{0:T(128)} %param.19) | copy-start | bytes 100
  20.7 15.8 %copy-start.8 = (f32[8,32,512]{2,1,0:T(8,128)S(1)}, f32[8,32,512]{2,1,0:T(8,128)}, u32[]{:S(2)}) copy-start(f32[8,32,512]{2,1,0:T(8,128)} %param.14) | copy-start | bytes 1572868
  20.8 15.8 %copy-start.17 = (f32[8,32,512]{2,1,0:T(8,128)S(1)}, f32[8,32,512]{2,1,0:T(8,128)}, u32[]{:S(2)}) copy-start(f32[8,32,512]{2,1,0:T(8,128)} %param.15) | copy-start | bytes 1572868
  20.8 15.7 %copy-start = (s32[8,32,512]{2,1,0:T(8,128)S(1)}, s32[8,32,512]{2,1,0:T(8,128)}, u32[]{:S(2)}) copy-start(s32[8,32,512]{2,1,0:T(8,128)} %param.11) | copy-start | bytes 1572868
  20.9 11.5 %collective-permute-start.6 = (f32[10,1,512]{2,1,0:T(1,128)S(1)}, f32[10,1,512]{2,1,0:T(1,128)S(1)}, u32[]{:S(2)}, u32[]{:S(2)}) collective-permute-start(f32[10,1,512]{2,1,0:T(1,128)S(1)} %get-tuple-element.47), channel_id=1, source_target_pairs={{0,1},{1,2},{2,3},{3,4},{4,5},{5,6},{6,7},{8,9},{9,10},{10,11},{11... | collective-permute-start | bytes 61448 | tf_op jit(solution)/shard_map/ppermute | solution.py:17
  24.5 7.9 %collective-permute-start.7 = (f32[10,1,512]{2,1,0:T(1,128)S(1)}, f32[10,1,512]{2,1,0:T(1,128)S(1)}, u32[]{:S(2)}, u32[]{:S(2)}) collective-permute-start(f32[10,1,512]{2,1,0:T(1,128)S(1)} %get-tuple-element.48), channel_id=1, source_target_pairs={{1,0},{2,1},{3,2},{4,3},{5,4},{6,5},{7,6},{9,8},{10,9},{11,10},{12... | collective-permute-start | bytes 61448 | tf_op jit(solution)/shard_map/ppermute | solution.py:19
  25.8 6.6 %collective-permute-start.2 = (f32[10,1,512]{2,1,0:T(1,128)S(1)}, f32[10,1,512]{2,1,0:T(1,128)S(1)}, u32[]{:S(2)}, u32[]{:S(2)}) collective-permute-start(f32[10,1,512]{2,1,0:T(1,128)S(1)} %get-tuple-element.45), channel_id=1, source_target_pairs={{0,1},{1,2},{2,3},{3,4},{4,5},{5,6},{6,7},{8,9},{9,10},{10,11},{11... | collective-permute-start | bytes 61448 | tf_op jit(solution)/shard_map/ppermute | solution.py:17
  30.4 6.1 %collective-permute-start.3 = (f32[10,1,512]{2,1,0:T(1,128)S(1)}, f32[10,1,512]{2,1,0:T(1,128)S(1)}, u32[]{:S(2)}, u32[]{:S(2)}) collective-permute-start(f32[10,1,512]{2,1,0:T(1,128)S(1)} %get-tuple-element.46), channel_id=1, source_target_pairs={{1,0},{2,1},{3,2},{4,3},{5,4},{6,5},{7,6},{9,8},{10,9},{11,10},{12... | collective-permute-start | bytes 61448 | tf_op jit(solution)/shard_map/ppermute | solution.py:19
  32.4 40.8 %copy-start.19 = (f32[10,1,512]{2,1,0:T(1,128)}, f32[10,1,512]{2,1,0:T(1,128)S(1)}, u32[]{:S(2)}) copy-start(f32[10,1,512]{2,1,0:T(1,128)S(1)} %collective-permute-done.2) | copy-start | bytes 61444
  36.5 36.8 %copy-start.23 = (f32[10,1,512]{2,1,0:T(1,128)}, f32[10,1,512]{2,1,0:T(1,128)S(1)}, u32[]{:S(2)}) copy-start(f32[10,1,512]{2,1,0:T(1,128)S(1)} %collective-permute-done.3) | copy-start | bytes 61444
  55.2 20.4 %copy-start.1 = (f32[8,32,512]{2,1,0:T(8,128)}, f32[8,32,512]{2,1,0:T(8,128)S(1)}, u32[]{:S(2)}) copy-start(f32[8,32,512]{2,1,0:T(8,128)S(1)} %get-tuple-element.22) | copy-start | bytes 1572868
  55.3 2.6 collective-permute-start.8
  56.6 6.1 %collective-permute-start.9 = (f32[1,32,512]{2,1,0:T(8,128)S(1)}, f32[1,32,512]{2,1,0:T(8,128)S(1)}, u32[]{:S(2)}, u32[]{:S(2)}) collective-permute-start(f32[1,32,512]{2,1,0:T(8,128)S(1)} %get-tuple-element.56), channel_id=1, source_target_pairs={{8,0},{16,8},{24,16},{9,1},{17,9},{25,17},{10,2},{18,10},{26,18},{... | collective-permute-start | bytes 196616 | tf_op jit(solution)/shard_map/ppermute | solution.py:19
  62.7 6.3 %collective-permute-start.10 = (f32[10,1,512]{2,1,0:T(1,128)S(1)}, f32[10,1,512]{2,1,0:T(1,128)S(1)}, u32[]{:S(2)}, u32[]{:S(2)}) collective-permute-start(f32[10,1,512]{2,1,0:T(1,128)S(1)} %get-tuple-element.43), channel_id=1, source_target_pairs={{0,1},{1,2},{2,3},{3,4},{4,5},{5,6},{6,7},{8,9},{9,10},{10,11},{11... | collective-permute-start | bytes 61448 | tf_op jit(solution)/shard_map/ppermute | solution.py:17
  67.6 5.7 %collective-permute-start.11 = (f32[10,1,512]{2,1,0:T(1,128)S(1)}, f32[10,1,512]{2,1,0:T(1,128)S(1)}, u32[]{:S(2)}, u32[]{:S(2)}) collective-permute-start(f32[10,1,512]{2,1,0:T(1,128)S(1)} %get-tuple-element.44), channel_id=1, source_target_pairs={{1,0},{2,1},{3,2},{4,3},{5,4},{6,5},{7,6},{9,8},{10,9},{11,10},{12... | collective-permute-start | bytes 61448 | tf_op jit(solution)/shard_map/ppermute | solution.py:19
  119.6 18.8 %copy-start.3 = (f32[8,32,512]{2,1,0:T(8,128)}, f32[8,32,512]{2,1,0:T(8,128)S(1)}, u32[]{:S(2)}) copy-start(f32[8,32,512]{2,1,0:T(8,128)S(1)} %fusion.77) | copy-start | bytes 1572868
  119.6 16.3 %copy-start.5 = (f32[8,32,512]{2,1,0:T(8,128)S(1)}, f32[8,32,512]{2,1,0:T(8,128)}, u32[]{:S(2)}) copy-start(f32[8,32,512]{2,1,0:T(8,128)} %get-tuple-element.21) | copy-start | bytes 1572868
  119.7 2.9 collective-permute-start.12
  121.1 14.9 %copy-start.20 = (f32[10,1,512]{2,1,0:T(1,128)S(1)}, f32[10,1,512]{2,1,0:T(1,128)}, u32[]{:S(2)}) copy-start(f32[10,1,512]{2,1,0:T(1,128)} %copy-done.19) | copy-start | bytes 61444
  121.1 14.9 %copy-start.24 = (f32[10,1,512]{2,1,0:T(1,128)S(1)}, f32[10,1,512]{2,1,0:T(1,128)}, u32[]{:S(2)}) copy-start(f32[10,1,512]{2,1,0:T(1,128)} %copy-done.23) | copy-start | bytes 61444
  121.1 5.8 %collective-permute-start.13 = (f32[1,32,512]{2,1,0:T(8,128)S(1)}, f32[1,32,512]{2,1,0:T(8,128)S(1)}, u32[]{:S(2)}, u32[]{:S(2)}) collective-permute-start(f32[1,32,512]{2,1,0:T(8,128)S(1)} %get-tuple-element.54), channel_id=1, source_target_pairs={{8,0},{16,8},{24,16},{9,1},{17,9},{25,17},{10,2},{18,10},{26,18},{... | collective-permute-start | bytes 196616 | tf_op jit(solution)/shard_map/ppermute | solution.py:19
  126.9 4.8 %collective-permute-start.14 = (f32[10,1,512]{2,1,0:T(1,128)S(1)}, f32[10,1,512]{2,1,0:T(1,128)S(1)}, u32[]{:S(2)}, u32[]{:S(2)}) collective-permute-start(f32[10,1,512]{2,1,0:T(1,128)S(1)} %get-tuple-element.41), channel_id=1, source_target_pairs={{0,1},{1,2},{2,3},{3,4},{4,5},{5,6},{6,7},{8,9},{9,10},{10,11},{11... | collective-permute-start | bytes 61448 | tf_op jit(solution)/shard_map/ppermute | solution.py:17
  130.3 5.7 %collective-permute-start.15 = (f32[10,1,512]{2,1,0:T(1,128)S(1)}, f32[10,1,512]{2,1,0:T(1,128)S(1)}, u32[]{:S(2)}, u32[]{:S(2)}) collective-permute-start(f32[10,1,512]{2,1,0:T(1,128)S(1)} %get-tuple-element.42), channel_id=1, source_target_pairs={{1,0},{2,1},{3,2},{4,3},{5,4},{6,5},{7,6},{9,8},{10,9},{11,10},{12... | collective-permute-start | bytes 61448 | tf_op jit(solution)/shard_map/ppermute | solution.py:19
  186.8 16.8 %copy-start.4 = (f32[8,32,512]{2,1,0:T(8,128)}, f32[8,32,512]{2,1,0:T(8,128)S(1)}, u32[]{:S(2)}) copy-start(f32[8,32,512]{2,1,0:T(8,128)S(1)} %get-tuple-element.19) | copy-start | bytes 1572868
  186.8 2.8 collective-permute-start.16
  188.1 13.9 %copy-start.21 = (f32[10,1,512]{2,1,0:T(1,128)S(1)}, f32[10,1,512]{2,1,0:T(1,128)}, u32[]{:S(2)}) copy-start(f32[10,1,512]{2,1,0:T(1,128)} %copy-done.19) | copy-start | bytes 61444
  188.1 13.9 %copy-start.25 = (f32[10,1,512]{2,1,0:T(1,128)S(1)}, f32[10,1,512]{2,1,0:T(1,128)}, u32[]{:S(2)}) copy-start(f32[10,1,512]{2,1,0:T(1,128)} %copy-done.23) | copy-start | bytes 61444
  188.1 5.8 %collective-permute-start.17 = (f32[1,32,512]{2,1,0:T(8,128)S(1)}, f32[1,32,512]{2,1,0:T(8,128)S(1)}, u32[]{:S(2)}, u32[]{:S(2)}) collective-permute-start(f32[1,32,512]{2,1,0:T(8,128)S(1)} %get-tuple-element.52), channel_id=1, source_target_pairs={{8,0},{16,8},{24,16},{9,1},{17,9},{25,17},{10,2},{18,10},{26,18},{... | collective-permute-start | bytes 196616 | tf_op jit(solution)/shard_map/ppermute | solution.py:19
  193.9 3.7 %collective-permute-start.18 = (f32[10,1,512]{2,1,0:T(1,128)S(1)}, f32[10,1,512]{2,1,0:T(1,128)S(1)}, u32[]{:S(2)}, u32[]{:S(2)}) collective-permute-start(f32[10,1,512]{2,1,0:T(1,128)S(1)} %get-tuple-element.39), channel_id=1, source_target_pairs={{0,1},{1,2},{2,3},{3,4},{4,5},{5,6},{6,7},{8,9},{9,10},{10,11},{11... | collective-permute-start | bytes 61448 | tf_op jit(solution)/shard_map/ppermute | solution.py:17
  196.1 54.3 %copy-start.2 = (f32[8,32,512]{2,1,0:T(8,128)S(1)}, f32[8,32,512]{2,1,0:T(8,128)}, u32[]{:S(2)}) copy-start(f32[8,32,512]{2,1,0:T(8,128)} %copy-done.1) | copy-start | bytes 1572868
  196.1 5.8 %collective-permute-start.19 = (f32[10,1,512]{2,1,0:T(1,128)S(1)}, f32[10,1,512]{2,1,0:T(1,128)S(1)}, u32[]{:S(2)}, u32[]{:S(2)}) collective-permute-start(f32[10,1,512]{2,1,0:T(1,128)S(1)} %get-tuple-element.40), channel_id=1, source_target_pairs={{1,0},{2,1},{3,2},{4,3},{5,4},{6,5},{7,6},{9,8},{10,9},{11,10},{12... | collective-permute-start | bytes 61448 | tf_op jit(solution)/shard_map/ppermute | solution.py:19
  263.4 15.1 %copy-start.7 = (f32[8,32,512]{2,1,0:T(8,128)}, f32[8,32,512]{2,1,0:T(8,128)S(1)}, u32[]{:S(2)}) copy-start(f32[8,32,512]{2,1,0:T(8,128)S(1)} %get-tuple-element.17) | copy-start | bytes 1572868
  263.4 2.7 collective-permute-start.20
  264.9 5.7 %collective-permute-start.21 = (f32[1,32,512]{2,1,0:T(8,128)S(1)}, f32[1,32,512]{2,1,0:T(8,128)S(1)}, u32[]{:S(2)}, u32[]{:S(2)}) collective-permute-start(f32[1,32,512]{2,1,0:T(8,128)S(1)} %get-tuple-element.50), channel_id=1, source_target_pairs={{8,0},{16,8},{24,16},{9,1},{17,9},{25,17},{10,2},{18,10},{26,18},{... | collective-permute-start | bytes 196616 | tf_op jit(solution)/shard_map/ppermute | solution.py:19
  270.5 4.5 %collective-permute-start.22 = (f32[10,1,512]{2,1,0:T(1,128)S(1)}, f32[10,1,512]{2,1,0:T(1,128)S(1)}, u32[]{:S(2)}, u32[]{:S(2)}) collective-permute-start(f32[10,1,512]{2,1,0:T(1,128)S(1)} %get-tuple-element.37), channel_id=1, source_target_pairs={{0,1},{1,2},{2,3},{3,4},{4,5},{5,6},{6,7},{8,9},{9,10},{10,11},{11... | collective-permute-start | bytes 61448 | tf_op jit(solution)/shard_map/ppermute | solution.py:17
  272.8 5.7 %collective-permute-start.23 = (f32[10,1,512]{2,1,0:T(1,128)S(1)}, f32[10,1,512]{2,1,0:T(1,128)S(1)}, u32[]{:S(2)}, u32[]{:S(2)}) collective-permute-start(f32[10,1,512]{2,1,0:T(1,128)S(1)} %get-tuple-element.38), channel_id=1, source_target_pairs={{1,0},{2,1},{3,2},{4,3},{5,4},{6,5},{7,6},{9,8},{10,9},{11,10},{12... | collective-permute-start | bytes 61448 | tf_op jit(solution)/shard_map/ppermute | solution.py:19
  (7 other events, 40.8 us)
where the time goes:
time: 327 us; the launch traced here: 325 us
  blocking collectives  168 us (51%)
  other arithmetic  52.6 us (16%)
  starting transfers between devices  49.7 us (15%)
  waiting for transfers between devices  38.5 us (12%)
  between operations  11.4 us (3%)
  local copies, waits for them, and re-layouts  3.84 us (1%)
    psum x3, blocking collectives, paired_totals(): lax.psum((jnp.sum(residual * precond), jnp.sum(precond * applied)), ('gz'...  126 us
    psum x1, blocking collectives, per_device(): lax.psum((jnp.sum(closing * closing), jnp.sum(change * change)), ('gz', '...  42.7 us
    ppermute x12, waiting for transfers between devices, with_halo(): lax.ppermute(head, axis, [((i + 1) % count, i) for i in range(ends)])  38.1 us
    ppermute x12, starting transfers between devices, with_halo(): lax.ppermute(tail, axis, [(i, (i + 1) % count) for i in range(ends)])  33.8 us
    div x2, other arithmetic, per_device(): precond = residual / diagonal  19.9 us
    ppermute x12, starting transfers between devices, with_halo(): lax.ppermute(head, axis, [((i + 1) % count, i) for i in range(ends)])  15.9 us
    reduce_sum x1, other arithmetic, per_device(): jnp.sum(change * change)  13 us
    select_n x1, other arithmetic, lookup(): result = jnp.where(zone_ids == zone_index, zone_table[zone_index], result)  6.75 us
  transfers between devices with their start and end apart: 24, of which 11 were waited for; matrix products, arithmetic and copies ran while one was open for 3% of the time, Pallas kernels for 0%

commit v1 on v0

v1 whole, which is shorter than its diff:
```python
import functools

import jax
import jax.numpy as jnp
from jax import lax
from jax.experimental import pallas as pl
from jax.experimental.pallas import tpu as pltpu
from jax.sharding import PartitionSpec as P

F32 = jnp.float32
ROWS = 8
LANES = 128
VMEM = pl.BlockSpec(memory_space=pltpu.VMEM)
SMEM = pl.BlockSpec(memory_space=pltpu.SMEM)

MOMENTS = (("q", 0, "u", 0), ("q", 0, "u", 1), ("q", 1, "u", 1), ("q", 1, "u", 2), ("q", 2, "u", 2), ("q", 2, "u", 3))
CLOSING = tuple(("u", i, "u", j) for i in range(4) for j in range(i, 4))
CHANGE = tuple(("y", i, "y", j) for i in range(3) for j in range(i, 3))
SUMS = MOMENTS + CLOSING + CHANGE
EARLY = tuple(s for s in SUMS if max(s[1], s[3]) <= 1)
MIDDLE = tuple(s for s in SUMS if max(s[1], s[3]) == 2)
LATE = tuple(s for s in SUMS if max(s[1], s[3]) == 3)


def table_row(table_ref):
    lane = lax.broadcasted_iota(jnp.int32, (ROWS, LANES), 1)
    row = jnp.zeros((ROWS, LANES), F32)
    for zone in range(table_ref.shape[0]):
        row = jnp.where(lane == zone, table_ref[zone], row)
    return row


def look_up(row, zones):
    parts = [
        jnp.take_along_axis(row, zones[:, at : at + LANES], axis=1, mode="promise_in_bounds")
        for at in range(0, zones.shape[1], LANES)
    ]
    return jnp.concatenate(parts, axis=1)


def harmonic(lower_side, upper_side):
    return 2.0 * lower_side * upper_side / (lower_side + upper_side)


def row_shifts(tiles, before, after):
    sub = lax.broadcasted_iota(jnp.int32, tiles[0].shape, 0)
    down = [pltpu.roll(tile, 1, 0) for tile in tiles]
    up = [pltpu.roll(tile, ROWS - 1, 0) for tile in tiles]
    lower, upper = [], []
    for at in range(len(tiles)):
        lower.append(jnp.where(sub == 0, down[at - 1] if at else before, down[at]))
        upper.append(jnp.where(sub == ROWS - 1, up[at + 1] if at + 1 < len(tiles) else after, up[at]))
    return lower, upper


def lane_shifts(tile):
    width = tile.shape[1]
    return pltpu.roll(tile, 1, 1), pltpu.roll(tile, width - 1, 1)


def pack_kernel(zone_ref, pressure_ref, perm_table, z_low, z_high, y_low, y_high):
    planes, rows, _ = zone_ref.shape
    perm_row = table_row(perm_table)
    for plane, out in ((0, z_low), (planes - 1, z_high)):
        for at in range(0, rows, ROWS):
            part = pl.ds(at, ROWS)
            out[0, part] = look_up(perm_row, zone_ref[plane, part])
        out[1] = pressure_ref[plane]
    for row, out in ((0, y_low), (rows - 1, y_high)):
        for plane in range(planes):
            out[1, pl.ds(plane, 1)] = pressure_ref[plane, pl.ds(row, 1)]
        zones = jnp.concatenate([zone_ref[plane, pl.ds(row, 1)] for plane in range(planes)], axis=0)
        out[0] = look_up(perm_row, zones)


def write_faces(values, z, at, planes, rows, z_low, z_high, y_low, y_high):
    if at == 0:
        y_low[pl.ds(z, 1)] = values[:1]
    if at == rows - ROWS:
        y_high[pl.ds(z, 1)] = values[ROWS - 1 :]


def setup_kernel(
    zone_ref, fixed_ref, old_ref, pressure_ref, strain_ref, source_ref,
    perm_table, storage_table, biot_table, bulk_table,
    below_z, above_z, below_y, above_y,
    faces, inverse, ratio, q_out, u_out, z_low, z_high, y_low, y_high,
    perm,
):
    planes, rows, width = zone_ref.shape
    gz, gy = lax.axis_index("gz"), lax.axis_index("gy")
    inside = [
        jnp.where(test, 1.0, 0.0).astype(F32)
        for test in (gz > 0, gz < lax.axis_size("gz") - 1, gy > 0, gy < lax.axis_size("gy") - 1)
    ]
    perm_row = table_row(perm_table)
    storage_row = table_row(storage_table)
    biot_row = table_row(biot_table)
    bulk_row = jnp.where(lax.broadcasted_iota(jnp.int32, (ROWS, LANES), 1) < bulk_table.shape[0], table_row(bulk_table), 1.0)
    ratio_row = biot_row / bulk_row
    coupling_row = biot_row * biot_row / bulk_row
    lane = lax.broadcasted_iota(jnp.int32, (ROWS, width), 1)
    perm[0] = below_z[0] * inside[0]
    perm[planes + 1] = above_z[0] * inside[1]

    def fill(z, carry):
        for at in range(0, rows, ROWS):
            part = pl.ds(at, ROWS)
            perm[z + 1, part] = look_up(perm_row, zone_ref[z, part])
        return carry

    lax.fori_loop(0, planes, fill, 0)

    def plane(z, low_pressure, high_pressure):
        parts = [pl.ds(at, ROWS) for at in range(0, rows, ROWS)]
        perms = [perm[z + 1, part] for part in parts]
        values = [pressure_ref[z, part] for part in parts]
        one = pl.ds(z, 1)
        full = (ROWS, width)
        perm_lower, perm_upper = row_shifts(
            perms,
            jnp.broadcast_to(below_y[0, one] * inside[2], full),
            jnp.broadcast_to(above_y[0, one] * inside[3], full),
        )
        value_lower, value_upper = row_shifts(
            values, jnp.broadcast_to(below_y[1, one], full), jnp.broadcast_to(above_y[1, one], full)
        )
        for at, part in enumerate(parts):
            zones = zone_ref[z, part]
            storage = look_up(storage_row, zones)
            coupling = look_up(coupling_row, zones)
            biot = look_up(biot_row, zones)
            ratio[z, part] = look_up(ratio_row, zones)
            here, value = perms[at], values[at]
            x_lower, x_upper = lane_shifts(here)
            x_lower = jnp.where(lane == 0, 0.0, x_lower)
            x_upper = jnp.where(lane == width - 1, 0.0, x_upper)
            value_left, value_right = lane_shifts(value)
            beside = (perm[z, part], perm[z + 2, part], perm_lower[at], perm_upper[at], x_lower, x_upper)
            terms = [harmonic(here, other) for other in beside]
            free = 1.0 - fixed_ref[z, part].astype(F32)
            diagonal = storage + coupling
            for term in terms:
                diagonal = diagonal + term
            views = (low_pressure[part], high_pressure[part], value_lower[at], value_upper[at], value_left, value_right)
            neighbours = terms[0] * views[0]
            for number in range(1, 6):
                neighbours = neighbours + terms[number] * views[number]
            right_side = (
                storage * old_ref[z, part] + coupling * value - biot * strain_ref[z, part] + source_ref[z, part]
            )
            residual = free * (right_side - (diagonal * value - neighbours))
            reciprocal = 1.0 / diagonal
            precond = residual * reciprocal
            for number in range(6):
                faces[number, z, part] = free * terms[number]
            inverse[z, part] = reciprocal
            u_out[z, part] = residual
            q_out[z, part] = precond
            write_faces(precond, z, part.start, planes, rows, z_low, z_high, y_low, y_high)

    plane(0, below_z.at[1], pressure_ref.at[1])
    lax.fori_loop(1, planes - 1, lambda z, c: (plane(z, pressure_ref.at[z - 1], pressure_ref.at[z + 1]), c)[1], 0)
    plane(planes - 1, pressure_ref.at[planes - 2], above_z.at[1])
    z_low[...] = q_out[0]
    z_high[...] = q_out[planes - 1]


def apply_plane(z, low, high, q_ref, faces, inverse, below_y, above_y, emit):
    rows, width = q_ref.shape[1:]
    parts = [pl.ds(at, ROWS) for at in range(0, rows, ROWS)]
    values = [q_ref[z, part] for part in parts]
    one, full = pl.ds(z, 1), (ROWS, width)
    lower, upper = row_shifts(
        values, jnp.broadcast_to(below_y[one], full), jnp.broadcast_to(above_y[one], full)
    )
    for at, part in enumerate(parts):
        left, right = lane_shifts(values[at])
        u = faces[0, z, part] * low[part] + faces[1, z, part] * high[part]
        u = u + faces[2, z, part] * lower[at] + faces[3, z, part] * upper[at]
        u = u + faces[4, z, part] * left + faces[5, z, part] * right
        emit(part, u, u * inverse[z, part])


def over_planes(planes, q_ref, below_z, above_z, body, carry):
    carry = body(0, below_z, q_ref.at[1], carry)
    carry = lax.fori_loop(1, planes - 1, lambda z, c: body(z, q_ref.at[z - 1], q_ref.at[z + 1], c), carry)
    return body(planes - 1, q_ref.at[planes - 2], above_z, carry)


def stage_kernel(
    q_ref, faces, inverse, below_z, above_z, below_y, above_y,
    q_out, u_out, z_low, z_high, y_low, y_high,
):
    planes, rows, _ = q_ref.shape

    def body(z, low, high, carry):
        def emit(part, u, q):
            u_out[z, part] = u
            q_out[z, part] = q
            write_faces(q, z, part.start, planes, rows, z_low, z_high, y_low, y_high)

        apply_plane(z, low, high, q_ref, faces, inverse, below_y, above_y, emit)
        return carry

    over_planes(planes, q_ref, below_z, above_z, body, 0)
    z_low[...] = q_out[0]
    z_high[...] = q_out[planes - 1]


def fold(product):
    total = product[:, :LANES]
    for at in range(LANES, product.shape[1], LANES):
        total = total + product[:, at : at + LANES]
    return total


def gram_kernel(sums, count, *refs):
    us, qs = refs[: count], refs[count : 2 * count]
    ratio, out = refs[2 * count :]
    planes, rows, _ = ratio.shape

    def body(z, totals):
        totals = list(totals)
        for at in range(0, rows, ROWS):
            part = pl.ds(at, ROWS)
            fields = {("u", i): us[i][z, part] for i in range(count)}
            fields |= {("q", i): qs[i][z, part] for i in range(count)}
            weight = ratio[z, part]
            fields |= {("y", i): weight * fields["q", i] for i in range(count)}
            for number, (a, i, b, j) in enumerate(sums):
                totals[number] = totals[number] + fold(fields[a, i] * fields[b, j])
        return tuple(totals)

    zero = jnp.zeros((ROWS, LANES), F32)
    for number, total in enumerate(lax.fori_loop(0, planes, body, (zero,) * len(sums))):
        out[number] = total


def last_kernel(
    q2_ref, faces, inverse, u0_ref, u1_ref, u2_ref, below_z, above_z, below_y, above_y, early, middle, out
):
    planes = q2_ref.shape[0]
    us = (u0_ref, u1_ref, u2_ref)

    def body(z, low, high, totals):
        totals = list(totals)

        def emit(part, u3, _):
            fields = {("u", i): us[i][z, part] for i in range(3)}
            fields |= {("u", 3): u3, ("q", 2): q2_ref[z, part]}
            for number, (a, i, b, j) in enumerate(LATE):
                totals[number] = totals[number] + fold(fields[a, i] * fields[b, j])

        apply_plane(z, low, high, q2_ref, faces, inverse, below_y, above_y, emit)
        return tuple(totals)

    zero = jnp.zeros((ROWS, LANES), F32)
    late = over_planes(planes, q2_ref, below_z, above_z, body, (zero,) * len(LATE))
    lane = lax.broadcasted_iota(jnp.int32, (1, LANES), 1)
    row = jnp.zeros((1, LANES), F32)
    for names, totals in ((EARLY, early), (MIDDLE, middle), (LATE, late)):
        for number, name in enumerate(names):
            row = jnp.where(lane == SUMS.index(name), jnp.sum(totals[number], keepdims=True), row)
    out[...] = jnp.broadcast_to(row, out.shape)


def quadratic(left, table, right):
    total = None
    for i, a in enumerate(left):
        for j, b in enumerate(right):
            if a is None or b is None:
                continue
            term = a * b * table(i, j)
            total = term if total is None else total + term
    return total


def combine(totals, cell_count, iterations=3):
    moment = lambda i, j: totals[i + j]
    drop = lambda i, j: totals[i + j] - totals[i + j + 1]
    zero = jnp.zeros_like(totals[0])
    one = zero + 1.0
    residual, direction, change = [one], [one], []
    inner = moment(0, 0)
    for step in range(iterations):
        curvature = quadratic(direction, drop, direction)
        alive = (inner > 0.0) & (curvature > 0.0)
        size = jnp.where(alive, inner / jnp.where(alive, curvature, 1.0), 0.0)
        change = [c + size * d for c, d in zip(change + [zero], direction)]
        image = [a - b for a, b in zip(direction + [zero], [zero] + direction)]
        residual = [r - size * a for r, a in zip(residual + [zero], image)]
        if step + 1 < iterations:
            following = quadratic(residual, moment, residual)
            noise = quadratic([abs(r) for r in residual], lambda i, j: abs(moment(i, j)), [abs(r) for r in residual])
            following = jnp.where(following > 1e-7 * noise, following, 0.0)
            growth = jnp.where(inner > 0.0, following / jnp.where(inner > 0.0, inner, 1.0), 0.0)
            direction = [z + growth * d for z, d in zip(residual, direction + [zero])]
            inner = following
    at = {name: total for name, total in zip(SUMS, totals)}
    closing = quadratic(residual, lambda i, j: at["u", min(i, j), "u", max(i, j)], residual)
    changed = quadratic(change, lambda i, j: at["y", min(i, j), "y", max(i, j)], change)
    scale = 1.0 / cell_count
    return change, jnp.sqrt(jnp.maximum(closing, 0.0) * scale), jnp.sqrt(jnp.maximum(changed, 0.0) * scale)


def final_kernel(cell_count, rows_ref, q0, q1, q2, pressure_ref, strain_ref, ratio, pressure_out, strain_out, norms):
    planes, rows, width = pressure_ref.shape
    lane = lax.broadcasted_iota(jnp.int32, (1, LANES), 1)
    row = jnp.sum(rows_ref[...], axis=0, keepdims=True)
    totals = [jnp.sum(jnp.where(lane == at, row, 0.0), axis=1, keepdims=True) for at in range(len(SUMS))]
    change, closing, changed = combine(totals, cell_count)
    norms[...] = jnp.where(lane == 0, closing, changed)[:, :2]
    weights = [jnp.broadcast_to(c, (ROWS, width)) for c in change]

    def body(z, carry):
        for at in range(0, rows, ROWS):
            part = pl.ds(at, ROWS)
            delta = weights[0] * q0[z, part] + weights[1] * q1[z, part] + weights[2] * q2[z, part]
            pressure_out[z, part] = pressure_ref[z, part] + delta
            strain_out[z, part] = strain_ref[z, part] + ratio[z, part] * delta
        return carry

    lax.fori_loop(0, planes, body, 0)


def ring(axis, step):
    count = lax.axis_size(axis)
    return [(i, (i + step) % count) for i in range(count)]


def exchange(z_low, z_high, y_low, y_high):
    return (
        lax.ppermute(z_high, "gz", ring("gz", 1)),
        lax.ppermute(z_low, "gz", ring("gz", -1)),
        lax.ppermute(y_high, "gy", ring("gy", 1)),
        lax.ppermute(y_low, "gy", ring("gy", -1)),
    )


def call(kernel, name, outs, specs, *operands, scratch=()):
    shapes = [jax.ShapeDtypeStruct(shape, F32) for shape in outs]
    single = len(shapes) == 1
    return pl.pallas_call(
        kernel,
        name=name,
        out_shape=shapes[0] if single else shapes,
        in_specs=specs,
        out_specs=VMEM if single else [VMEM] * len(shapes),
        scratch_shapes=list(scratch),
    )(*operands)


def per_device(
    zone_ids, fixed_cells, pressure_old, pressure_iter, strain_change, source,
    zone_perm, zone_storage, zone_biot, zone_bulk,
):
    planes, rows, width = zone_ids.shape
    field = (planes, rows, width)
    sides = ((rows, width), (rows, width), (planes, width), (planes, width))
    devices = lax.axis_size("gz") * lax.axis_size("gy")
    cell_count = zone_ids.size * devices

    packed = call(
        pack_kernel, "pack", [(2, *side) for side in sides], [VMEM, VMEM, SMEM], zone_ids, pressure_iter, zone_perm
    )
    halo = exchange(*packed)
    faces, inverse, ratio, q0, u0, *edges = call(
        setup_kernel, "setup", [(6, *field), field, field, field, field, *sides],
        [VMEM] * 6 + [SMEM] * 4 + [VMEM] * 4,
        zone_ids, fixed_cells, pressure_old, pressure_iter, strain_change, source,
        zone_perm, zone_storage, zone_biot, zone_bulk, *halo,
        scratch=[pltpu.VMEM((planes + 2, rows, width), F32)],
    )
    halo = exchange(*edges)
    q1, u1, *edges = call(stage_kernel, "stage", [field, field, *sides], [VMEM] * 7, q0, faces, inverse, *halo)
    halo = exchange(*edges)
    early = call(
        functools.partial(gram_kernel, EARLY, 2), "gram_early", [(len(EARLY), ROWS, LANES)], [VMEM] * 5,
        u0, u1, q0, q1, ratio,
    )
    q2, u2, *edges = call(stage_kernel, "stage", [field, field, *sides], [VMEM] * 7, q1, faces, inverse, *halo)
    halo = exchange(*edges)
    middle = call(
        functools.partial(gram_kernel, MIDDLE, 3), "gram_middle", [(len(MIDDLE), ROWS, LANES)], [VMEM] * 7,
        u0, u1, u2, q0, q1, q2, ratio,
    )
    sums = call(
        last_kernel, "last", [(devices, LANES)], [VMEM] * 12,
        q2, faces, inverse, u0, u1, u2, *halo, early, middle,
    )
    gathered = lax.all_to_all(sums, ("gz", "gy"), 0, 0, tiled=True)
    pressure, strain_next, norms = call(
        functools.partial(final_kernel, cell_count), "final", [field, field, (1, 2)], [VMEM] * 7,
        gathered, q0, q1, q2, pressure_iter, strain_change, ratio,
    )
    return pressure, strain_next, norms.reshape(2)


def solution(mesh):
    split = P("gz", "gy", None)
    return jax.shard_map(
        per_device,
        mesh=mesh,
        in_specs=(split,) * 6 + (P(),) * 4,
        out_specs=(split, split, P()),
        check_vma=False,
    )
```

time: 327 us -> 79.7 us (0.24)
  blocking collectives: 168 us -> 10.7 us
  other arithmetic: 52.6 us -> 0 us
  waiting for transfers between devices: 38.5 us -> 5.98 us
  Pallas kernels: 0 us -> 30.9 us
  starting transfers between devices: 49.7 us -> 27.2 us
  between operations: 11.4 us -> 0.78 us
    psum x4 -> x0, blocking collectives: 168 us -> none  [the longest x3 126 us: paired_totals(): lax.psum((jnp.sum(residual * precond), jnp.sum(precond * applied)), ('gz'...]
    ppermute x24 -> x16, waiting for transfers between devices: 38.5 us -> 5.98 us  [the longest x4 5.95 us: exchange(): lax.ppermute(y_high, 'gy', ring('gy', 1))]
    pallas_call x0 -> x8, Pallas kernels: none -> 30.9 us  [call(): pl.pallas_call(kernel, name=name, out_shape=shapes[0] if single else shap...]
    reduce_sum x6 -> x0, other arithmetic: 23.1 us -> none  [the longest x1 13 us: per_device(): jnp.sum(change * change)]
    ppermute x24 -> x16, starting transfers between devices: 49.7 us -> 27.2 us  [the longest x4 15.6 us: exchange(): lax.ppermute(y_low, 'gy', ring('gy', -1))]
    div x2 -> x0, other arithmetic: 19.9 us -> none  [per_device(): precond = residual / diagonal]
    all_to_all x0 -> x1, blocking collectives: none -> 10.7 us  [per_device(): gathered = lax.all_to_all(sums, ('gz', 'gy'), 0, 0, tiled=True)]
    select_n x1 -> x0, other arithmetic: 6.75 us -> none  [lookup(): result = jnp.where(zone_ids == zone_index, zone_table[zone_index], result)]
  transfers between devices with their start and end apart: 24 -> 16, of which waited for: 11 -> 3; matrix products, arithmetic and copies ran while one was open for 3% -> 0% of each run, Pallas kernels for 0% -> 7%
where the time goes in v1:
time: 79.7 us; the launch traced here: 79.5 us
  Pallas kernels  30.9 us (39%)
  starting transfers between devices  27.2 us (34%)
  blocking collectives  10.7 us (13%)
  waiting for transfers between devices  5.98 us (8%)
  local copies, waits for them, and re-layouts  3.81 us (5%)
    pallas_call x8, Pallas kernels, call(): pl.pallas_call(kernel, name=name, out_shape=shapes[0] if single else shap...  30.9 us
    ppermute x4, starting transfers between devices, exchange(): lax.ppermute(y_low, 'gy', ring('gy', -1))  15.6 us
    all_to_all x1, blocking collectives, per_device(): gathered = lax.all_to_all(sums, ('gz', 'gy'), 0, 0, tiled=True)  10.7 us
    ppermute x4, starting transfers between devices, exchange(): lax.ppermute(z_low, 'gz', ring('gz', -1))  7.15 us
    ppermute x4, waiting for transfers between devices, exchange(): lax.ppermute(y_high, 'gy', ring('gy', 1))  5.95 us
    ppermute x4, starting transfers between devices, exchange(): lax.ppermute(y_high, 'gy', ring('gy', 1))  3.91 us
    unnamed x32, local copies, waits for them, and re-layouts  3.81 us
  transfers between devices with their start and end apart: 16, of which 3 were waited for; matrix products, arithmetic and copies ran while one was open for 0% of the time, Pallas kernels for 7%

profile of v1, /device:TPU:0, one launch (start us, length us, event | category | flops | bytes accessed | tf_op | source)
XLA Modules:
  0.0 79.5 jit_solution(8611261770312023759)
XLA Ops:
  0.6 2.0 %pack.1 = (f32[2,32,512]{2,1,0:T(8,128)}, f32[2,32,512]{2,1,0:T(8,128)}, f32[2,8,512]{2,1,0:T(8,128)}, f32[2,8,512]{2,1,0:T(8,128)}) custom-call(s32[8,32,512]{2,1,0:T(8,128)} %zone_ref.3, f32[8,32,512]{2,1,0:T(8,128)} %pressure_ref.5, f32[8]{0:T(128)} %perm_table.3), custom_call_target="tpu_custom_call" | custom-call | tf_op jit(solution)/shard_map/pack/pallas_call | solution.py:344
  2.7 0.5 collective-permute-start
  3.2 1.9 %collective-permute-start.1 = (f32[2,32,512]{2,1,0:T(8,128)}, f32[2,32,512]{2,1,0:T(8,128)S(1)}, u32[]{:S(2)}, u32[]{:S(2)}) collective-permute-start(f32[2,32,512]{2,1,0:T(8,128)} %get-tuple-element.32), channel_id=1, source_target_pairs={{0,24},{8,0},{16,8},{24,16},{1,25},{9,1},{17,9},{25,17},{2,26},{10... | collective-permute-start | bytes 393224 | tf_op jit(solution)/shard_map/ppermute | solution.py:335
  5.1 2.3 %collective-permute-start.2 = (f32[2,8,512]{2,1,0:T(8,128)}, f32[2,8,512]{2,1,0:T(8,128)S(1)}, u32[]{:S(2)}, u32[]{:S(2)}) collective-permute-start(f32[2,8,512]{2,1,0:T(8,128)} %get-tuple-element.33), channel_id=1, source_target_pairs={{0,1},{1,2},{2,3},{3,4},{4,5},{5,6},{6,7},{7,0},{8,9},{9,10},{10,1... | collective-permute-start | bytes 98312 | tf_op jit(solution)/shard_map/ppermute | solution.py:336
  7.4 3.0 %collective-permute-start.3 = (f32[2,8,512]{2,1,0:T(8,128)}, f32[2,8,512]{2,1,0:T(8,128)S(1)}, u32[]{:S(2)}, u32[]{:S(2)}) collective-permute-start(f32[2,8,512]{2,1,0:T(8,128)} %get-tuple-element.34), channel_id=1, source_target_pairs={{0,7},{1,0},{2,1},{3,2},{4,3},{5,4},{6,5},{7,6},{8,15},{9,8},{10,9... | collective-permute-start | bytes 98312 | tf_op jit(solution)/shard_map/ppermute | solution.py:337
  10.5 2.1 %collective-permute-done.2.below_y = f32[2,8,512]{2,1,0:T(8,128)S(1)} collective-permute-done((f32[2,8,512]{2,1,0:T(8,128)}, f32[2,8,512]{2,1,0:T(8,128)S(1)}, u32[]{:S(2)}, u32[]{:S(2)}) %collective-permute-start.2) | collective-permute-done | bytes 32800 | tf_op jit(solution)/shard_map/ppermute | solution.py:336
  12.6 0.0 collective-permute-done.below_z
  12.6 0.6 copy-done.8
  13.2 0.0 copy-done.9
  13.2 0.1 copy-done
  13.2 0.7 copy-done.1
  13.9 7.7 %setup.1 = (f32[6,8,32,512]{3,2,1,0:T(8,128)}, f32[8,32,512]{2,1,0:T(8,128)}, f32[8,32,512]{2,1,0:T(8,128)}, f32[8,32,512]{2,1,0:T(8,128)}, f32[8,32,512]{2,1,0:...) custom-call(s32[8,32,512]{2,1,0:T(8,128)} %zone_ref.3, ...), custom_call_target="tpu_custom_call" | custom-call | tf_op jit(solution)/shard_map/setup/pallas_call | solution.py:344
  21.6 0.1 collective-permute-start.4
  21.6 1.7 %collective-permute-start.5 = (f32[32,512]{1,0:T(8,128)}, f32[32,512]{1,0:T(8,128)S(1)}, u32[]{:S(2)}, u32[]{:S(2)}) collective-permute-start(f32[32,512]{1,0:T(8,128)} %get-tuple-element.39), channel_id=1, source_target_pairs={{0,24},{8,0},{16,8},{24,16},{1,25},{9,1},{17,9},{25,17},{2,26},{10... | collective-permute-start | bytes 196616 | tf_op jit(solution)/shard_map/ppermute | solution.py:335
  23.4 1.4 %collective-permute-start.6 = (f32[8,512]{1,0:T(8,128)}, f32[8,512]{1,0:T(8,128)S(1)}, u32[]{:S(2)}, u32[]{:S(2)}) collective-permute-start(f32[8,512]{1,0:T(8,128)} %get-tuple-element.40), channel_id=1, source_target_pairs={{0,1},{1,2},{2,3},{3,4},{4,5},{5,6},{6,7},{7,0},{8,9},{9,10},{10,1... | collective-permute-start | bytes 49160 | tf_op jit(solution)/shard_map/ppermute | solution.py:336
  24.8 3.3 %collective-permute-start.7 = (f32[8,512]{1,0:T(8,128)}, f32[8,512]{1,0:T(8,128)S(1)}, u32[]{:S(2)}, u32[]{:S(2)}) collective-permute-start(f32[8,512]{1,0:T(8,128)} %get-tuple-element.41), channel_id=1, source_target_pairs={{0,7},{1,0},{2,1},{3,2},{4,3},{5,4},{6,5},{7,6},{8,15},{9,8},{10,9... | collective-permute-start | bytes 49160 | tf_op jit(solution)/shard_map/ppermute | solution.py:337
  28.1 1.9 %collective-permute-done.6.below_y = f32[8,512]{1,0:T(8,128)S(1)} collective-permute-done((f32[8,512]{1,0:T(8,128)}, f32[8,512]{1,0:T(8,128)S(1)}, u32[]{:S(2)}, u32[]{:S(2)}) %collective-permute-start.6) | collective-permute-done | bytes 16416 | tf_op jit(solution)/shard_map/ppermute | solution.py:336
  30.0 0.0 collective-permute-done.7.above_y
  30.0 0.0 collective-permute-done.4.below_z
  30.1 0.0 collective-permute-done.5.above_z
  30.1 0.6 copy-done.12
  30.6 0.0 copy-done.14
  30.6 0.0 copy-done.4
  30.7 0.0 copy-done.6
  30.7 4.1 %stage.2 = (f32[8,32,512]{2,1,0:T(8,128)}, f32[8,32,512]{2,1,0:T(8,128)}, f32[32,512]{1,0:T(8,128)}, f32[32,512]{1,0:T(8,128)}, f32[8,512]{1,0:T(8,128)}, /*index=5*/f32[8,512]{1,0:T(8,128)}) custom-call(f32[8,32,512]{2,1,0:T(8,128)} %get-tuple-element.35.q_ref.refs_2_.refs_3_.q0, f32[6,8,32,512]{3,2,1,0:T(8,128)} %get-tuple-element.36.faces, ...), custom_call_target="tpu_custom_call" | custom-call | tf_op jit(solution)/shard_map/stage/pallas_call | solution.py:344
  34.8 1.7 %collective-permute-start.9 = (f32[32,512]{1,0:T(8,128)}, f32[32,512]{1,0:T(8,128)S(1)}, u32[]{:S(2)}, u32[]{:S(2)}) collective-permute-start(f32[32,512]{1,0:T(8,128)} %get-tuple-element.44), channel_id=1, source_target_pairs={{0,24},{8,0},{16,8},{24,16},{1,25},{9,1},{17,9},{25,17},{2,26},{10... | collective-permute-start | bytes 196616 | tf_op jit(solution)/shard_map/ppermute | solution.py:335
  36.5 0.2 collective-permute-start.10
  36.7 4.5 %collective-permute-start.11 = (f32[8,512]{1,0:T(8,128)}, f32[8,512]{1,0:T(8,128)S(1)}, u32[]{:S(2)}, u32[]{:S(2)}) collective-permute-start(f32[8,512]{1,0:T(8,128)} %get-tuple-element.46), channel_id=1, source_target_pairs={{0,7},{1,0},{2,1},{3,2},{4,3},{5,4},{6,5},{7,6},{8,15},{9,8},{10,9... | collective-permute-start | bytes 49160 | tf_op jit(solution)/shard_map/ppermute | solution.py:337
  41.2 1.9 %collective-permute-done.10.below_y = f32[8,512]{1,0:T(8,128)S(1)} collective-permute-done((f32[8,512]{1,0:T(8,128)}, f32[8,512]{1,0:T(8,128)S(1)}, u32[]{:S(2)}, u32[]{:S(2)}) %collective-permute-start.10) | collective-permute-done | bytes 16416 | tf_op jit(solution)/shard_map/ppermute | solution.py:336
  43.2 0.0 collective-permute-done.11.above_y
  43.2 0.0 collective-permute-done.8.below_z
  43.2 0.0 collective-permute-done.9.above_z
  43.2 0.6 copy-done.13
  43.8 0.0 copy-done.15
  43.8 0.0 copy-done.5
  43.8 0.0 copy-done.7
  43.8 4.1 %stage.3 = (f32[8,32,512]{2,1,0:T(8,128)}, f32[8,32,512]{2,1,0:T(8,128)}, f32[32,512]{1,0:T(8,128)}, f32[32,512]{1,0:T(8,128)}, f32[8,512]{1,0:T(8,128)}, /*index=5*/f32[8,512]{1,0:T(8,128)}) custom-call(f32[8,32,512]{2,1,0:T(8,128)} %get-tuple-element.42.q_ref.refs_3_.refs_4_.q1, f32[6,8,32,512]{3,2,1,0:T(8,128)} %get-tuple-element.36.faces, ...), custom_call_target="tpu_custom_call" | custom-call | tf_op jit(solution)/shard_map/stage/pallas_call | solution.py:344
  47.9 1.7 %collective-permute-start.13 = (f32[32,512]{1,0:T(8,128)}, f32[32,512]{1,0:T(8,128)S(1)}, u32[]{:S(2)}, u32[]{:S(2)}) collective-permute-start(f32[32,512]{1,0:T(8,128)} %get-tuple-element.52), channel_id=1, source_target_pairs={{0,24},{8,0},{16,8},{24,16},{1,25},{9,1},{17,9},{25,17},{2,26},{10... | collective-permute-start | bytes 196616 | tf_op jit(solution)/shard_map/ppermute | solution.py:335
  49.6 4.7 %collective-permute-start.15 = (f32[8,512]{1,0:T(8,128)}, f32[8,512]{1,0:T(8,128)S(1)}, u32[]{:S(2)}, u32[]{:S(2)}) collective-permute-start(f32[8,512]{1,0:T(8,128)} %get-tuple-element.54), channel_id=1, source_target_pairs={{0,7},{1,0},{2,1},{3,2},{4,3},{5,4},{6,5},{7,6},{8,15},{9,8},{10,9... | collective-permute-start | bytes 49160 | tf_op jit(solution)/shard_map/ppermute | solution.py:337
  54.4 2.6 %gram_early.1.early = f32[9,8,128]{2,1,0:T(8,128)} custom-call(f32[8,32,512]{2,1,0:T(8,128)} %get-tuple-element.48.refs_0_.u0_ref, f32[8,32,512]{2,1,0:T(8,128)} %get-tuple-element.49.refs_1_.u1_ref, f32[8,32,512]{2,1,0:T(8,128)} %get-tuple-element.35.q_ref.refs_2_.refs_3_.q0, f32[8,32,512]{2,1,0:T(8,128)} %get-tuple-element.42.q_ref.refs_3_.refs_4_.q1, ...), custom_call_target="tpu_custom_call" | custom-call | tf_op jit(solution)/shard_map/gram_early/pallas_call | solution.py:344
  57.0 3.0 %gram_middle.1.middle = f32[8,8,128]{2,1,0:T(8,128)} custom-call(f32[8,32,512]{2,1,0:T(8,128)} %get-tuple-element.48.refs_0_.u0_ref, f32[8,32,512]{2,1,0:T(8,128)} %get-tuple-element.49.refs_1_.u1_ref, f32[8,32,512]{2,1,0:T(8,128)} %get-tuple-element.50.refs_2_.u2_ref, f32[8,32,512]{2,1,0:T(8,128)} %get-tuple-element.35.q_ref.refs_2_.refs_3_.q0, ...), custom_call_target="tpu_custom_call" | custom-call | tf_op jit(solution)/shard_map/gram_middle/pallas_call | solution.py:344
  60.0 0.6 copy-done.10
  60.6 0.0 copy-done.11
  60.6 0.1 copy-done.2
  60.6 0.6 copy-done.3
  61.3 4.3 %last.1 = f32[32,128]{1,0:T(8,128)} custom-call(f32[8,32,512]{2,1,0:T(8,128)} %get-tuple-element.47.refs_5_.q2_ref.q2, f32[6,8,32,512]{3,2,1,0:T(8,128)} %get-tuple-element.36.faces, f32[8,32,512]{2,1,0:T(8,128)} %get-tuple-element.37.inverse, f32[8,32,512]{2,1,0:T(8,128)} %get-tuple-element.48.refs_0_.u0_ref, ...), custom_call_target="tpu_custom_call" | custom-call | tf_op jit(solution)/shard_map/last/pallas_call | solution.py:344
  65.5 10.7 %all_to_all.11 = f32[32,1,128]{2,1,0:T(1,128)} all-to-all(f32[32,1,128]{2,1,0:T(1,128)} %bitcast.5), channel_id=1, replica_groups=mesh['gz'=4,'gy'=8] {'gz','gy'}, dimensions={0} | all-to-all | bytes 32768 | tf_op jit(solution)/shard_map/all_to_all | solution.py:392
  76.3 3.2 %final.1 = (f32[8,32,512]{2,1,0:T(8,128)}, f32[8,32,512]{2,1,0:T(8,128)}, f32[1,2]{1,0:T(1,128)}) custom-call(f32[32,128]{1,0:T(8,128)} %bitcast.6, f32[8,32,512]{2,1,0:T(8,128)} %get-tuple-element.35.q_ref.refs_2_.refs_3_.q0, f32[8,32,512]{2,1,0:T(8,128)} %get-tuple-element.42.q_ref.refs_3_.refs_4_.q1, f32[8,32,512]{2,1,0:T(8,128)} %get-tuple-element.47.refs_5_.q2_ref.q2, ...), custom_call_target="tpu_custom_call" | custom-call | tf_op jit(solution)/shard_map/final/pallas_call | solution.py:344
  (25 shorter events, 0.1 us)
Async XLA Ops:
  2.7 9.9 %collective-permute-start = (f32[2,32,512]{2,1,0:T(8,128)}, f32[2,32,512]{2,1,0:T(8,128)S(1)}, u32[]{:S(2)}, u32[]{:S(2)}) collective-permute-start(f32[2,32,512]{2,1,0:T(8,128)} %get-tuple-element.31), channel_id=1, source_target_pairs={{0,8},{8,16},{16,24},{24,0},{1,9},{9,17},{17,25},{25,1},{2,10},{10... | collective-permute-start | bytes 393224 | tf_op jit(solution)/shard_map/ppermute | solution.py:334
  3.2 9.4 %collective-permute-start.1 = (f32[2,32,512]{2,1,0:T(8,128)}, f32[2,32,512]{2,1,0:T(8,128)S(1)}, u32[]{:S(2)}, u32[]{:S(2)}) collective-permute-start(f32[2,32,512]{2,1,0:T(8,128)} %get-tuple-element.32), channel_id=1, source_target_pairs={{0,24},{8,0},{16,8},{24,16},{1,25},{9,1},{17,9},{25,17},{2,26},{10... | collective-permute-start | bytes 393224 | tf_op jit(solution)/shard_map/ppermute | solution.py:335
  5.1 7.5 %collective-permute-start.2 = (f32[2,8,512]{2,1,0:T(8,128)}, f32[2,8,512]{2,1,0:T(8,128)S(1)}, u32[]{:S(2)}, u32[]{:S(2)}) collective-permute-start(f32[2,8,512]{2,1,0:T(8,128)} %get-tuple-element.33), channel_id=1, source_target_pairs={{0,1},{1,2},{2,3},{3,4},{4,5},{5,6},{6,7},{7,0},{8,9},{9,10},{10,1... | collective-permute-start | bytes 98312 | tf_op jit(solution)/shard_map/ppermute | solution.py:336
  7.4 5.1 %collective-permute-start.3 = (f32[2,8,512]{2,1,0:T(8,128)}, f32[2,8,512]{2,1,0:T(8,128)S(1)}, u32[]{:S(2)}, u32[]{:S(2)}) collective-permute-start(f32[2,8,512]{2,1,0:T(8,128)} %get-tuple-element.34), channel_id=1, source_target_pairs={{0,7},{1,0},{2,1},{3,2},{4,3},{5,4},{6,5},{7,6},{8,15},{9,8},{10,9... | collective-permute-start | bytes 98312 | tf_op jit(solution)/shard_map/ppermute | solution.py:337
  12.6 0.6 copy-start.8
  12.6 0.6 copy-start.9
  12.6 0.7 copy-start
  13.2 0.7 copy-start.1
  21.6 8.5 %collective-permute-start.4 = (f32[32,512]{1,0:T(8,128)}, f32[32,512]{1,0:T(8,128)S(1)}, u32[]{:S(2)}, u32[]{:S(2)}) collective-permute-start(f32[32,512]{1,0:T(8,128)} %get-tuple-element.38), channel_id=1, source_target_pairs={{0,8},{8,16},{16,24},{24,0},{1,9},{9,17},{17,25},{25,1},{2,10},{10... | collective-permute-start | bytes 196616 | tf_op jit(solution)/shard_map/ppermute | solution.py:334
  21.6 8.4 %collective-permute-start.5 = (f32[32,512]{1,0:T(8,128)}, f32[32,512]{1,0:T(8,128)S(1)}, u32[]{:S(2)}, u32[]{:S(2)}) collective-permute-start(f32[32,512]{1,0:T(8,128)} %get-tuple-element.39), channel_id=1, source_target_pairs={{0,24},{8,0},{16,8},{24,16},{1,25},{9,1},{17,9},{25,17},{2,26},{10... | collective-permute-start | bytes 196616 | tf_op jit(solution)/shard_map/ppermute | solution.py:335
  23.4 6.6 %collective-permute-start.6 = (f32[8,512]{1,0:T(8,128)}, f32[8,512]{1,0:T(8,128)S(1)}, u32[]{:S(2)}, u32[]{:S(2)}) collective-permute-start(f32[8,512]{1,0:T(8,128)} %get-tuple-element.40), channel_id=1, source_target_pairs={{0,1},{1,2},{2,3},{3,4},{4,5},{5,6},{6,7},{7,0},{8,9},{9,10},{10,1... | collective-permute-start | bytes 49160 | tf_op jit(solution)/shard_map/ppermute | solution.py:336
  24.8 5.3 %collective-permute-start.7 = (f32[8,512]{1,0:T(8,128)}, f32[8,512]{1,0:T(8,128)S(1)}, u32[]{:S(2)}, u32[]{:S(2)}) collective-permute-start(f32[8,512]{1,0:T(8,128)} %get-tuple-element.41), channel_id=1, source_target_pairs={{0,7},{1,0},{2,1},{3,2},{4,3},{5,4},{6,5},{7,6},{8,15},{9,8},{10,9... | collective-permute-start | bytes 49160 | tf_op jit(solution)/shard_map/ppermute | solution.py:337
  30.0 0.6 copy-start.12
  30.0 0.6 copy-start.14
  30.0 0.6 copy-start.4
  30.1 0.6 copy-start.6
  34.8 8.4 %collective-permute-start.8 = (f32[32,512]{1,0:T(8,128)}, f32[32,512]{1,0:T(8,128)S(1)}, u32[]{:S(2)}, u32[]{:S(2)}) collective-permute-start(f32[32,512]{1,0:T(8,128)} %get-tuple-element.43), channel_id=1, source_target_pairs={{0,8},{8,16},{16,24},{24,0},{1,9},{9,17},{17,25},{25,1},{2,10},{10... | collective-permute-start | bytes 196616 | tf_op jit(solution)/shard_map/ppermute | solution.py:334
  34.8 8.4 %collective-permute-start.9 = (f32[32,512]{1,0:T(8,128)}, f32[32,512]{1,0:T(8,128)S(1)}, u32[]{:S(2)}, u32[]{:S(2)}) collective-permute-start(f32[32,512]{1,0:T(8,128)} %get-tuple-element.44), channel_id=1, source_target_pairs={{0,24},{8,0},{16,8},{24,16},{1,25},{9,1},{17,9},{25,17},{2,26},{10... | collective-permute-start | bytes 196616 | tf_op jit(solution)/shard_map/ppermute | solution.py:335
  36.5 6.6 %collective-permute-start.10 = (f32[8,512]{1,0:T(8,128)}, f32[8,512]{1,0:T(8,128)S(1)}, u32[]{:S(2)}, u32[]{:S(2)}) collective-permute-start(f32[8,512]{1,0:T(8,128)} %get-tuple-element.45), channel_id=1, source_target_pairs={{0,1},{1,2},{2,3},{3,4},{4,5},{5,6},{6,7},{7,0},{8,9},{9,10},{10,1... | collective-permute-start | bytes 49160 | tf_op jit(solution)/shard_map/ppermute | solution.py:336
  36.7 6.4 %collective-permute-start.11 = (f32[8,512]{1,0:T(8,128)}, f32[8,512]{1,0:T(8,128)S(1)}, u32[]{:S(2)}, u32[]{:S(2)}) collective-permute-start(f32[8,512]{1,0:T(8,128)} %get-tuple-element.46), channel_id=1, source_target_pairs={{0,7},{1,0},{2,1},{3,2},{4,3},{5,4},{6,5},{7,6},{8,15},{9,8},{10,9... | collective-permute-start | bytes 49160 | tf_op jit(solution)/shard_map/ppermute | solution.py:337
  43.2 0.6 copy-start.13
  43.2 0.6 copy-start.15
  43.2 0.6 copy-start.5
  43.2 0.6 copy-start.7
  47.9 12.1 %collective-permute-start.12 = (f32[32,512]{1,0:T(8,128)}, f32[32,512]{1,0:T(8,128)S(1)}, u32[]{:S(2)}, u32[]{:S(2)}) collective-permute-start(f32[32,512]{1,0:T(8,128)} %get-tuple-element.51), channel_id=1, source_target_pairs={{0,8},{8,16},{16,24},{24,0},{1,9},{9,17},{17,25},{25,1},{2,10},{10... | collective-permute-start | bytes 196616 | tf_op jit(solution)/shard_map/ppermute | solution.py:334
  47.9 12.1 %collective-permute-start.13 = (f32[32,512]{1,0:T(8,128)}, f32[32,512]{1,0:T(8,128)S(1)}, u32[]{:S(2)}, u32[]{:S(2)}) collective-permute-start(f32[32,512]{1,0:T(8,128)} %get-tuple-element.52), channel_id=1, source_target_pairs={{0,24},{8,0},{16,8},{24,16},{1,25},{9,1},{17,9},{25,17},{2,26},{10... | collective-permute-start | bytes 196616 | tf_op jit(solution)/shard_map/ppermute | solution.py:335
  49.6 10.3 %collective-permute-start.14 = (f32[8,512]{1,0:T(8,128)}, f32[8,512]{1,0:T(8,128)S(1)}, u32[]{:S(2)}, u32[]{:S(2)}) collective-permute-start(f32[8,512]{1,0:T(8,128)} %get-tuple-element.53), channel_id=1, source_target_pairs={{0,1},{1,2},{2,3},{3,4},{4,5},{5,6},{6,7},{7,0},{8,9},{9,10},{10,1... | collective-permute-start | bytes 49160 | tf_op jit(solution)/shard_map/ppermute | solution.py:336
  49.6 10.3 %collective-permute-start.15 = (f32[8,512]{1,0:T(8,128)}, f32[8,512]{1,0:T(8,128)S(1)}, u32[]{:S(2)}, u32[]{:S(2)}) collective-permute-start(f32[8,512]{1,0:T(8,128)} %get-tuple-element.54), channel_id=1, source_target_pairs={{0,7},{1,0},{2,1},{3,2},{4,3},{5,4},{6,5},{7,6},{8,15},{9,8},{10,9... | collective-permute-start | bytes 49160 | tf_op jit(solution)/shard_map/ppermute | solution.py:337
  60.0 0.6 copy-start.10
  60.0 0.6 copy-start.11
  60.0 0.6 copy-start.2
  60.6 0.6 copy-start.3

commit v2 on v1

v2 whole, which is shorter than its diff:
```python
import functools

import jax
import jax.numpy as jnp
from jax import lax
from jax.experimental import pallas as pl
from jax.experimental.pallas import tpu as pltpu
from jax.sharding import PartitionSpec as P

F32 = jnp.float32
ROWS = 8
LANES = 128
VMEM = pl.BlockSpec(memory_space=pltpu.VMEM)
HBM = pl.BlockSpec(memory_space=pltpu.HBM)

MOMENTS = (("q", 0, "u", 0), ("q", 0, "u", 1), ("q", 1, "u", 1), ("q", 1, "u", 2), ("q", 2, "u", 2), ("q", 2, "u", 3))
CLOSING = tuple(("u", i, "u", j) for i in range(4) for j in range(i, 4))
CHANGE = tuple(("y", i, "y", j) for i in range(3) for j in range(i, 3))
SUMS = MOMENTS + CLOSING + CHANGE
EARLY = tuple(s for s in SUMS if max(s[1], s[3]) <= 1)
MIDDLE = tuple(s for s in SUMS if max(s[1], s[3]) == 2)
LATE = tuple(s for s in SUMS if max(s[1], s[3]) == 3)


def table_row(table_ref):
    lane = lax.broadcasted_iota(jnp.int32, (ROWS, LANES), 1)
    row = jnp.zeros((ROWS, LANES), F32)
    for zone in range(table_ref.shape[0]):
        row = jnp.where(lane == zone, table_ref[zone], row)
    return row


def look_up(row, zones):
    parts = [
        jnp.take_along_axis(row, zones[:, at : at + LANES], axis=1, mode="promise_in_bounds")
        for at in range(0, zones.shape[1], LANES)
    ]
    return jnp.concatenate(parts, axis=1)


def harmonic(lower_side, upper_side):
    return 2.0 * lower_side * upper_side / (lower_side + upper_side)


def row_shifts(tiles, before, after):
    sub = lax.broadcasted_iota(jnp.int32, tiles[0].shape, 0)
    down = [pltpu.roll(tile, 1, 0) for tile in tiles]
    up = [pltpu.roll(tile, ROWS - 1, 0) for tile in tiles]
    lower, upper = [], []
    for at in range(len(tiles)):
        lower.append(jnp.where(sub == 0, down[at - 1] if at else before, down[at]))
        upper.append(jnp.where(sub == ROWS - 1, up[at + 1] if at + 1 < len(tiles) else after, up[at]))
    return lower, upper


def lane_shifts(tile):
    width = tile.shape[1]
    return pltpu.roll(tile, 1, 1), pltpu.roll(tile, width - 1, 1)


def paired(count_z, count_y):
    return count_z % 2 == 0 and count_y % 2 == 0


def to_send(low, high):
    if not paired(lax.axis_size("gz"), lax.axis_size("gy")):
        return high, low
    odd = lax.rem(lax.axis_index("gy"), 2) == 1
    return jnp.where(odd, low, high), jnp.where(odd, high, low)


def as_sides(first, second):
    if not paired(lax.axis_size("gz"), lax.axis_size("gy")):
        return first, second
    odd = lax.rem(lax.axis_index("gy"), 2) == 1
    return jnp.where(odd, first, second), jnp.where(odd, second, first)


def inside_flags():
    flags = []
    for axis in ("gz", "gy"):
        place = lax.axis_index(axis)
        flags += [place > 0, place < lax.axis_size(axis) - 1]
    return [jnp.where(flag, 1.0, 0.0).astype(F32) for flag in flags]


def row_parts(rows):
    return [pl.ds(at, ROWS) for at in range(0, rows, ROWS)]


def pack_kernel(
    zone_hbm, pressure_hbm, perm_hbm, z_low, z_high, y_first, y_second, zone_z, zone_y, pressure_y, perm_table, sems
):
    planes, rows, _ = zone_hbm.shape
    ends = ((0, pl.ds(0, ROWS)), (planes - 1, pl.ds(rows - ROWS, ROWS)))
    copies = [pltpu.make_async_copy(perm_hbm, perm_table, sems.at[8])]
    for side, (plane, part) in enumerate(ends):
        out = (z_low, z_high)[side]
        for source, target in (
            (zone_hbm.at[plane], zone_z.at[side]),
            (pressure_hbm.at[plane], out.at[1]),
            (zone_hbm.at[:, part], zone_y.at[side]),
            (pressure_hbm.at[:, part], pressure_y.at[side]),
        ):
            copies.append(pltpu.make_async_copy(source, target, sems.at[len(copies) - 1]))
    for copy in copies:
        copy.start()
    copies[0].wait()
    perm_row = table_row(perm_table)
    for copy in copies[1:]:
        copy.wait()
    faces_y = []
    for side, out in enumerate((z_low, z_high)):
        for part in row_parts(rows):
            out[0, part] = look_up(perm_row, zone_z[side, part])
        row = pl.ds((0, ROWS - 1)[side], 1)
        zones = jnp.concatenate([zone_y[side, plane, row] for plane in range(planes)], axis=0)
        values = jnp.concatenate([pressure_y[side, plane, row] for plane in range(planes)], axis=0)
        faces_y.append((look_up(perm_row, zones), values))
    for number in range(2):
        y_first[number], y_second[number] = to_send(faces_y[0][number], faces_y[1][number])


def prepare_kernel(
    zone_hbm, fixed_hbm, old_hbm, pressure_hbm, strain_hbm, source_hbm,
    perm_hbm, storage_hbm, biot_hbm, bulk_hbm,
    faces, perm, diagonal_out, residual_out, free_out, ratio, pressure, strain,
    zone, fixed, old, source, perm_table, storage_table, biot_table, bulk_table, sems,
):
    planes, rows, width = zone_hbm.shape
    pairs = (
        (perm_hbm, perm_table), (storage_hbm, storage_table), (biot_hbm, biot_table), (bulk_hbm, bulk_table),
        (zone_hbm, zone), (pressure_hbm, pressure), (old_hbm, old), (strain_hbm, strain), (source_hbm, source),
        (fixed_hbm, fixed),
    )
    copies = [pltpu.make_async_copy(*pair, sems.at[number]) for number, pair in enumerate(pairs)]
    for copy in copies:
        copy.start()
    for copy in copies[:4]:
        copy.wait()
    perm_row = table_row(perm_table)
    storage_row = table_row(storage_table)
    biot_row = table_row(biot_table)
    known = lax.broadcasted_iota(jnp.int32, (ROWS, LANES), 1) < bulk_table.shape[0]
    bulk_row = jnp.where(known, table_row(bulk_table), 1.0)
    ratio_row = biot_row / bulk_row
    coupling_row = biot_row * biot_row / bulk_row
    lane = lax.broadcasted_iota(jnp.int32, (ROWS, width), 1)
    copies[4].wait()

    def fill(z, carry):
        for part in row_parts(rows):
            perm[z, part] = look_up(perm_row, zone[z, part])
        return carry

    lax.fori_loop(0, planes, fill, 0)
    for copy in copies[5:]:
        copy.wait()
    closed = jnp.zeros((ROWS, width), F32)

    def plane(z, low, high):
        parts = row_parts(rows)
        perms = [perm[z, part] for part in parts]
        values = [pressure[z, part] for part in parts]
        perm_lower, perm_upper = row_shifts(perms, closed, closed)
        value_lower, value_upper = row_shifts(values, closed, closed)
        for at, part in enumerate(parts):
            zones = zone[z, part]
            storage = look_up(storage_row, zones)
            coupling = look_up(coupling_row, zones)
            biot = look_up(biot_row, zones)
            ratio[z, part] = look_up(ratio_row, zones)
            here, value = perms[at], values[at]
            x_lower, x_upper = lane_shifts(here)
            x_lower = jnp.where(lane == 0, 0.0, x_lower)
            x_upper = jnp.where(lane == width - 1, 0.0, x_upper)
            value_left, value_right = lane_shifts(value)
            beside = (
                closed if low is None else perm[low, part], closed if high is None else perm[high, part],
                perm_lower[at], perm_upper[at], x_lower, x_upper,
            )
            views = (
                closed if low is None else pressure[low, part], closed if high is None else pressure[high, part],
                value_lower[at], value_upper[at], value_left, value_right,
            )
            terms = [harmonic(here, other) for other in beside]
            free = 1.0 - fixed[z, part].astype(F32)
            diagonal = storage + coupling
            for term in terms:
                diagonal = diagonal + term
            neighbours = terms[0] * views[0]
            for number in range(1, 6):
                neighbours = neighbours + terms[number] * views[number]
            right_side = storage * old[z, part] + coupling * value - biot * strain[z, part] + source[z, part]
            for number in range(6):
                faces[number, z, part] = free * terms[number]
            diagonal_out[z, part] = diagonal
            residual_out[z, part] = right_side - (diagonal * value - neighbours)
            free_out[z, part] = free

    plane(0, None, 1)
    lax.fori_loop(1, planes - 1, lambda z, c: (plane(z, z - 1, z + 1), c)[1], 0)
    plane(planes - 1, planes - 2, None)


def begin_kernel(
    perm, diagonal_ref, residual_ref, free_ref, pressure, below_z, above_z, y_got, y_got_too,
    inverse, q_out, u_out, face_z, face_y, z_low, z_high, y_first, y_second,
    y_low, y_high,
):
    planes, rows, width = pressure.shape
    inside = inside_flags()
    below_perm, above_perm = as_sides(y_got[0], y_got_too[0])
    below_value, above_value = as_sides(y_got[1], y_got_too[1])
    below_perm, above_perm = below_perm * inside[2], above_perm * inside[3]
    sub = lax.broadcasted_iota(jnp.int32, (ROWS, width), 0)
    ends = (
        (pl.ds(0, 1), below_perm, below_value),
        (pl.ds(rows - 1, 1), above_perm, above_value),
    )
    gain_y = []
    for side, (row, other, value) in enumerate(ends):
        here = jnp.concatenate([perm[z, row] for z in range(planes)], axis=0)
        own = jnp.concatenate([pressure[z, row] for z in range(planes)], axis=0)
        free = jnp.concatenate([free_ref[z, row] for z in range(planes)], axis=0)
        term = harmonic(here, other)
        face_y[side] = free * term
        gain_y.append((term, term * (value - own)))

    def plane(z, outer):
        for part in row_parts(rows):
            diagonal, residual, free = diagonal_ref[z, part], residual_ref[z, part], free_ref[z, part]
            if outer is not None:
                side, halo = outer
                term = harmonic(perm[z, part], halo[0, part] * inside[side])
                diagonal = diagonal + term
                residual = residual + term * (halo[1, part] - pressure[z, part])
                face_z[side, part] = free * term
            for side, tile, row in ((0, 0, 0), (1, rows - ROWS, ROWS - 1)):
                if part.start == tile:
                    term, gain = (jnp.broadcast_to(value[z : z + 1], (ROWS, width)) for value in gain_y[side])
                    diagonal = diagonal + jnp.where(sub == row, term, 0.0)
                    residual = residual + jnp.where(sub == row, gain, 0.0)
            reciprocal = 1.0 / diagonal
            residual = free * residual
            precond = residual * reciprocal
            inverse[z, part] = reciprocal
            u_out[z, part] = residual
            q_out[z, part] = precond
            if part.start == 0:
                y_low[z : z + 1] = precond[:1]
            if part.start == rows - ROWS:
                y_high[z : z + 1] = precond[ROWS - 1 :]

    for z in range(planes):
        plane(z, (0, below_z) if z == 0 else (1, above_z) if z == planes - 1 else None)
    z_low[...] = q_out[0]
    z_high[...] = q_out[planes - 1]
    y_first[...], y_second[...] = to_send(y_low[...], y_high[...])


def apply_planes(q_ref, faces, face_z, face_y, below_z, above_z, y_got, y_got_too, emit, carry):
    planes, rows, width = q_ref.shape
    parts = row_parts(rows)
    below_y, above_y = as_sides(y_got[...], y_got_too[...])
    gain = (face_y[0] * below_y, face_y[1] * above_y)
    sub = lax.broadcasted_iota(jnp.int32, (ROWS, width), 0)
    closed = jnp.zeros((ROWS, width), F32)
    for z in range(planes):
        values = [q_ref[z, part] for part in parts]
        lower, upper = row_shifts(values, closed, closed)
        for at, part in enumerate(parts):
            left, right = lane_shifts(values[at])
            if z == 0:
                u = face_z[0, part] * below_z[part] + faces[1, z, part] * q_ref[z + 1, part]
            elif z == planes - 1:
                u = faces[0, z, part] * q_ref[z - 1, part] + face_z[1, part] * above_z[part]
            else:
                u = faces[0, z, part] * q_ref[z - 1, part] + faces[1, z, part] * q_ref[z + 1, part]
            u = u + faces[2, z, part] * lower[at] + faces[3, z, part] * upper[at]
            u = u + faces[4, z, part] * left + faces[5, z, part] * right
            for side, tile, row in ((0, 0, 0), (1, rows - ROWS, ROWS - 1)):
                if part.start == tile:
                    u = u + jnp.where(sub == row, jnp.broadcast_to(gain[side][z : z + 1], (ROWS, width)), 0.0)
            carry = emit(z, part, u, carry)
    return carry


def stage_kernel(
    q_ref, faces, face_z, face_y, inverse, below_z, above_z, y_got, y_got_too,
    q_out, u_out, z_low, z_high, y_first, y_second,
    y_low, y_high,
):
    planes, rows, _ = q_ref.shape

    def emit(z, part, u, carry):
        q = u * inverse[z, part]
        u_out[z, part] = u
        q_out[z, part] = q
        if z == 0:
            z_low[part] = q
        if z == planes - 1:
            z_high[part] = q
        if part.start == 0:
            y_low[z : z + 1] = q[:1]
        if part.start == rows - ROWS:
            y_high[z : z + 1] = q[ROWS - 1 :]
        return carry

    apply_planes(q_ref, faces, face_z, face_y, below_z, above_z, y_got, y_got_too, emit, 0)
    y_first[...], y_second[...] = to_send(y_low[...], y_high[...])


def fold(product):
    total = product[:, :LANES]
    for at in range(LANES, product.shape[1], LANES):
        total = total + product[:, at : at + LANES]
    return total


def gram_kernel(sums, count, *refs):
    us, qs = refs[: count], refs[count : 2 * count]
    ratio, out = refs[2 * count :]
    planes, rows, _ = ratio.shape

    def body(z, totals):
        totals = list(totals)
        for at in range(0, rows, ROWS):
            part = pl.ds(at, ROWS)
            fields = {("u", i): us[i][z, part] for i in range(count)}
            fields |= {("q", i): qs[i][z, part] for i in range(count)}
            weight = ratio[z, part]
            fields |= {("y", i): weight * fields["q", i] for i in range(count)}
            for number, (a, i, b, j) in enumerate(sums):
                totals[number] = totals[number] + fold(fields[a, i] * fields[b, j])
        return tuple(totals)

    zero = jnp.zeros((ROWS, LANES), F32)
    for number, total in enumerate(lax.fori_loop(0, planes, body, (zero,) * len(sums))):
        out[number] = total


def last_kernel(
    q2_ref, faces, face_z, face_y, u0_ref, u1_ref, u2_ref, below_z, above_z, y_got, y_got_too, early, middle, out
):
    us = (u0_ref, u1_ref, u2_ref)

    def emit(z, part, u3, totals):
        fields = {("u", i): us[i][z, part] for i in range(3)}
        fields |= {("u", 3): u3, ("q", 2): q2_ref[z, part]}
        return [
            total + fold(fields[a, i] * fields[b, j]) for total, (a, i, b, j) in zip(totals, LATE)
        ]

    zero = jnp.zeros((ROWS, LANES), F32)
    late = apply_planes(
        q2_ref, faces, face_z, face_y, below_z, above_z, y_got, y_got_too, emit, [zero] * len(LATE)
    )
    lane = lax.broadcasted_iota(jnp.int32, (1, LANES), 1)
    row = jnp.zeros((1, LANES), F32)
    for names, totals in ((EARLY, early), (MIDDLE, middle), (LATE, late)):
        for number, name in enumerate(names):
            row = jnp.where(lane == SUMS.index(name), jnp.sum(totals[number], keepdims=True), row)
    out[...] = jnp.broadcast_to(row, out.shape)


def quadratic(left, table, right):
    total = None
    for i, a in enumerate(left):
        for j, b in enumerate(right):
            if a is None or b is None:
                continue
            term = a * b * table(i, j)
            total = term if total is None else total + term
    return total


def combine(totals, cell_count, iterations=3):
    moment = lambda i, j: totals[i + j]
    drop = lambda i, j: totals[i + j] - totals[i + j + 1]
    zero = jnp.zeros_like(totals[0])
    one = zero + 1.0
    residual, direction, change = [one], [one], []
    inner = moment(0, 0)
    for step in range(iterations):
        curvature = quadratic(direction, drop, direction)
        alive = (inner > 0.0) & (curvature > 0.0)
        size = jnp.where(alive, inner / jnp.where(alive, curvature, 1.0), 0.0)
        change = [c + size * d for c, d in zip(change + [zero], direction)]
        image = [a - b for a, b in zip(direction + [zero], [zero] + direction)]
        residual = [r - size * a for r, a in zip(residual + [zero], image)]
        if step + 1 < iterations:
            following = quadratic(residual, moment, residual)
            noise = quadratic([abs(r) for r in residual], lambda i, j: abs(moment(i, j)), [abs(r) for r in residual])
            following = jnp.where(following > 1e-7 * noise, following, 0.0)
            growth = jnp.where(inner > 0.0, following / jnp.where(inner > 0.0, inner, 1.0), 0.0)
            direction = [z + growth * d for z, d in zip(residual, direction + [zero])]
            inner = following
    at = {name: total for name, total in zip(SUMS, totals)}
    closing = quadratic(residual, lambda i, j: at["u", min(i, j), "u", max(i, j)], residual)
    changed = quadratic(change, lambda i, j: at["y", min(i, j), "y", max(i, j)], change)
    scale = 1.0 / cell_count
    return change, jnp.sqrt(jnp.maximum(closing, 0.0) * scale), jnp.sqrt(jnp.maximum(changed, 0.0) * scale)


def final_kernel(cell_count, rows_ref, q0, q1, q2, pressure_ref, strain_ref, ratio, pressure_out, strain_out, norms):
    planes, rows, width = pressure_ref.shape
    lane = lax.broadcasted_iota(jnp.int32, (1, LANES), 1)
    row = jnp.sum(rows_ref[...], axis=0, keepdims=True)
    totals = [jnp.sum(jnp.where(lane == at, row, 0.0), axis=1, keepdims=True) for at in range(len(SUMS))]
    change, closing, changed = combine(totals, cell_count)
    norms[...] = jnp.where(lane == 0, closing, changed)[:, :2]
    weights = [jnp.broadcast_to(c, (ROWS, width)) for c in change]

    def body(z, carry):
        for at in range(0, rows, ROWS):
            part = pl.ds(at, ROWS)
            delta = weights[0] * q0[z, part] + weights[1] * q1[z, part] + weights[2] * q2[z, part]
            pressure_out[z, part] = pressure_ref[z, part] + delta
            strain_out[z, part] = strain_ref[z, part] + ratio[z, part] * delta
        return carry

    lax.fori_loop(0, planes, body, 0)


def ring(count, step):
    return [(i, (i + step) % count) for i in range(count)]


def pairs_along_y(count_z, count_y, start):
    pairs = []
    for z in range(count_z):
        partner = list(range(count_y))
        for y in range(start, count_y - 1, 2):
            partner[y], partner[y + 1] = y + 1, y
        pairs += [
            (z * count_y + y, (z if partner[y] != y else z ^ 1) * count_y + partner[y]) for y in range(count_y)
        ]
    return pairs


def exchange(z_low, z_high, y_first, y_second):
    count_z, count_y = lax.axis_size("gz"), lax.axis_size("gy")
    both = ("gz", "gy")
    if paired(count_z, count_y):
        ways = [(both, pairs_along_y(count_z, count_y, start)) for start in (0, 1)]
    else:
        ways = [("gy", ring(count_y, step)) for step in (1, -1)]
    got = {}
    for name, field, axis, pairs in (
        ("send_low", z_low, "gz", ring(count_z, -1)),
        ("send_high", z_high, "gz", ring(count_z, 1)),
        ("send_first", y_first, *ways[0]),
        ("send_second", y_second, *ways[1]),
    ):
        got[name] = lax.ppermute(field, axis, pairs)
    return got["send_high"], got["send_low"], got["send_first"], got["send_second"]


def call(kernel, outs, specs, *operands, scratch=(), keep=True):
    shapes = [pltpu.VMEM(shape, F32) if keep else jax.ShapeDtypeStruct(shape, F32) for shape in outs]
    operands = [
        pltpu.with_memory_space_constraint(operand, spec.memory_space) for operand, spec in zip(operands, specs)
    ]
    single = len(shapes) == 1
    return pl.pallas_call(
        kernel,
        out_shape=shapes[0] if single else shapes,
        in_specs=specs,
        out_specs=VMEM if single else [VMEM] * len(shapes),
        scratch_shapes=list(scratch),
        compiler_params=pltpu.CompilerParams(vmem_limit_bytes=16 << 20),
    )(*operands)


def per_device(
    zone_ids, fixed_cells, pressure_old, pressure_iter, strain_change, source,
    zone_perm, zone_storage, zone_biot, zone_bulk,
):
    planes, rows, width = zone_ids.shape
    field = (planes, rows, width)
    sides = ((rows, width), (rows, width), (planes, width), (planes, width))
    devices = lax.axis_size("gz") * lax.axis_size("gy")
    cell_count = zone_ids.size * devices
    line = pltpu.VMEM((planes, width), F32)

    packed = call(
        pack_kernel, [(2, *side) for side in sides], [HBM] * 3, zone_ids, pressure_iter, zone_perm,
        scratch=[
            pltpu.VMEM((2, rows, width), jnp.int32), pltpu.VMEM((2, planes, ROWS, width), jnp.int32),
            pltpu.VMEM((2, planes, ROWS, width), F32), pltpu.SMEM(zone_perm.shape, F32), pltpu.SemaphoreType.DMA((9,)),
        ],
    )
    halo = exchange(*packed)
    faces, perm, diagonal, residual, free, ratio, pressure_kept, strain_kept = call(
        prepare_kernel, [(6, *field)] + [field] * 7, [HBM] * 10,
        zone_ids, fixed_cells, pressure_old, pressure_iter, strain_change, source,
        zone_perm, zone_storage, zone_biot, zone_bulk,
        scratch=[
            *[pltpu.VMEM(field, jnp.int32)] * 2, *[pltpu.VMEM(field, F32)] * 2,
            *[pltpu.SMEM(zone_perm.shape, F32)] * 4, pltpu.SemaphoreType.DMA((10,)),
        ],
    )
    inverse, q0, u0, face_z, face_y, *edges = call(
        begin_kernel, [field, field, field, (2, rows, width), (2, planes, width), *sides], [VMEM] * 9,
        perm, diagonal, residual, free, pressure_kept, *halo, scratch=[line, line],
    )
    parts = (faces, face_z, face_y)
    halo = exchange(*edges)
    q1, u1, *edges = call(
        stage_kernel, [field, field, *sides], [VMEM] * 9, q0, *parts, inverse, *halo, scratch=[line, line]
    )
    halo = exchange(*edges)
    early = call(
        functools.partial(gram_kernel, EARLY, 2), [(len(EARLY), ROWS, LANES)], [VMEM] * 5,
        u0, u1, q0, q1, ratio,
    )
    q2, u2, *edges = call(
        stage_kernel, [field, field, *sides], [VMEM] * 9, q1, *parts, inverse, *halo, scratch=[line, line]
    )
    halo = exchange(*edges)
    middle = call(
        functools.partial(gram_kernel, MIDDLE, 3), [(len(MIDDLE), ROWS, LANES)], [VMEM] * 7,
        u0, u1, u2, q0, q1, q2, ratio,
    )
    sums = call(
        last_kernel, [(devices, LANES)], [VMEM] * 13,
        q2, *parts, u0, u1, u2, *halo, early, middle,
    )
    gathered = lax.all_to_all(sums, ("gz", "gy"), 0, 0, tiled=True)
    pressure, strain_next, norms = call(
        functools.partial(final_kernel, cell_count), [field, field, (1, 2)], [VMEM] * 7,
        gathered, q0, q1, q2, pressure_kept, strain_kept, ratio, keep=False,
    )
    return pressure, strain_next, norms.reshape(2)


def solution(mesh):
    split = P("gz", "gy", None)
    return jax.shard_map(
        per_device,
        mesh=mesh,
        in_specs=(split,) * 6 + (P(),) * 4,
        out_specs=(split, split, P()),
        check_vma=False,
    )
```

time: 79.7 us -> 50 us (0.63)
  Pallas kernels: 30.9 us -> 9.82 us
  starting transfers between devices: 27.2 us -> 19.3 us
  blocking collectives: 10.7 us -> 15.5 us
  local copies, waits for them, and re-layouts: 3.81 us -> 0 us
  waiting for transfers between devices: 5.98 us -> 4.41 us
    pallas_call x8 -> x9, Pallas kernels: 30.9 us -> 9.82 us  [call(): pl.pallas_call(kernel, out_shape=shapes[0] if single else shapes, in_spec...]
    ppermute x16, starting transfers between devices: 27.2 us -> 19.3 us  [exchange(): got[name] = lax.ppermute(field, axis, pairs)]
    all_to_all x1, blocking collectives: 10.7 us -> 15.5 us  [per_device(): gathered = lax.all_to_all(sums, ('gz', 'gy'), 0, 0, tiled=True)]
    unnamed x32 -> x0, local copies, waits for them, and re-layouts: 3.81 us -> none
    ppermute x16, waiting for transfers between devices: 5.98 us -> 4.41 us  [exchange(): got[name] = lax.ppermute(field, axis, pairs)]
  transfers between devices with their start and end apart: 16 -> 16, of which waited for: 3 -> 3; matrix products, arithmetic and copies ran while one was open for 0% -> 0% of each run, Pallas kernels for 7% -> 11%
where the time goes in v2:
time: 50 us; the launch traced here: 49.8 us
  starting transfers between devices  19.3 us (39%)
  blocking collectives  15.5 us (31%)
  Pallas kernels  9.82 us (20%)
  waiting for transfers between devices  4.41 us (9%)
  between operations  0.75 us (2%)
    ppermute x16, starting transfers between devices, exchange(): got[name] = lax.ppermute(field, axis, pairs)  19.3 us
    all_to_all x1, blocking collectives, per_device(): gathered = lax.all_to_all(sums, ('gz', 'gy'), 0, 0, tiled=True)  15.5 us
    pallas_call x9, Pallas kernels, call(): pl.pallas_call(kernel, out_shape=shapes[0] if single else shapes, in_spec...  9.82 us
    ppermute x16, waiting for transfers between devices, exchange(): got[name] = lax.ppermute(field, axis, pairs)  4.41 us
  transfers between devices with their start and end apart: 16, of which 3 were waited for; matrix products, arithmetic and copies ran while one was open for 0% of the time, Pallas kernels for 11%

profile of v2, /device:TPU:0, one launch (start us, length us, event | category | flops | bytes accessed | tf_op | source)
XLA Modules:
  0.0 49.8 jit_solution(6973563506080176007)
XLA Ops:
  0.6 1.5 %shard_map.122 = (f32[2,32,512]{2,1,0:T(8,128)S(1)}, f32[2,32,512]{2,1,0:T(8,128)S(1)}, f32[2,8,512]{2,1,0:T(8,128)S(1)}, f32[2,8,512]{2,1,0:T(8,128)S(1)}) custom-call(s32[8,32,512]{2,1,0:T(8,128)} %zone_hbm.3, f32[8,32,512]{2,1,0:T(8,128)} %pressure_hbm.3, f32[8]{0:T(128)} %perm_hbm.3), custom_call_target="tpu_custom_call" | custom-call | tf_op jit(solution)/shard_map/pallas_call | solution.py:466
  2.1 0.5 %collective-permute-start = (f32[2,32,512]{2,1,0:T(8,128)S(1)}, f32[2,32,512]{2,1,0:T(8,128)S(1)}, u32[]{:S(2)}, u32[]{:S(2)}) collective-permute-start(f32[2,32,512]{2,1,0:T(8,128)S(1)} %get-tuple-element.44), channel_id=1, source_target_pairs={{0,8},{8,16},{16,24},{24,0},{1,9},{9,17},{17,25},{25,1},{2,10},{10... | collective-permute-start | bytes 393224 | tf_op jit(solution)/shard_map/ppermute | solution.py:456
  2.7 2.0 %collective-permute-start.1 = (f32[2,32,512]{2,1,0:T(8,128)S(1)}, f32[2,32,512]{2,1,0:T(8,128)S(1)}, u32[]{:S(2)}, u32[]{:S(2)}) collective-permute-start(f32[2,32,512]{2,1,0:T(8,128)S(1)} %get-tuple-element.45), channel_id=1, source_target_pairs={{0,24},{8,0},{16,8},{24,16},{1,25},{9,1},{17,9},{25,17},{2,26},{10... | collective-permute-start | bytes 393224 | tf_op jit(solution)/shard_map/ppermute | solution.py:456
  4.6 2.3 %collective-permute-start.2 = (f32[2,8,512]{2,1,0:T(8,128)S(1)}, f32[2,8,512]{2,1,0:T(8,128)S(1)}, u32[]{:S(2)}, u32[]{:S(2)}) collective-permute-start(f32[2,8,512]{2,1,0:T(8,128)S(1)} %get-tuple-element.46), channel_id=1, source_target_pairs={{0,1},{1,0},{2,3},{3,2},{4,5},{5,4},{6,7},{7,6},{8,9},{9,8},{10,11... | collective-permute-start | bytes 98312 | tf_op jit(solution)/shard_map/ppermute | solution.py:456
  6.9 0.0 collective-permute-start.3
  6.9 4.5 %shard_map.121 = (f32[6,8,32,512]{3,2,1,0:T(8,128)S(1)}, f32[8,32,512]{2,1,0:T(8,128)S(1)}, f32[8,32,512]{2,1,0:T(8,128)S(1)}, f32[8,32,512]{2,1,0:T(8,128)S(1)}...) custom-call(s32[8,32,512]{2,1,0:T(8,128)} %zone_hbm.3, ...), custom_call_target="tpu_custom_call" | custom-call | tf_op jit(solution)/shard_map/pallas_call | solution.py:466
  11.4 0.0 collective-permute-done.2.y_got
  11.4 0.0 collective-permute-done.3.y_got_too
  11.5 0.0 collective-permute-done.below_z
  11.5 0.0 collective-permute-done.1.above_z
  11.5 0.2 shard_map.123
  11.7 0.6 %collective-permute-start.4 = (f32[32,512]{1,0:T(8,128)S(1)}, f32[32,512]{1,0:T(8,128)S(1)}, u32[]{:S(2)}, u32[]{:S(2)}) collective-permute-start(f32[32,512]{1,0:T(8,128)S(1)} %get-tuple-element.53), channel_id=1, source_target_pairs={{0,8},{8,16},{16,24},{24,0},{1,9},{9,17},{17,25},{25,1},{2,10},{10... | collective-permute-start | bytes 196616 | tf_op jit(solution)/shard_map/ppermute | solution.py:456
  12.3 1.2 %collective-permute-start.5 = (f32[32,512]{1,0:T(8,128)S(1)}, f32[32,512]{1,0:T(8,128)S(1)}, u32[]{:S(2)}, u32[]{:S(2)}) collective-permute-start(f32[32,512]{1,0:T(8,128)S(1)} %get-tuple-element.54), channel_id=1, source_target_pairs={{0,24},{8,0},{16,8},{24,16},{1,25},{9,1},{17,9},{25,17},{2,26},{10... | collective-permute-start | bytes 196616 | tf_op jit(solution)/shard_map/ppermute | solution.py:456
  13.5 3.0 %collective-permute-start.6 = (f32[8,512]{1,0:T(8,128)S(1)}, f32[8,512]{1,0:T(8,128)S(1)}, u32[]{:S(2)}, u32[]{:S(2)}) collective-permute-start(f32[8,512]{1,0:T(8,128)S(1)} %get-tuple-element.55), channel_id=1, source_target_pairs={{0,1},{1,0},{2,3},{3,2},{4,5},{5,4},{6,7},{7,6},{8,9},{9,8},{10,11... | collective-permute-start | bytes 49160 | tf_op jit(solution)/shard_map/ppermute | solution.py:456
  16.6 0.0 collective-permute-start.7
  16.6 1.7 %collective-permute-done.6.y_got = f32[8,512]{1,0:T(8,128)S(1)} collective-permute-done((f32[8,512]{1,0:T(8,128)S(1)}, f32[8,512]{1,0:T(8,128)S(1)}, u32[]{:S(2)}, u32[]{:S(2)}) %collective-permute-start.6) | collective-permute-done | bytes 16416 | tf_op jit(solution)/shard_map/ppermute | solution.py:456
  18.3 0.0 collective-permute-done.7.y_got_too
  18.3 0.0 collective-permute-done.4.below_z
  18.3 0.0 collective-permute-done.5.above_z
  18.3 0.4 shard_map.124
  18.7 0.1 collective-permute-start.8
  18.8 1.7 %collective-permute-start.9 = (f32[32,512]{1,0:T(8,128)S(1)}, f32[32,512]{1,0:T(8,128)S(1)}, u32[]{:S(2)}, u32[]{:S(2)}) collective-permute-start(f32[32,512]{1,0:T(8,128)S(1)} %get-tuple-element.59), channel_id=1, source_target_pairs={{0,24},{8,0},{16,8},{24,16},{1,25},{9,1},{17,9},{25,17},{2,26},{10... | collective-permute-start | bytes 196616 | tf_op jit(solution)/shard_map/ppermute | solution.py:456
  20.5 3.0 %collective-permute-start.10 = (f32[8,512]{1,0:T(8,128)S(1)}, f32[8,512]{1,0:T(8,128)S(1)}, u32[]{:S(2)}, u32[]{:S(2)}) collective-permute-start(f32[8,512]{1,0:T(8,128)S(1)} %get-tuple-element.60), channel_id=1, source_target_pairs={{0,1},{1,0},{2,3},{3,2},{4,5},{5,4},{6,7},{7,6},{8,9},{9,8},{10,11... | collective-permute-start | bytes 49160 | tf_op jit(solution)/shard_map/ppermute | solution.py:456
  23.5 0.0 collective-permute-start.11
  23.5 1.7 %collective-permute-done.10.y_got = f32[8,512]{1,0:T(8,128)S(1)} collective-permute-done((f32[8,512]{1,0:T(8,128)S(1)}, f32[8,512]{1,0:T(8,128)S(1)}, u32[]{:S(2)}, u32[]{:S(2)}) %collective-permute-start.10) | collective-permute-done | bytes 16416 | tf_op jit(solution)/shard_map/ppermute | solution.py:456
  25.2 0.0 collective-permute-done.11.y_got_too
  25.3 0.0 collective-permute-done.8.below_z
  25.3 0.0 collective-permute-done.9.above_z
  25.3 0.4 shard_map.125
  25.7 0.1 collective-permute-start.12
  25.7 1.7 %collective-permute-start.13 = (f32[32,512]{1,0:T(8,128)S(1)}, f32[32,512]{1,0:T(8,128)S(1)}, u32[]{:S(2)}, u32[]{:S(2)}) collective-permute-start(f32[32,512]{1,0:T(8,128)S(1)} %get-tuple-element.67), channel_id=1, source_target_pairs={{0,24},{8,0},{16,8},{24,16},{1,25},{9,1},{17,9},{25,17},{2,26},{10... | collective-permute-start | bytes 196616 | tf_op jit(solution)/shard_map/ppermute | solution.py:456
  27.5 3.0 %collective-permute-start.14 = (f32[8,512]{1,0:T(8,128)S(1)}, f32[8,512]{1,0:T(8,128)S(1)}, u32[]{:S(2)}, u32[]{:S(2)}) collective-permute-start(f32[8,512]{1,0:T(8,128)S(1)} %get-tuple-element.68), channel_id=1, source_target_pairs={{0,1},{1,0},{2,3},{3,2},{4,5},{5,4},{6,7},{7,6},{8,9},{9,8},{10,11... | collective-permute-start | bytes 49160 | tf_op jit(solution)/shard_map/ppermute | solution.py:456
  30.5 0.0 collective-permute-start.15
  30.5 0.4 shard_map.126.early
  30.9 0.4 shard_map.127.middle
  31.3 0.9 %collective-permute-done.14.y_got = f32[8,512]{1,0:T(8,128)S(1)} collective-permute-done((f32[8,512]{1,0:T(8,128)S(1)}, f32[8,512]{1,0:T(8,128)S(1)}, u32[]{:S(2)}, u32[]{:S(2)}) %collective-permute-start.14) | collective-permute-done | bytes 16416 | tf_op jit(solution)/shard_map/ppermute | solution.py:456
  32.2 0.0 collective-permute-done.15.y_got_too
  32.2 0.0 collective-permute-done.12.below_z
  32.2 0.0 collective-permute-done.13.above_z
  32.2 0.7 %shard_map.128 = f32[32,128]{1,0:T(8,128)S(1)} custom-call(f32[8,32,512]{2,1,0:T(8,128)S(1)} %get-tuple-element.62.refs_5_.q2_ref.q2, f32[6,8,32,512]{3,2,1,0:T(8,128)S(1)} %get-tuple-element.49.faces, f32[2,32,512]{2,1,0:T(8,128)S(1)} %get-tuple-element.50.face_z, f32[2,8,512]{2,1,0:T(8,128)S(1)} %get-tuple-element.51.face_y, ...), custom_call_target="tpu_custom_call" | custom-call | tf_op jit(solution)/shard_map/pallas_call | solution.py:466
  32.9 15.5 %all_to_all.11 = f32[32,1,128]{2,1,0:T(1,128)S(1)} all-to-all(f32[32,1,128]{2,1,0:T(1,128)S(1)} %bitcast.5), channel_id=1, replica_groups=mesh['gz'=4,'gy'=8] {'gz','gy'}, dimensions={0} | all-to-all | bytes 32768 | tf_op jit(solution)/shard_map/all_to_all | solution.py:530
  48.4 1.4 %shard_map.129 = (f32[8,32,512]{2,1,0:T(8,128)}, f32[8,32,512]{2,1,0:T(8,128)}, f32[1,2]{1,0:T(1,128)}) custom-call(f32[32,128]{1,0:T(8,128)S(1)} %bitcast.6, f32[8,32,512]{2,1,0:T(8,128)S(1)} %get-tuple-element.48.q_ref.refs_2_.refs_3_.q0, f32[8,32,512]{2,1,0:T(8,128)S(1)} %get-tuple-element.57.q_ref.refs_3_.refs_4_.q1, ...), custom_call_target="tpu_custom_call" | custom-call | tf_op jit(solution)/shard_map/pallas_call | solution.py:466
Async XLA Ops:
  2.1 9.4 %collective-permute-start = (f32[2,32,512]{2,1,0:T(8,128)S(1)}, f32[2,32,512]{2,1,0:T(8,128)S(1)}, u32[]{:S(2)}, u32[]{:S(2)}) collective-permute-start(f32[2,32,512]{2,1,0:T(8,128)S(1)} %get-tuple-element.44), channel_id=1, source_target_pairs={{0,8},{8,16},{16,24},{24,0},{1,9},{9,17},{17,25},{25,1},{2,10},{10... | collective-permute-start | bytes 393224 | tf_op jit(solution)/shard_map/ppermute | solution.py:456
  2.7 8.8 %collective-permute-start.1 = (f32[2,32,512]{2,1,0:T(8,128)S(1)}, f32[2,32,512]{2,1,0:T(8,128)S(1)}, u32[]{:S(2)}, u32[]{:S(2)}) collective-permute-start(f32[2,32,512]{2,1,0:T(8,128)S(1)} %get-tuple-element.45), channel_id=1, source_target_pairs={{0,24},{8,0},{16,8},{24,16},{1,25},{9,1},{17,9},{25,17},{2,26},{10... | collective-permute-start | bytes 393224 | tf_op jit(solution)/shard_map/ppermute | solution.py:456
  4.6 6.8 %collective-permute-start.2 = (f32[2,8,512]{2,1,0:T(8,128)S(1)}, f32[2,8,512]{2,1,0:T(8,128)S(1)}, u32[]{:S(2)}, u32[]{:S(2)}) collective-permute-start(f32[2,8,512]{2,1,0:T(8,128)S(1)} %get-tuple-element.46), channel_id=1, source_target_pairs={{0,1},{1,0},{2,3},{3,2},{4,5},{5,4},{6,7},{7,6},{8,9},{9,8},{10,11... | collective-permute-start | bytes 98312 | tf_op jit(solution)/shard_map/ppermute | solution.py:456
  6.9 4.5 %collective-permute-start.3 = (f32[2,8,512]{2,1,0:T(8,128)S(1)}, f32[2,8,512]{2,1,0:T(8,128)S(1)}, u32[]{:S(2)}, u32[]{:S(2)}) collective-permute-start(f32[2,8,512]{2,1,0:T(8,128)S(1)} %get-tuple-element.47), channel_id=1, source_target_pairs={{0,8},{1,2},{2,1},{3,4},{4,3},{5,6},{6,5},{7,15},{8,0},{9,10},{10,... | collective-permute-start | bytes 98312 | tf_op jit(solution)/shard_map/ppermute | solution.py:456
  11.7 6.6 %collective-permute-start.4 = (f32[32,512]{1,0:T(8,128)S(1)}, f32[32,512]{1,0:T(8,128)S(1)}, u32[]{:S(2)}, u32[]{:S(2)}) collective-permute-start(f32[32,512]{1,0:T(8,128)S(1)} %get-tuple-element.53), channel_id=1, source_target_pairs={{0,8},{8,16},{16,24},{24,0},{1,9},{9,17},{17,25},{25,1},{2,10},{10... | collective-permute-start | bytes 196616 | tf_op jit(solution)/shard_map/ppermute | solution.py:456
  12.3 6.0 %collective-permute-start.5 = (f32[32,512]{1,0:T(8,128)S(1)}, f32[32,512]{1,0:T(8,128)S(1)}, u32[]{:S(2)}, u32[]{:S(2)}) collective-permute-start(f32[32,512]{1,0:T(8,128)S(1)} %get-tuple-element.54), channel_id=1, source_target_pairs={{0,24},{8,0},{16,8},{24,16},{1,25},{9,1},{17,9},{25,17},{2,26},{10... | collective-permute-start | bytes 196616 | tf_op jit(solution)/shard_map/ppermute | solution.py:456
  13.5 4.8 %collective-permute-start.6 = (f32[8,512]{1,0:T(8,128)S(1)}, f32[8,512]{1,0:T(8,128)S(1)}, u32[]{:S(2)}, u32[]{:S(2)}) collective-permute-start(f32[8,512]{1,0:T(8,128)S(1)} %get-tuple-element.55), channel_id=1, source_target_pairs={{0,1},{1,0},{2,3},{3,2},{4,5},{5,4},{6,7},{7,6},{8,9},{9,8},{10,11... | collective-permute-start | bytes 49160 | tf_op jit(solution)/shard_map/ppermute | solution.py:456
  16.6 1.7 %collective-permute-start.7 = (f32[8,512]{1,0:T(8,128)S(1)}, f32[8,512]{1,0:T(8,128)S(1)}, u32[]{:S(2)}, u32[]{:S(2)}) collective-permute-start(f32[8,512]{1,0:T(8,128)S(1)} %get-tuple-element.56), channel_id=1, source_target_pairs={{0,8},{1,2},{2,1},{3,4},{4,3},{5,6},{6,5},{7,15},{8,0},{9,10},{10,... | collective-permute-start | bytes 49160 | tf_op jit(solution)/shard_map/ppermute | solution.py:456
  18.7 6.5 %collective-permute-start.8 = (f32[32,512]{1,0:T(8,128)S(1)}, f32[32,512]{1,0:T(8,128)S(1)}, u32[]{:S(2)}, u32[]{:S(2)}) collective-permute-start(f32[32,512]{1,0:T(8,128)S(1)} %get-tuple-element.58), channel_id=1, source_target_pairs={{0,8},{8,16},{16,24},{24,0},{1,9},{9,17},{17,25},{25,1},{2,10},{10... | collective-permute-start | bytes 196616 | tf_op jit(solution)/shard_map/ppermute | solution.py:456
  18.8 6.5 %collective-permute-start.9 = (f32[32,512]{1,0:T(8,128)S(1)}, f32[32,512]{1,0:T(8,128)S(1)}, u32[]{:S(2)}, u32[]{:S(2)}) collective-permute-start(f32[32,512]{1,0:T(8,128)S(1)} %get-tuple-element.59), channel_id=1, source_target_pairs={{0,24},{8,0},{16,8},{24,16},{1,25},{9,1},{17,9},{25,17},{2,26},{10... | collective-permute-start | bytes 196616 | tf_op jit(solution)/shard_map/ppermute | solution.py:456
  20.5 4.7 %collective-permute-start.10 = (f32[8,512]{1,0:T(8,128)S(1)}, f32[8,512]{1,0:T(8,128)S(1)}, u32[]{:S(2)}, u32[]{:S(2)}) collective-permute-start(f32[8,512]{1,0:T(8,128)S(1)} %get-tuple-element.60), channel_id=1, source_target_pairs={{0,1},{1,0},{2,3},{3,2},{4,5},{5,4},{6,7},{7,6},{8,9},{9,8},{10,11... | collective-permute-start | bytes 49160 | tf_op jit(solution)/shard_map/ppermute | solution.py:456
  23.5 1.7 %collective-permute-start.11 = (f32[8,512]{1,0:T(8,128)S(1)}, f32[8,512]{1,0:T(8,128)S(1)}, u32[]{:S(2)}, u32[]{:S(2)}) collective-permute-start(f32[8,512]{1,0:T(8,128)S(1)} %get-tuple-element.61), channel_id=1, source_target_pairs={{0,8},{1,2},{2,1},{3,4},{4,3},{5,6},{6,5},{7,15},{8,0},{9,10},{10,... | collective-permute-start | bytes 49160 | tf_op jit(solution)/shard_map/ppermute | solution.py:456
  25.7 6.5 %collective-permute-start.12 = (f32[32,512]{1,0:T(8,128)S(1)}, f32[32,512]{1,0:T(8,128)S(1)}, u32[]{:S(2)}, u32[]{:S(2)}) collective-permute-start(f32[32,512]{1,0:T(8,128)S(1)} %get-tuple-element.66), channel_id=1, source_target_pairs={{0,8},{8,16},{16,24},{24,0},{1,9},{9,17},{17,25},{25,1},{2,10},{10... | collective-permute-start | bytes 196616 | tf_op jit(solution)/shard_map/ppermute | solution.py:456
  25.7 6.5 %collective-permute-start.13 = (f32[32,512]{1,0:T(8,128)S(1)}, f32[32,512]{1,0:T(8,128)S(1)}, u32[]{:S(2)}, u32[]{:S(2)}) collective-permute-start(f32[32,512]{1,0:T(8,128)S(1)} %get-tuple-element.67), channel_id=1, source_target_pairs={{0,24},{8,0},{16,8},{24,16},{1,25},{9,1},{17,9},{25,17},{2,26},{10... | collective-permute-start | bytes 196616 | tf_op jit(solution)/shard_map/ppermute | solution.py:456
  27.5 4.7 %collective-permute-start.14 = (f32[8,512]{1,0:T(8,128)S(1)}, f32[8,512]{1,0:T(8,128)S(1)}, u32[]{:S(2)}, u32[]{:S(2)}) collective-permute-start(f32[8,512]{1,0:T(8,128)S(1)} %get-tuple-element.68), channel_id=1, source_target_pairs={{0,1},{1,0},{2,3},{3,2},{4,5},{5,4},{6,7},{7,6},{8,9},{9,8},{10,11... | collective-permute-start | bytes 49160 | tf_op jit(solution)/shard_map/ppermute | solution.py:456
  30.5 1.7 %collective-permute-start.15 = (f32[8,512]{1,0:T(8,128)S(1)}, f32[8,512]{1,0:T(8,128)S(1)}, u32[]{:S(2)}, u32[]{:S(2)}) collective-permute-start(f32[8,512]{1,0:T(8,128)S(1)} %get-tuple-element.69), channel_id=1, source_target_pairs={{0,8},{1,2},{2,1},{3,4},{4,3},{5,6},{6,5},{7,15},{8,0},{9,10},{10,... | collective-permute-start | bytes 49160 | tf_op jit(solution)/shard_map/ppermute | solution.py:456

commit v3 on v2

--- a/solution.py
+++ b/solution.py
@@ -36,6 +36,17 @@
         for at in range(0, zones.shape[1], LANES)
     ]
     return jnp.concatenate(parts, axis=1)
+
+
+def zone_bits(zones, count):
+    return [(zones & (1 << bit)) != 0 for bit in range(max(count - 1, 1).bit_length())]
+
+
+def pick(bits, entries):
+    entries = list(entries) + [entries[-1]] * (2 ** len(bits) - len(entries))
+    for bit in bits:
+        entries = [jnp.where(bit, odd, even) for even, odd in zip(entries[::2], entries[1::2])]
+    return entries[0]
 
 
 def harmonic(lower_side, upper_side):
@@ -81,7 +92,7 @@
     for axis in ("gz", "gy"):
         place = lax.axis_index(axis)
         flags += [place > 0, place < lax.axis_size(axis) - 1]
-    return [jnp.where(flag, 1.0, 0.0).astype(F32) for flag in flags]
+    return flags
 
 
 def row_parts(rows):
@@ -89,11 +100,11 @@
 
 
 def pack_kernel(
-    zone_hbm, pressure_hbm, perm_hbm, z_low, z_high, y_first, y_second, zone_z, zone_y, pressure_y, perm_table, sems
+    zone_hbm, pressure_hbm, z_low, z_high, y_first, y_second, zone_z, zone_y, pressure_y, sems
 ):
     planes, rows, _ = zone_hbm.shape
     ends = ((0, pl.ds(0, ROWS)), (planes - 1, pl.ds(rows - ROWS, ROWS)))
-    copies = [pltpu.make_async_copy(perm_hbm, perm_table, sems.at[8])]
+    copies = []
     for side, (plane, part) in enumerate(ends):
         out = (z_low, z_high)[side]
         for source, target in (
@@ -102,128 +113,155 @@
             (zone_hbm.at[:, part], zone_y.at[side]),
             (pressure_hbm.at[:, part], pressure_y.at[side]),
         ):
-            copies.append(pltpu.make_async_copy(source, target, sems.at[len(copies) - 1]))
+            copies.append(pltpu.make_async_copy(source, target, sems.at[len(copies)]))
     for copy in copies:
         copy.start()
-    copies[0].wait()
-    perm_row = table_row(perm_table)
-    for copy in copies[1:]:
+    for copy in copies:
         copy.wait()
     faces_y = []
     for side, out in enumerate((z_low, z_high)):
-        for part in row_parts(rows):
-            out[0, part] = look_up(perm_row, zone_z[side, part])
+        out[0] = zone_z[side].astype(F32)
         row = pl.ds((0, ROWS - 1)[side], 1)
         zones = jnp.concatenate([zone_y[side, plane, row] for plane in range(planes)], axis=0)
         values = jnp.concatenate([pressure_y[side, plane, row] for plane in range(planes)], axis=0)
-        faces_y.append((look_up(perm_row, zones), values))
+        faces_y.append((zones.astype(F32), values))
     for number in range(2):
         y_first[number], y_second[number] = to_send(faces_y[0][number], faces_y[1][number])
+
+
+NO_FACE = LANES - 1
+
+
+def face_row(perm_row, zones):
+    lane = lax.broadcasted_iota(jnp.int32, (ROWS, LANES), 1)
+    known = lane < zones * zones
+    pair = jnp.where(known, lane, 0)
+    sides = [
+        jnp.take_along_axis(perm_row, side, axis=1, mode="promise_in_bounds")
+        for side in (lax.div(pair, zones), lax.rem(pair, zones))
+    ]
+    return jnp.where(known, harmonic(*sides), 0.0)
 
 
 def prepare_kernel(
     zone_hbm, fixed_hbm, old_hbm, pressure_hbm, strain_hbm, source_hbm,
     perm_hbm, storage_hbm, biot_hbm, bulk_hbm,
-    faces, perm, diagonal_out, residual_out, free_out, ratio, pressure, strain,
-    zone, fixed, old, source, perm_table, storage_table, biot_table, bulk_table, sems,
+    faces, diagonal_out, residual_out, free_out, ratio, pressure, strain, face_table, zone,
+    fixed, old, source, perm, storage_of, biot_of, term_z, perm_table, storage_table, biot_table, bulk_table, sems, half_sems,
 ):
     planes, rows, width = zone_hbm.shape
+    half = planes // 2
     pairs = (
-        (perm_hbm, perm_table), (storage_hbm, storage_table), (biot_hbm, biot_table), (bulk_hbm, bulk_table),
-        (zone_hbm, zone), (pressure_hbm, pressure), (old_hbm, old), (strain_hbm, strain), (source_hbm, source),
-        (fixed_hbm, fixed),
+        (zone_hbm, zone), (perm_hbm, perm_table), (storage_hbm, storage_table), (biot_hbm, biot_table),
+        (bulk_hbm, bulk_table), (pressure_hbm, pressure),
     )
     copies = [pltpu.make_async_copy(*pair, sems.at[number]) for number, pair in enumerate(pairs)]
-    for copy in copies:
+    halves = [
+        [
+            pltpu.make_async_copy(whole.at[part], kept.at[part], half_sems.at[at, number])
+            for number, (whole, kept) in enumerate(
+                ((fixed_hbm, fixed), (old_hbm, old), (strain_hbm, strain), (source_hbm, source))
+            )
+        ]
+        for at, part in enumerate((pl.ds(0, half), pl.ds(half, planes - half)))
+    ]
+    for copy in copies + halves[0] + halves[1]:
         copy.start()
-    for copy in copies[:4]:
+    for copy in copies[1:5]:
         copy.wait()
-    perm_row = table_row(perm_table)
-    storage_row = table_row(storage_table)
-    biot_row = table_row(biot_table)
-    known = lax.broadcasted_iota(jnp.int32, (ROWS, LANES), 1) < bulk_table.shape[0]
-    bulk_row = jnp.where(known, table_row(bulk_table), 1.0)
-    ratio_row = biot_row / bulk_row
-    coupling_row = biot_row * biot_row / bulk_row
+    zones = perm_table.shape[0]
+    face_table[...] = face_row(table_row(perm_table), zones)
+    entries = [[table[number] for number in range(zones)] for table in (perm_table, storage_table, biot_table)]
+    one = jnp.ones((ROWS, width), F32)
+    entries.append([entries[2][number] * one / (bulk_table[number] * one) for number in range(zones)])
     lane = lax.broadcasted_iota(jnp.int32, (ROWS, width), 1)
-    copies[4].wait()
+    closed = jnp.zeros((ROWS, width), F32)
+    parts = row_parts(rows)
+    copies[0].wait()
 
     def fill(z, carry):
-        for part in row_parts(rows):
-            perm[z, part] = look_up(perm_row, zone[z, part])
+        for part in parts:
+            bits = zone_bits(zone[z, part], zones)
+            for out, entry in zip((perm, storage_of, biot_of, ratio), entries):
+                out[z, part] = pick(bits, entry)
         return carry
 
     lax.fori_loop(0, planes, fill, 0)
-    for copy in copies[5:]:
-        copy.wait()
-    closed = jnp.zeros((ROWS, width), F32)
+    copies[5].wait()
 
     def plane(z, low, high):
-        parts = row_parts(rows)
         perms = [perm[z, part] for part in parts]
         values = [pressure[z, part] for part in parts]
-        perm_lower, perm_upper = row_shifts(perms, closed, closed)
+        perm_lower, _ = row_shifts(perms, closed, closed)
+        lower = [harmonic(*pair) for pair in zip(perms, perm_lower)]
+        _, upper = row_shifts(lower, closed, closed)
         value_lower, value_upper = row_shifts(values, closed, closed)
         for at, part in enumerate(parts):
-            zones = zone[z, part]
-            storage = look_up(storage_row, zones)
-            coupling = look_up(coupling_row, zones)
-            biot = look_up(biot_row, zones)
-            ratio[z, part] = look_up(ratio_row, zones)
             here, value = perms[at], values[at]
-            x_lower, x_upper = lane_shifts(here)
-            x_lower = jnp.where(lane == 0, 0.0, x_lower)
-            x_upper = jnp.where(lane == width - 1, 0.0, x_upper)
-            value_left, value_right = lane_shifts(value)
-            beside = (
-                closed if low is None else perm[low, part], closed if high is None else perm[high, part],
-                perm_lower[at], perm_upper[at], x_lower, x_upper,
-            )
-            views = (
-                closed if low is None else pressure[low, part], closed if high is None else pressure[high, part],
-                value_lower[at], value_upper[at], value_left, value_right,
-            )
-            terms = [harmonic(here, other) for other in beside]
+            left = harmonic(here, jnp.where(lane == 0, 0.0, pltpu.roll(here, 1, 1)))
+            right = pltpu.roll(left, width - 1, 1)
+            terms, views = [None, None], [None, None]
+            if low is not None:
+                terms[0], views[0] = term_z[z, part], pressure[low, part]
+            if high is not None:
+                terms[1], views[1] = harmonic(here, perm[high, part]), pressure[high, part]
+                term_z[high, part] = terms[1]
+            terms += [lower[at], upper[at], left, right]
+            views += [value_lower[at], value_upper[at], *lane_shifts(value)]
+            storage, biot = storage_of[z, part], biot_of[z, part]
+            coupling = biot * ratio[z, part]
             free = 1.0 - fixed[z, part].astype(F32)
-            diagonal = storage + coupling
-            for term in terms:
-                diagonal = diagonal + term
-            neighbours = terms[0] * views[0]
-            for number in range(1, 6):
-                neighbours = neighbours + terms[number] * views[number]
+            diagonal, neighbours = storage + coupling, None
+            for number, (term, view) in enumerate(zip(terms, views)):
+                if term is not None:
+                    faces[number, z, part] = free * term
+                    diagonal = diagonal + term
+                    neighbours = term * view if neighbours is None else neighbours + term * view
             right_side = storage * old[z, part] + coupling * value - biot * strain[z, part] + source[z, part]
-            for number in range(6):
-                faces[number, z, part] = free * terms[number]
             diagonal_out[z, part] = diagonal
             residual_out[z, part] = right_side - (diagonal * value - neighbours)
             free_out[z, part] = free
 
+    def middle(start, stop):
+        lax.fori_loop(start, stop, lambda z, c: (plane(z, z - 1, z + 1), c)[1], 0)
+
+    for copy in halves[0]:
+        copy.wait()
     plane(0, None, 1)
-    lax.fori_loop(1, planes - 1, lambda z, c: (plane(z, z - 1, z + 1), c)[1], 0)
+    middle(1, half)
+    for copy in halves[1]:
+        copy.wait()
+    middle(half, planes - 1)
     plane(planes - 1, planes - 2, None)
 
 
 def begin_kernel(
-    perm, diagonal_ref, residual_ref, free_ref, pressure, below_z, above_z, y_got, y_got_too,
+    zones,
+    zone, face_table, diagonal_ref, residual_ref, free_ref, pressure, below_z, above_z, y_got, y_got_too,
     inverse, q_out, u_out, face_z, face_y, z_low, z_high, y_first, y_second,
     y_low, y_high,
 ):
     planes, rows, width = pressure.shape
     inside = inside_flags()
-    below_perm, above_perm = as_sides(y_got[0], y_got_too[0])
+    below_zone, above_zone = as_sides(y_got[0], y_got_too[0])
     below_value, above_value = as_sides(y_got[1], y_got_too[1])
-    below_perm, above_perm = below_perm * inside[2], above_perm * inside[3]
+    table = face_table[...]
+
+    def outer_term(own, other, side):
+        index = own * zones + other.astype(jnp.int32)
+        return look_up(table, jnp.where(inside[side], index, NO_FACE))
+
     sub = lax.broadcasted_iota(jnp.int32, (ROWS, width), 0)
     ends = (
-        (pl.ds(0, 1), below_perm, below_value),
-        (pl.ds(rows - 1, 1), above_perm, above_value),
+        (pl.ds(0, 1), below_zone, below_value),
+        (pl.ds(rows - 1, 1), above_zone, above_value),
     )
     gain_y = []
     for side, (row, other, value) in enumerate(ends):
-        here = jnp.concatenate([perm[z, row] for z in range(planes)], axis=0)
+        here = jnp.concatenate([zone[z, row] for z in range(planes)], axis=0)
         own = jnp.concatenate([pressure[z, row] for z in range(planes)], axis=0)
         free = jnp.concatenate([free_ref[z, row] for z in range(planes)], axis=0)
-        term = harmonic(here, other)
+        term = outer_term(here, other, 2 + side)
         face_y[side] = free * term
         gain_y.append((term, term * (value - own)))
 
@@ -232,7 +270,7 @@
             diagonal, residual, free = diagonal_ref[z, part], residual_ref[z, part], free_ref[z, part]
             if outer is not None:
                 side, halo = outer
-                term = harmonic(perm[z, part], halo[0, part] * inside[side])
+                term = outer_term(zone[z, part], halo[0, part], side)
                 diagonal = diagonal + term
                 residual = residual + term * (halo[1, part] - pressure[z, part])
                 face_z[side, part] = free * term
@@ -403,24 +441,44 @@
     return change, jnp.sqrt(jnp.maximum(closing, 0.0) * scale), jnp.sqrt(jnp.maximum(changed, 0.0) * scale)
 
 
-def final_kernel(cell_count, rows_ref, q0, q1, q2, pressure_ref, strain_ref, ratio, pressure_out, strain_out, norms):
+def final_kernel(
+    cell_count, rows_ref, q0, q1, q2, pressure_ref, strain_ref, ratio, pressure_hbm, strain_hbm, norms_hbm,
+    pressure_out, strain_out, norms, sems, norms_sem,
+):
     planes, rows, width = pressure_ref.shape
+    total = rows_ref[:ROWS]
+    for at in range(ROWS, rows_ref.shape[0], ROWS):
+        total = total + rows_ref[at : at + ROWS]
+    for step in (4, 2, 1):
+        total = total + pltpu.roll(total, step, 0)
+    totals = [
+        jnp.take_along_axis(total, jnp.full((ROWS, LANES), at, jnp.int32), axis=1, mode="promise_in_bounds")
+        for at in range(len(SUMS))
+    ]
+    change, closing, changed = combine(totals, cell_count)
     lane = lax.broadcasted_iota(jnp.int32, (1, LANES), 1)
-    row = jnp.sum(rows_ref[...], axis=0, keepdims=True)
-    totals = [jnp.sum(jnp.where(lane == at, row, 0.0), axis=1, keepdims=True) for at in range(len(SUMS))]
-    change, closing, changed = combine(totals, cell_count)
-    norms[...] = jnp.where(lane == 0, closing, changed)[:, :2]
-    weights = [jnp.broadcast_to(c, (ROWS, width)) for c in change]
-
-    def body(z, carry):
-        for at in range(0, rows, ROWS):
-            part = pl.ds(at, ROWS)
+    norms[...] = jnp.where(lane == 0, closing[:1], changed[:1])[:, :2]
+    norms_copy = pltpu.make_async_copy(norms, norms_hbm, norms_sem)
+    norms_copy.start()
+    weights = [jnp.concatenate([c] * (width // LANES), axis=1) for c in change]
+
+    def copies(z):
+        return [
+            pltpu.make_async_copy(kept.at[z], whole.at[z], sems.at[number, z])
+            for number, (kept, whole) in enumerate(((pressure_out, pressure_hbm), (strain_out, strain_hbm)))
+        ]
+
+    for z in range(planes):
+        for part in row_parts(rows):
             delta = weights[0] * q0[z, part] + weights[1] * q1[z, part] + weights[2] * q2[z, part]
             pressure_out[z, part] = pressure_ref[z, part] + delta
             strain_out[z, part] = strain_ref[z, part] + ratio[z, part] * delta
-        return carry
-
-    lax.fori_loop(0, planes, body, 0)
+        for copy in copies(z):
+            copy.start()
+    for z in range(planes):
+        for copy in copies(z):
+            copy.wait()
+    norms_copy.wait()
 
 
 def ring(count, step):
@@ -457,17 +515,18 @@
     return got["send_high"], got["send_low"], got["send_first"], got["send_second"]
 
 
-def call(kernel, outs, specs, *operands, scratch=(), keep=True):
-    shapes = [pltpu.VMEM(shape, F32) if keep else jax.ShapeDtypeStruct(shape, F32) for shape in outs]
+def call(kernel, outs, specs, *operands, scratch=(), out_specs=None):
+    results = [pltpu.VMEM(out, F32) if isinstance(out, tuple) else out for out in outs]
+    out_specs = out_specs or [VMEM] * len(results)
     operands = [
         pltpu.with_memory_space_constraint(operand, spec.memory_space) for operand, spec in zip(operands, specs)
     ]
-    single = len(shapes) == 1
+    single = len(results) == 1
     return pl.pallas_call(
         kernel,
-        out_shape=shapes[0] if single else shapes,
+        out_shape=results[0] if single else results,
         in_specs=specs,
-        out_specs=VMEM if single else [VMEM] * len(shapes),
+        out_specs=out_specs[0] if single else out_specs,
         scratch_shapes=list(scratch),
         compiler_params=pltpu.CompilerParams(vmem_limit_bytes=16 << 20),
     )(*operands)
@@ -485,25 +544,27 @@
     line = pltpu.VMEM((planes, width), F32)
 
     packed = call(
-        pack_kernel, [(2, *side) for side in sides], [HBM] * 3, zone_ids, pressure_iter, zone_perm,
+        pack_kernel, [(2, *side) for side in sides], [HBM] * 2, zone_ids, pressure_iter,
         scratch=[
             pltpu.VMEM((2, rows, width), jnp.int32), pltpu.VMEM((2, planes, ROWS, width), jnp.int32),
-            pltpu.VMEM((2, planes, ROWS, width), F32), pltpu.SMEM(zone_perm.shape, F32), pltpu.SemaphoreType.DMA((9,)),
+            pltpu.VMEM((2, planes, ROWS, width), F32), pltpu.SemaphoreType.DMA((8,)),
         ],
     )
     halo = exchange(*packed)
-    faces, perm, diagonal, residual, free, ratio, pressure_kept, strain_kept = call(
-        prepare_kernel, [(6, *field)] + [field] * 7, [HBM] * 10,
+    faces, diagonal, residual, free, ratio, pressure_kept, strain_kept, face_table, zone_kept = call(
+        prepare_kernel,
+        [(6, *field)] + [field] * 6 + [(ROWS, LANES), pltpu.VMEM(field, jnp.int32)], [HBM] * 10,
         zone_ids, fixed_cells, pressure_old, pressure_iter, strain_change, source,
         zone_perm, zone_storage, zone_biot, zone_bulk,
         scratch=[
-            *[pltpu.VMEM(field, jnp.int32)] * 2, *[pltpu.VMEM(field, F32)] * 2,
-            *[pltpu.SMEM(zone_perm.shape, F32)] * 4, pltpu.SemaphoreType.DMA((10,)),
+            pltpu.VMEM(field, jnp.int32), *[pltpu.VMEM(field, F32)] * 6, *[pltpu.SMEM(zone_perm.shape, F32)] * 4,
+            pltpu.SemaphoreType.DMA((6,)), pltpu.SemaphoreType.DMA((2, 4)),
         ],
     )
     inverse, q0, u0, face_z, face_y, *edges = call(
-        begin_kernel, [field, field, field, (2, rows, width), (2, planes, width), *sides], [VMEM] * 9,
-        perm, diagonal, residual, free, pressure_kept, *halo, scratch=[line, line],
+        functools.partial(begin_kernel, zone_perm.shape[0]),
+        [field, field, field, (2, rows, width), (2, planes, width), *sides], [VMEM] * 10,
+        zone_kept, face_table, diagonal, residual, free, pressure_kept, *halo, scratch=[line, line],
     )
     parts = (faces, face_z, face_y)
     halo = exchange(*edges)
@@ -529,8 +590,13 @@
     )
     gathered = lax.all_to_all(sums, ("gz", "gy"), 0, 0, tiled=True)
     pressure, strain_next, norms = call(
-        functools.partial(final_kernel, cell_count), [field, field, (1, 2)], [VMEM] * 7,
-        gathered, q0, q1, q2, pressure_kept, strain_kept, ratio, keep=False,
+        functools.partial(final_kernel, cell_count),
+        [jax.ShapeDtypeStruct(shape, F32) for shape in (field, field, (1, 2))], [VMEM] * 7,
+        gathered, q0, q1, q2, pressure_kept, strain_kept, ratio, out_specs=[HBM] * 3,
+        scratch=[
+            *[pltpu.VMEM(field, F32)] * 2, pltpu.VMEM((1, 2), F32), pltpu.SemaphoreType.DMA((2, planes)),
+            pltpu.SemaphoreType.DMA,
+        ],
     )
     return pressure, strain_next, norms.reshape(2)
 

time: 50 us -> 49 us (0.980)
  Pallas kernels: 9.82 us -> 8.84 us
    pallas_call x9, Pallas kernels: 9.82 us -> 8.84 us  [call(): pl.pallas_call(kernel, out_shape=results[0] if single else results, in_sp...]
  transfers between devices with their start and end apart: 16 -> 16, of which waited for: 3 -> 3; matrix products, arithmetic and copies ran while one was open for 0% -> 0% of each run, Pallas kernels for 11% -> 9%
where the time goes in v3:
time: 49 us; the launch traced here: 48.8 us
  starting transfers between devices  19.5 us (40%)
  blocking collectives  15.3 us (31%)
  Pallas kernels  8.84 us (18%)
  waiting for transfers between devices  4.38 us (9%)
  between operations  0.75 us (2%)
    ppermute x16, starting transfers between devices, exchange(): got[name] = lax.ppermute(field, axis, pairs)  19.5 us
    all_to_all x1, blocking collectives, per_device(): gathered = lax.all_to_all(sums, ('gz', 'gy'), 0, 0, tiled=True)  15.3 us
    pallas_call x9, Pallas kernels, call(): pl.pallas_call(kernel, out_shape=results[0] if single else results, in_sp...  8.84 us
    ppermute x16, waiting for transfers between devices, exchange(): got[name] = lax.ppermute(field, axis, pairs)  4.38 us
  transfers between devices with their start and end apart: 16, of which 3 were waited for; matrix products, arithmetic and copies ran while one was open for 0% of the time, Pallas kernels for 9%

profile of v3, /device:TPU:0, one launch (start us, length us, event | category | flops | bytes accessed | tf_op | source)
XLA Modules:
  0.0 48.8 jit_solution(12354019630792710060)
XLA Ops:
  0.6 1.3 %shard_map.122 = (f32[2,32,512]{2,1,0:T(8,128)S(1)}, f32[2,32,512]{2,1,0:T(8,128)S(1)}, f32[2,8,512]{2,1,0:T(8,128)S(1)}, f32[2,8,512]{2,1,0:T(8,128)S(1)}) custom-call(s32[8,32,512]{2,1,0:T(8,128)} %zone_hbm.3, f32[8,32,512]{2,1,0:T(8,128)} %pressure_hbm.3), custom_call_target="tpu_custom_call" | custom-call | tf_op jit(solution)/shard_map/pallas_call | solution.py:525
  2.0 0.5 %collective-permute-start = (f32[2,32,512]{2,1,0:T(8,128)S(1)}, f32[2,32,512]{2,1,0:T(8,128)S(1)}, u32[]{:S(2)}, u32[]{:S(2)}) collective-permute-start(f32[2,32,512]{2,1,0:T(8,128)S(1)} %get-tuple-element.46), channel_id=1, source_target_pairs={{0,8},{8,16},{16,24},{24,0},{1,9},{9,17},{17,25},{25,1},{2,10},{10... | collective-permute-start | bytes 393224 | tf_op jit(solution)/shard_map/ppermute | solution.py:514
  2.5 2.0 %collective-permute-start.1 = (f32[2,32,512]{2,1,0:T(8,128)S(1)}, f32[2,32,512]{2,1,0:T(8,128)S(1)}, u32[]{:S(2)}, u32[]{:S(2)}) collective-permute-start(f32[2,32,512]{2,1,0:T(8,128)S(1)} %get-tuple-element.47), channel_id=1, source_target_pairs={{0,24},{8,0},{16,8},{24,16},{1,25},{9,1},{17,9},{25,17},{2,26},{10... | collective-permute-start | bytes 393224 | tf_op jit(solution)/shard_map/ppermute | solution.py:514
  4.5 2.3 %collective-permute-start.2 = (f32[2,8,512]{2,1,0:T(8,128)S(1)}, f32[2,8,512]{2,1,0:T(8,128)S(1)}, u32[]{:S(2)}, u32[]{:S(2)}) collective-permute-start(f32[2,8,512]{2,1,0:T(8,128)S(1)} %get-tuple-element.48), channel_id=1, source_target_pairs={{0,1},{1,0},{2,3},{3,2},{4,5},{5,4},{6,7},{7,6},{8,9},{9,8},{10,11... | collective-permute-start | bytes 98312 | tf_op jit(solution)/shard_map/ppermute | solution.py:514
  6.8 0.0 collective-permute-start.3
  6.8 3.4 %shard_map.121 = (f32[6,8,32,512]{3,2,1,0:T(8,128)S(1)}, f32[8,32,512]{2,1,0:T(8,128)S(1)}, f32[8,32,512]{2,1,0:T(8,128)S(1)}, f32[8,32,512]{2,1,0:T(8,128)S(1)}...) custom-call(s32[8,32,512]{2,1,0:T(8,128)} %zone_hbm.3, ...), custom_call_target="tpu_custom_call" | custom-call | tf_op jit(solution)/shard_map/pallas_call | solution.py:525
  10.1 0.0 collective-permute-done.2.y_got
  10.2 0.0 collective-permute-done.3.y_got_too
  10.2 0.0 collective-permute-done.below_z
  10.2 0.0 collective-permute-done.1.above_z
  10.2 0.3 shard_map.123
  10.5 0.6 %collective-permute-start.4 = (f32[32,512]{1,0:T(8,128)S(1)}, f32[32,512]{1,0:T(8,128)S(1)}, u32[]{:S(2)}, u32[]{:S(2)}) collective-permute-start(f32[32,512]{1,0:T(8,128)S(1)} %get-tuple-element.55), channel_id=1, source_target_pairs={{0,8},{8,16},{16,24},{24,0},{1,9},{9,17},{17,25},{25,1},{2,10},{10... | collective-permute-start | bytes 196616 | tf_op jit(solution)/shard_map/ppermute | solution.py:514
  11.1 1.2 %collective-permute-start.5 = (f32[32,512]{1,0:T(8,128)S(1)}, f32[32,512]{1,0:T(8,128)S(1)}, u32[]{:S(2)}, u32[]{:S(2)}) collective-permute-start(f32[32,512]{1,0:T(8,128)S(1)} %get-tuple-element.56), channel_id=1, source_target_pairs={{0,24},{8,0},{16,8},{24,16},{1,25},{9,1},{17,9},{25,17},{2,26},{10... | collective-permute-start | bytes 196616 | tf_op jit(solution)/shard_map/ppermute | solution.py:514
  12.3 3.0 %collective-permute-start.6 = (f32[8,512]{1,0:T(8,128)S(1)}, f32[8,512]{1,0:T(8,128)S(1)}, u32[]{:S(2)}, u32[]{:S(2)}) collective-permute-start(f32[8,512]{1,0:T(8,128)S(1)} %get-tuple-element.57), channel_id=1, source_target_pairs={{0,1},{1,0},{2,3},{3,2},{4,5},{5,4},{6,7},{7,6},{8,9},{9,8},{10,11... | collective-permute-start | bytes 49160 | tf_op jit(solution)/shard_map/ppermute | solution.py:514
  15.3 0.0 collective-permute-start.7
  15.3 1.7 %collective-permute-done.6.y_got = f32[8,512]{1,0:T(8,128)S(1)} collective-permute-done((f32[8,512]{1,0:T(8,128)S(1)}, f32[8,512]{1,0:T(8,128)S(1)}, u32[]{:S(2)}, u32[]{:S(2)}) %collective-permute-start.6) | collective-permute-done | bytes 16416 | tf_op jit(solution)/shard_map/ppermute | solution.py:514
  17.1 0.0 collective-permute-done.7.y_got_too
  17.1 0.0 collective-permute-done.4.below_z
  17.1 0.0 collective-permute-done.5.above_z
  17.1 0.5 %shard_map.124 = (f32[8,32,512]{2,1,0:T(8,128)S(1)}, f32[8,32,512]{2,1,0:T(8,128)S(1)}, f32[32,512]{1,0:T(8,128)S(1)}, f32[32,512]{1,0:T(8,128)S(1)}, f32[8,512]{1,0:T(8,128)S(1)}, /*index=5*/f32[8,512]{1,0:T(8,128)S(1)}) custom-call(f32[8,32,512]{2,1,0:T(8,128)S(1)} %get-tuple-element.50.q_ref.refs_2_.refs_3_.q0, ...), custom_call_target="tpu_custom_call" | custom-call | tf_op jit(solution)/shard_map/pallas_call | solution.py:525
  17.6 0.1 collective-permute-start.8
  17.6 1.7 %collective-permute-start.9 = (f32[32,512]{1,0:T(8,128)S(1)}, f32[32,512]{1,0:T(8,128)S(1)}, u32[]{:S(2)}, u32[]{:S(2)}) collective-permute-start(f32[32,512]{1,0:T(8,128)S(1)} %get-tuple-element.61), channel_id=1, source_target_pairs={{0,24},{8,0},{16,8},{24,16},{1,25},{9,1},{17,9},{25,17},{2,26},{10... | collective-permute-start | bytes 196616 | tf_op jit(solution)/shard_map/ppermute | solution.py:514
  19.4 3.0 %collective-permute-start.10 = (f32[8,512]{1,0:T(8,128)S(1)}, f32[8,512]{1,0:T(8,128)S(1)}, u32[]{:S(2)}, u32[]{:S(2)}) collective-permute-start(f32[8,512]{1,0:T(8,128)S(1)} %get-tuple-element.62), channel_id=1, source_target_pairs={{0,1},{1,0},{2,3},{3,2},{4,5},{5,4},{6,7},{7,6},{8,9},{9,8},{10,11... | collective-permute-start | bytes 49160 | tf_op jit(solution)/shard_map/ppermute | solution.py:514
  22.4 0.0 collective-permute-start.11
  22.4 1.7 %collective-permute-done.10.y_got = f32[8,512]{1,0:T(8,128)S(1)} collective-permute-done((f32[8,512]{1,0:T(8,128)S(1)}, f32[8,512]{1,0:T(8,128)S(1)}, u32[]{:S(2)}, u32[]{:S(2)}) %collective-permute-start.10) | collective-permute-done | bytes 16416 | tf_op jit(solution)/shard_map/ppermute | solution.py:514
  24.1 0.0 collective-permute-done.11.y_got_too
  24.1 0.0 collective-permute-done.8.below_z
  24.1 0.0 collective-permute-done.9.above_z
  24.1 0.5 %shard_map.125 = (f32[8,32,512]{2,1,0:T(8,128)S(1)}, f32[8,32,512]{2,1,0:T(8,128)S(1)}, f32[32,512]{1,0:T(8,128)S(1)}, f32[32,512]{1,0:T(8,128)S(1)}, f32[8,512]{1,0:T(8,128)S(1)}, /*index=5*/f32[8,512]{1,0:T(8,128)S(1)}) custom-call(f32[8,32,512]{2,1,0:T(8,128)S(1)} %get-tuple-element.59.q_ref.refs_3_.refs_4_.q1, ...), custom_call_target="tpu_custom_call" | custom-call | tf_op jit(solution)/shard_map/pallas_call | solution.py:525
  24.6 0.1 collective-permute-start.12
  24.7 1.7 %collective-permute-start.13 = (f32[32,512]{1,0:T(8,128)S(1)}, f32[32,512]{1,0:T(8,128)S(1)}, u32[]{:S(2)}, u32[]{:S(2)}) collective-permute-start(f32[32,512]{1,0:T(8,128)S(1)} %get-tuple-element.69), channel_id=1, source_target_pairs={{0,24},{8,0},{16,8},{24,16},{1,25},{9,1},{17,9},{25,17},{2,26},{10... | collective-permute-start | bytes 196616 | tf_op jit(solution)/shard_map/ppermute | solution.py:514
  26.4 3.3 %collective-permute-start.14 = (f32[8,512]{1,0:T(8,128)S(1)}, f32[8,512]{1,0:T(8,128)S(1)}, u32[]{:S(2)}, u32[]{:S(2)}) collective-permute-start(f32[8,512]{1,0:T(8,128)S(1)} %get-tuple-element.70), channel_id=1, source_target_pairs={{0,1},{1,0},{2,3},{3,2},{4,5},{5,4},{6,7},{7,6},{8,9},{9,8},{10,11... | collective-permute-start | bytes 49160 | tf_op jit(solution)/shard_map/ppermute | solution.py:514
  29.7 0.0 collective-permute-start.15
  29.7 0.4 shard_map.126.early
  30.1 0.4 shard_map.127.middle
  30.5 0.9 %collective-permute-done.14.y_got = f32[8,512]{1,0:T(8,128)S(1)} collective-permute-done((f32[8,512]{1,0:T(8,128)S(1)}, f32[8,512]{1,0:T(8,128)S(1)}, u32[]{:S(2)}, u32[]{:S(2)}) %collective-permute-start.14) | collective-permute-done | bytes 16416 | tf_op jit(solution)/shard_map/ppermute | solution.py:514
  31.4 0.0 collective-permute-done.15.y_got_too
  31.4 0.0 collective-permute-done.12.below_z
  31.4 0.0 collective-permute-done.13.above_z
  31.4 0.8 %shard_map.128 = f32[32,128]{1,0:T(8,128)S(1)} custom-call(f32[8,32,512]{2,1,0:T(8,128)S(1)} %get-tuple-element.64.refs_5_.q2_ref.q2, f32[6,8,32,512]{3,2,1,0:T(8,128)S(1)} %get-tuple-element.51.faces, f32[2,32,512]{2,1,0:T(8,128)S(1)} %get-tuple-element.52.face_z, f32[2,8,512]{2,1,0:T(8,128)S(1)} %get-tuple-element.53.face_y, ...), custom_call_target="tpu_custom_call" | custom-call | tf_op jit(solution)/shard_map/pallas_call | solution.py:525
  32.2 15.3 %all_to_all.11 = f32[32,1,128]{2,1,0:T(1,128)S(1)} all-to-all(f32[32,1,128]{2,1,0:T(1,128)S(1)} %bitcast.5), channel_id=1, replica_groups=mesh['gz'=4,'gy'=8] {'gz','gy'}, dimensions={0} | all-to-all | bytes 32768 | tf_op jit(solution)/shard_map/all_to_all | solution.py:591
  47.5 1.3 %shard_map.129 = (f32[8,32,512]{2,1,0:T(8,128)}, f32[8,32,512]{2,1,0:T(8,128)}, f32[1,2]{1,0:T(1,128)}) custom-call(f32[32,128]{1,0:T(8,128)S(1)} %bitcast.6, f32[8,32,512]{2,1,0:T(8,128)S(1)} %get-tuple-element.50.q_ref.refs_2_.refs_3_.q0, f32[8,32,512]{2,1,0:T(8,128)S(1)} %get-tuple-element.59.q_ref.refs_3_.refs_4_.q1, ...), custom_call_target="tpu_custom_call" | custom-call | tf_op jit(solution)/shard_map/pallas_call | solution.py:525
Async XLA Ops:
  2.0 8.2 %collective-permute-start = (f32[2,32,512]{2,1,0:T(8,128)S(1)}, f32[2,32,512]{2,1,0:T(8,128)S(1)}, u32[]{:S(2)}, u32[]{:S(2)}) collective-permute-start(f32[2,32,512]{2,1,0:T(8,128)S(1)} %get-tuple-element.46), channel_id=1, source_target_pairs={{0,8},{8,16},{16,24},{24,0},{1,9},{9,17},{17,25},{25,1},{2,10},{10... | collective-permute-start | bytes 393224 | tf_op jit(solution)/shard_map/ppermute | solution.py:514
  2.5 7.7 %collective-permute-start.1 = (f32[2,32,512]{2,1,0:T(8,128)S(1)}, f32[2,32,512]{2,1,0:T(8,128)S(1)}, u32[]{:S(2)}, u32[]{:S(2)}) collective-permute-start(f32[2,32,512]{2,1,0:T(8,128)S(1)} %get-tuple-element.47), channel_id=1, source_target_pairs={{0,24},{8,0},{16,8},{24,16},{1,25},{9,1},{17,9},{25,17},{2,26},{10... | collective-permute-start | bytes 393224 | tf_op jit(solution)/shard_map/ppermute | solution.py:514
  4.5 5.7 %collective-permute-start.2 = (f32[2,8,512]{2,1,0:T(8,128)S(1)}, f32[2,8,512]{2,1,0:T(8,128)S(1)}, u32[]{:S(2)}, u32[]{:S(2)}) collective-permute-start(f32[2,8,512]{2,1,0:T(8,128)S(1)} %get-tuple-element.48), channel_id=1, source_target_pairs={{0,1},{1,0},{2,3},{3,2},{4,5},{5,4},{6,7},{7,6},{8,9},{9,8},{10,11... | collective-permute-start | bytes 98312 | tf_op jit(solution)/shard_map/ppermute | solution.py:514
  6.8 3.4 %collective-permute-start.3 = (f32[2,8,512]{2,1,0:T(8,128)S(1)}, f32[2,8,512]{2,1,0:T(8,128)S(1)}, u32[]{:S(2)}, u32[]{:S(2)}) collective-permute-start(f32[2,8,512]{2,1,0:T(8,128)S(1)} %get-tuple-element.49), channel_id=1, source_target_pairs={{0,8},{1,2},{2,1},{3,4},{4,3},{5,6},{6,5},{7,15},{8,0},{9,10},{10,... | collective-permute-start | bytes 98312 | tf_op jit(solution)/shard_map/ppermute | solution.py:514
  10.5 6.6 %collective-permute-start.4 = (f32[32,512]{1,0:T(8,128)S(1)}, f32[32,512]{1,0:T(8,128)S(1)}, u32[]{:S(2)}, u32[]{:S(2)}) collective-permute-start(f32[32,512]{1,0:T(8,128)S(1)} %get-tuple-element.55), channel_id=1, source_target_pairs={{0,8},{8,16},{16,24},{24,0},{1,9},{9,17},{17,25},{25,1},{2,10},{10... | collective-permute-start | bytes 196616 | tf_op jit(solution)/shard_map/ppermute | solution.py:514
  11.1 6.0 %collective-permute-start.5 = (f32[32,512]{1,0:T(8,128)S(1)}, f32[32,512]{1,0:T(8,128)S(1)}, u32[]{:S(2)}, u32[]{:S(2)}) collective-permute-start(f32[32,512]{1,0:T(8,128)S(1)} %get-tuple-element.56), channel_id=1, source_target_pairs={{0,24},{8,0},{16,8},{24,16},{1,25},{9,1},{17,9},{25,17},{2,26},{10... | collective-permute-start | bytes 196616 | tf_op jit(solution)/shard_map/ppermute | solution.py:514
  12.3 4.8 %collective-permute-start.6 = (f32[8,512]{1,0:T(8,128)S(1)}, f32[8,512]{1,0:T(8,128)S(1)}, u32[]{:S(2)}, u32[]{:S(2)}) collective-permute-start(f32[8,512]{1,0:T(8,128)S(1)} %get-tuple-element.57), channel_id=1, source_target_pairs={{0,1},{1,0},{2,3},{3,2},{4,5},{5,4},{6,7},{7,6},{8,9},{9,8},{10,11... | collective-permute-start | bytes 49160 | tf_op jit(solution)/shard_map/ppermute | solution.py:514
  15.3 1.7 %collective-permute-start.7 = (f32[8,512]{1,0:T(8,128)S(1)}, f32[8,512]{1,0:T(8,128)S(1)}, u32[]{:S(2)}, u32[]{:S(2)}) collective-permute-start(f32[8,512]{1,0:T(8,128)S(1)} %get-tuple-element.58), channel_id=1, source_target_pairs={{0,8},{1,2},{2,1},{3,4},{4,3},{5,6},{6,5},{7,15},{8,0},{9,10},{10,... | collective-permute-start | bytes 49160 | tf_op jit(solution)/shard_map/ppermute | solution.py:514
  17.6 6.6 %collective-permute-start.8 = (f32[32,512]{1,0:T(8,128)S(1)}, f32[32,512]{1,0:T(8,128)S(1)}, u32[]{:S(2)}, u32[]{:S(2)}) collective-permute-start(f32[32,512]{1,0:T(8,128)S(1)} %get-tuple-element.60), channel_id=1, source_target_pairs={{0,8},{8,16},{16,24},{24,0},{1,9},{9,17},{17,25},{25,1},{2,10},{10... | collective-permute-start | bytes 196616 | tf_op jit(solution)/shard_map/ppermute | solution.py:514
  17.6 6.5 %collective-permute-start.9 = (f32[32,512]{1,0:T(8,128)S(1)}, f32[32,512]{1,0:T(8,128)S(1)}, u32[]{:S(2)}, u32[]{:S(2)}) collective-permute-start(f32[32,512]{1,0:T(8,128)S(1)} %get-tuple-element.61), channel_id=1, source_target_pairs={{0,24},{8,0},{16,8},{24,16},{1,25},{9,1},{17,9},{25,17},{2,26},{10... | collective-permute-start | bytes 196616 | tf_op jit(solution)/shard_map/ppermute | solution.py:514
  19.4 4.7 %collective-permute-start.10 = (f32[8,512]{1,0:T(8,128)S(1)}, f32[8,512]{1,0:T(8,128)S(1)}, u32[]{:S(2)}, u32[]{:S(2)}) collective-permute-start(f32[8,512]{1,0:T(8,128)S(1)} %get-tuple-element.62), channel_id=1, source_target_pairs={{0,1},{1,0},{2,3},{3,2},{4,5},{5,4},{6,7},{7,6},{8,9},{9,8},{10,11... | collective-permute-start | bytes 49160 | tf_op jit(solution)/shard_map/ppermute | solution.py:514
  22.4 1.7 %collective-permute-start.11 = (f32[8,512]{1,0:T(8,128)S(1)}, f32[8,512]{1,0:T(8,128)S(1)}, u32[]{:S(2)}, u32[]{:S(2)}) collective-permute-start(f32[8,512]{1,0:T(8,128)S(1)} %get-tuple-element.63), channel_id=1, source_target_pairs={{0,8},{1,2},{2,1},{3,4},{4,3},{5,6},{6,5},{7,15},{8,0},{9,10},{10,... | collective-permute-start | bytes 49160 | tf_op jit(solution)/shard_map/ppermute | solution.py:514
  24.6 6.8 %collective-permute-start.12 = (f32[32,512]{1,0:T(8,128)S(1)}, f32[32,512]{1,0:T(8,128)S(1)}, u32[]{:S(2)}, u32[]{:S(2)}) collective-permute-start(f32[32,512]{1,0:T(8,128)S(1)} %get-tuple-element.68), channel_id=1, source_target_pairs={{0,8},{8,16},{16,24},{24,0},{1,9},{9,17},{17,25},{25,1},{2,10},{10... | collective-permute-start | bytes 196616 | tf_op jit(solution)/shard_map/ppermute | solution.py:514
  24.7 6.7 %collective-permute-start.13 = (f32[32,512]{1,0:T(8,128)S(1)}, f32[32,512]{1,0:T(8,128)S(1)}, u32[]{:S(2)}, u32[]{:S(2)}) collective-permute-start(f32[32,512]{1,0:T(8,128)S(1)} %get-tuple-element.69), channel_id=1, source_target_pairs={{0,24},{8,0},{16,8},{24,16},{1,25},{9,1},{17,9},{25,17},{2,26},{10... | collective-permute-start | bytes 196616 | tf_op jit(solution)/shard_map/ppermute | solution.py:514
  26.4 5.0 %collective-permute-start.14 = (f32[8,512]{1,0:T(8,128)S(1)}, f32[8,512]{1,0:T(8,128)S(1)}, u32[]{:S(2)}, u32[]{:S(2)}) collective-permute-start(f32[8,512]{1,0:T(8,128)S(1)} %get-tuple-element.70), channel_id=1, source_target_pairs={{0,1},{1,0},{2,3},{3,2},{4,5},{5,4},{6,7},{7,6},{8,9},{9,8},{10,11... | collective-permute-start | bytes 49160 | tf_op jit(solution)/shard_map/ppermute | solution.py:514
  29.7 1.7 %collective-permute-start.15 = (f32[8,512]{1,0:T(8,128)S(1)}, f32[8,512]{1,0:T(8,128)S(1)}, u32[]{:S(2)}, u32[]{:S(2)}) collective-permute-start(f32[8,512]{1,0:T(8,128)S(1)} %get-tuple-element.71), channel_id=1, source_target_pairs={{0,8},{1,2},{2,1},{3,4},{4,3},{5,6},{6,5},{7,15},{8,0},{9,10},{10,... | collective-permute-start | bytes 49160 | tf_op jit(solution)/shard_map/ppermute | solution.py:514

commit v4 on v3

--- a/solution.py
+++ b/solution.py
@@ -99,36 +99,6 @@
     return [pl.ds(at, ROWS) for at in range(0, rows, ROWS)]
 
 
-def pack_kernel(
-    zone_hbm, pressure_hbm, z_low, z_high, y_first, y_second, zone_z, zone_y, pressure_y, sems
-):
-    planes, rows, _ = zone_hbm.shape
-    ends = ((0, pl.ds(0, ROWS)), (planes - 1, pl.ds(rows - ROWS, ROWS)))
-    copies = []
-    for side, (plane, part) in enumerate(ends):
-        out = (z_low, z_high)[side]
-        for source, target in (
-            (zone_hbm.at[plane], zone_z.at[side]),
-            (pressure_hbm.at[plane], out.at[1]),
-            (zone_hbm.at[:, part], zone_y.at[side]),
-            (pressure_hbm.at[:, part], pressure_y.at[side]),
-        ):
-            copies.append(pltpu.make_async_copy(source, target, sems.at[len(copies)]))
-    for copy in copies:
-        copy.start()
-    for copy in copies:
-        copy.wait()
-    faces_y = []
-    for side, out in enumerate((z_low, z_high)):
-        out[0] = zone_z[side].astype(F32)
-        row = pl.ds((0, ROWS - 1)[side], 1)
-        zones = jnp.concatenate([zone_y[side, plane, row] for plane in range(planes)], axis=0)
-        values = jnp.concatenate([pressure_y[side, plane, row] for plane in range(planes)], axis=0)
-        faces_y.append((zones.astype(F32), values))
-    for number in range(2):
-        y_first[number], y_second[number] = to_send(faces_y[0][number], faces_y[1][number])
-
-
 NO_FACE = LANES - 1
 
 
@@ -143,51 +113,62 @@
     return jnp.where(known, harmonic(*sides), 0.0)
 
 
-def prepare_kernel(
-    zone_hbm, fixed_hbm, old_hbm, pressure_hbm, strain_hbm, source_hbm,
-    perm_hbm, storage_hbm, biot_hbm, bulk_hbm,
-    faces, diagonal_out, residual_out, free_out, ratio, pressure, strain, face_table, zone,
-    fixed, old, source, perm, storage_of, biot_of, term_z, perm_table, storage_table, biot_table, bulk_table, sems, half_sems,
-):
-    planes, rows, width = zone_hbm.shape
-    half = planes // 2
+def load_kernel(
+    zone_hbm, pressure_hbm, fixed_hbm, old_hbm, strain_hbm, source_hbm, perm_hbm, storage_hbm, biot_hbm, bulk_hbm,
+    zone, pressure, fixed, old, strain, source, perm, storage, biot, ratio, face_table,
+    z_low, z_high, y_first, y_second,
+    perm_table, storage_table, biot_table, bulk_table, sems,
+):
+    planes, rows, width = zone.shape
     pairs = (
-        (zone_hbm, zone), (perm_hbm, perm_table), (storage_hbm, storage_table), (biot_hbm, biot_table),
-        (bulk_hbm, bulk_table), (pressure_hbm, pressure),
+        (perm_hbm, perm_table), (storage_hbm, storage_table), (biot_hbm, biot_table), (bulk_hbm, bulk_table),
+        (zone_hbm, zone), (pressure_hbm, pressure),
+        (fixed_hbm, fixed), (old_hbm, old), (strain_hbm, strain), (source_hbm, source),
     )
     copies = [pltpu.make_async_copy(*pair, sems.at[number]) for number, pair in enumerate(pairs)]
-    halves = [
-        [
-            pltpu.make_async_copy(whole.at[part], kept.at[part], half_sems.at[at, number])
-            for number, (whole, kept) in enumerate(
-                ((fixed_hbm, fixed), (old_hbm, old), (strain_hbm, strain), (source_hbm, source))
-            )
-        ]
-        for at, part in enumerate((pl.ds(0, half), pl.ds(half, planes - half)))
-    ]
-    for copy in copies + halves[0] + halves[1]:
+    for copy in copies:
         copy.start()
-    for copy in copies[1:5]:
+    for copy in copies[:4]:
         copy.wait()
     zones = perm_table.shape[0]
     face_table[...] = face_row(table_row(perm_table), zones)
     entries = [[table[number] for number in range(zones)] for table in (perm_table, storage_table, biot_table)]
     one = jnp.ones((ROWS, width), F32)
     entries.append([entries[2][number] * one / (bulk_table[number] * one) for number in range(zones)])
+    copies[4].wait()
+
+    def fill(z, carry):
+        for part in row_parts(rows):
+            bits = zone_bits(zone[z, part], zones)
+            for out, entry in zip((perm, storage, biot, ratio), entries):
+                out[z, part] = pick(bits, entry)
+        return carry
+
+    lax.fori_loop(0, planes, fill, 0)
+    copies[5].wait()
+    faces_y = []
+    for side, out in enumerate((z_low, z_high)):
+        plane = (0, planes - 1)[side]
+        out[0] = zone[plane].astype(F32)
+        out[1] = pressure[plane]
+        row = pl.ds((0, rows - 1)[side], 1)
+        ids = jnp.concatenate([zone[z, row] for z in range(planes)], axis=0)
+        values = jnp.concatenate([pressure[z, row] for z in range(planes)], axis=0)
+        faces_y.append((ids.astype(F32), values))
+    for number in range(2):
+        y_first[number], y_second[number] = to_send(faces_y[0][number], faces_y[1][number])
+    for copy in copies[6:]:
+        copy.wait()
+
+
+def prepare_kernel(
+    pressure, fixed, old, strain, source, perm, storage_of, biot_of, ratio,
+    faces, diagonal_out, residual_out, free_out, term_z,
+):
+    planes, rows, width = pressure.shape
     lane = lax.broadcasted_iota(jnp.int32, (ROWS, width), 1)
     closed = jnp.zeros((ROWS, width), F32)
     parts = row_parts(rows)
-    copies[0].wait()
-
-    def fill(z, carry):
-        for part in parts:
-            bits = zone_bits(zone[z, part], zones)
-            for out, entry in zip((perm, storage_of, biot_of, ratio), entries):
-                out[z, part] = pick(bits, entry)
-        return carry
-
-    lax.fori_loop(0, planes, fill, 0)
-    copies[5].wait()
 
     def plane(z, low, high):
         perms = [perm[z, part] for part in parts]
@@ -222,16 +203,8 @@
             residual_out[z, part] = right_side - (diagonal * value - neighbours)
             free_out[z, part] = free
 
-    def middle(start, stop):
-        lax.fori_loop(start, stop, lambda z, c: (plane(z, z - 1, z + 1), c)[1], 0)
-
-    for copy in halves[0]:
-        copy.wait()
     plane(0, None, 1)
-    middle(1, half)
-    for copy in halves[1]:
-        copy.wait()
-    middle(half, planes - 1)
+    lax.fori_loop(1, planes - 1, lambda z, c: (plane(z, z - 1, z + 1), c)[1], 0)
     plane(planes - 1, planes - 2, None)
 
 
@@ -543,28 +516,23 @@
     cell_count = zone_ids.size * devices
     line = pltpu.VMEM((planes, width), F32)
 
-    packed = call(
-        pack_kernel, [(2, *side) for side in sides], [HBM] * 2, zone_ids, pressure_iter,
-        scratch=[
-            pltpu.VMEM((2, rows, width), jnp.int32), pltpu.VMEM((2, planes, ROWS, width), jnp.int32),
-            pltpu.VMEM((2, planes, ROWS, width), F32), pltpu.SemaphoreType.DMA((8,)),
-        ],
-    )
-    halo = exchange(*packed)
-    faces, diagonal, residual, free, ratio, pressure_kept, strain_kept, face_table, zone_kept = call(
-        prepare_kernel,
-        [(6, *field)] + [field] * 6 + [(ROWS, LANES), pltpu.VMEM(field, jnp.int32)], [HBM] * 10,
-        zone_ids, fixed_cells, pressure_old, pressure_iter, strain_change, source,
+    ints = pltpu.VMEM(field, jnp.int32)
+    zone, pressure, fixed, old, strain, source, perm, storage, biot, ratio, face_table, *edges = call(
+        load_kernel,
+        [ints, field, ints, *[field] * 7, (ROWS, LANES), *[(2, *side) for side in sides]], [HBM] * 10,
+        zone_ids, pressure_iter, fixed_cells, pressure_old, strain_change, source,
         zone_perm, zone_storage, zone_biot, zone_bulk,
-        scratch=[
-            pltpu.VMEM(field, jnp.int32), *[pltpu.VMEM(field, F32)] * 6, *[pltpu.SMEM(zone_perm.shape, F32)] * 4,
-            pltpu.SemaphoreType.DMA((6,)), pltpu.SemaphoreType.DMA((2, 4)),
-        ],
+        scratch=[*[pltpu.SMEM(zone_perm.shape, F32)] * 4, pltpu.SemaphoreType.DMA((10,))],
+    )
+    halo = exchange(*edges)
+    faces, diagonal, residual, free = call(
+        prepare_kernel, [(6, *field)] + [field] * 3, [VMEM] * 9,
+        pressure, fixed, old, strain, source, perm, storage, biot, ratio, scratch=[pltpu.VMEM(field, F32)],
     )
     inverse, q0, u0, face_z, face_y, *edges = call(
         functools.partial(begin_kernel, zone_perm.shape[0]),
         [field, field, field, (2, rows, width), (2, planes, width), *sides], [VMEM] * 10,
-        zone_kept, face_table, diagonal, residual, free, pressure_kept, *halo, scratch=[line, line],
+        zone, face_table, diagonal, residual, free, pressure, *halo, scratch=[line, line],
     )
     parts = (faces, face_z, face_y)
     halo = exchange(*edges)
@@ -589,16 +557,16 @@
         q2, *parts, u0, u1, u2, *halo, early, middle,
     )
     gathered = lax.all_to_all(sums, ("gz", "gy"), 0, 0, tiled=True)
-    pressure, strain_next, norms = call(
+    pressure_next, strain_next, norms = call(
         functools.partial(final_kernel, cell_count),
         [jax.ShapeDtypeStruct(shape, F32) for shape in (field, field, (1, 2))], [VMEM] * 7,
-        gathered, q0, q1, q2, pressure_kept, strain_kept, ratio, out_specs=[HBM] * 3,
+        gathered, q0, q1, q2, pressure, strain, ratio, out_specs=[HBM] * 3,
         scratch=[
             *[pltpu.VMEM(field, F32)] * 2, pltpu.VMEM((1, 2), F32), pltpu.SemaphoreType.DMA((2, planes)),
             pltpu.SemaphoreType.DMA,
         ],
     )
-    return pressure, strain_next, norms.reshape(2)
+    return pressure_next, strain_next, norms.reshape(2)
 
 
 def solution(mesh):

time: 49 us -> 49.1 us (level)
  starting transfers between devices: 19.5 us -> 21.1 us
  Pallas kernels: 8.84 us -> 7.24 us
    pallas_call x9, Pallas kernels: 8.84 us -> 7.24 us  [call(): pl.pallas_call(kernel, out_shape=results[0] if single else results, in_sp...]
    ppermute x16, starting transfers between devices: 19.5 us -> 21.1 us  [exchange(): got[name] = lax.ppermute(field, axis, pairs)]
  transfers between devices with their start and end apart: 16 -> 16, of which waited for: 3 -> 4; matrix products, arithmetic and copies ran while one was open for 0% -> 0% of each run, Pallas kernels for 9% -> 5%
where the time goes in v4:
time: 49.1 us; the launch traced here: 48.9 us
  starting transfers between devices  21.1 us (43%)
  blocking collectives  15.1 us (31%)
  Pallas kernels  7.24 us (15%)
  waiting for transfers between devices  4.78 us (10%)
  between operations  0.74 us (2%)
    ppermute x16, starting transfers between devices, exchange(): got[name] = lax.ppermute(field, axis, pairs)  21.1 us
    all_to_all x1, blocking collectives, per_device(): gathered = lax.all_to_all(sums, ('gz', 'gy'), 0, 0, tiled=True)  15.1 us
    pallas_call x9, Pallas kernels, call(): pl.pallas_call(kernel, out_shape=results[0] if single else results, in_sp...  7.24 us
    ppermute x16, waiting for transfers between devices, exchange(): got[name] = lax.ppermute(field, axis, pairs)  4.78 us
  transfers between devices with their start and end apart: 16, of which 4 were waited for; matrix products, arithmetic and copies ran while one was open for 0% of the time, Pallas kernels for 5%

profile of v4, /device:TPU:0, one launch (start us, length us, event | category | flops | bytes accessed | tf_op | source)
XLA Modules:
  0.0 48.9 jit_solution(1197341244170959909)
XLA Ops:
  0.6 1.9 %shard_map.121 = (s32[8,32,512]{2,1,0:T(8,128)S(1)}, f32[8,32,512]{2,1,0:T(8,128)S(1)}, s32[8,32,512]{2,1,0:T(8,128)S(1)}, f32[8,32,512]{2,1,0:T(8,128)S(1)}, f3...) custom-call(s32[8,32,512]{2,1,0:T(8,128)} %zone_hbm.1, ...), custom_call_target="tpu_custom_call" | custom-call | tf_op jit(solution)/shard_map/pallas_call | solution.py:498
  2.6 0.5 %collective-permute-start = (f32[2,32,512]{2,1,0:T(8,128)S(1)}, f32[2,32,512]{2,1,0:T(8,128)S(1)}, u32[]{:S(2)}, u32[]{:S(2)}) collective-permute-start(f32[2,32,512]{2,1,0:T(8,128)S(1)} %get-tuple-element.60), channel_id=1, source_target_pairs={{0,8},{8,16},{16,24},{24,0},{1,9},{9,17},{17,25},{25,1},{2,10},{10... | collective-permute-start | bytes 393224 | tf_op jit(solution)/shard_map/ppermute | solution.py:487
  3.1 2.0 %collective-permute-start.1 = (f32[2,32,512]{2,1,0:T(8,128)S(1)}, f32[2,32,512]{2,1,0:T(8,128)S(1)}, u32[]{:S(2)}, u32[]{:S(2)}) collective-permute-start(f32[2,32,512]{2,1,0:T(8,128)S(1)} %get-tuple-element.61), channel_id=1, source_target_pairs={{0,24},{8,0},{16,8},{24,16},{1,25},{9,1},{17,9},{25,17},{2,26},{10... | collective-permute-start | bytes 393224 | tf_op jit(solution)/shard_map/ppermute | solution.py:487
  5.1 2.3 %collective-permute-start.2 = (f32[2,8,512]{2,1,0:T(8,128)S(1)}, f32[2,8,512]{2,1,0:T(8,128)S(1)}, u32[]{:S(2)}, u32[]{:S(2)}) collective-permute-start(f32[2,8,512]{2,1,0:T(8,128)S(1)} %get-tuple-element.62), channel_id=1, source_target_pairs={{0,1},{1,0},{2,3},{3,2},{4,5},{5,4},{6,7},{7,6},{8,9},{9,8},{10,11... | collective-permute-start | bytes 98312 | tf_op jit(solution)/shard_map/ppermute | solution.py:487
  7.4 0.0 collective-permute-start.3
  7.4 1.5 %shard_map.122 = (f32[6,8,32,512]{3,2,1,0:T(8,128)S(1)}, f32[8,32,512]{2,1,0:T(8,128)S(1)}, f32[8,32,512]{2,1,0:T(8,128)S(1)}, f32[8,32,512]{2,1,0:T(8,128)S(1)}) custom-call(f32[8,32,512]{2,1,0:T(8,128)S(1)} %get-tuple-element.48.pressure.pressure_ref, s32[8,32,512]{2,1,0:T(8,128)S(1)} %get-tuple-element.49.fixed, f32[8,32,512]{2,1,0:T(8,128)S(1)} %get-tuple-element.50.old, ...), custom_call_target="tpu_custom_call" | custom-call | tf_op jit(solution)/shard_map/pallas_call | solution.py:498
  8.9 0.4 collective-permute-done.2.y_got
  9.3 0.0 collective-permute-done.3.y_got_too
  9.3 0.0 collective-permute-done.below_z
  9.3 0.0 collective-permute-done.1.above_z
  9.3 0.3 shard_map.123
  9.6 0.9 %collective-permute-start.4 = (f32[32,512]{1,0:T(8,128)S(1)}, f32[32,512]{1,0:T(8,128)S(1)}, u32[]{:S(2)}, u32[]{:S(2)}) collective-permute-start(f32[32,512]{1,0:T(8,128)S(1)} %get-tuple-element.69), channel_id=1, source_target_pairs={{0,8},{8,16},{16,24},{24,0},{1,9},{9,17},{17,25},{25,1},{2,10},{10... | collective-permute-start | bytes 196616 | tf_op jit(solution)/shard_map/ppermute | solution.py:487
  10.4 1.0 %collective-permute-start.5 = (f32[32,512]{1,0:T(8,128)S(1)}, f32[32,512]{1,0:T(8,128)S(1)}, u32[]{:S(2)}, u32[]{:S(2)}) collective-permute-start(f32[32,512]{1,0:T(8,128)S(1)} %get-tuple-element.70), channel_id=1, source_target_pairs={{0,24},{8,0},{16,8},{24,16},{1,25},{9,1},{17,9},{25,17},{2,26},{10... | collective-permute-start | bytes 196616 | tf_op jit(solution)/shard_map/ppermute | solution.py:487
  11.4 3.0 %collective-permute-start.6 = (f32[8,512]{1,0:T(8,128)S(1)}, f32[8,512]{1,0:T(8,128)S(1)}, u32[]{:S(2)}, u32[]{:S(2)}) collective-permute-start(f32[8,512]{1,0:T(8,128)S(1)} %get-tuple-element.71), channel_id=1, source_target_pairs={{0,1},{1,0},{2,3},{3,2},{4,5},{5,4},{6,7},{7,6},{8,9},{9,8},{10,11... | collective-permute-start | bytes 49160 | tf_op jit(solution)/shard_map/ppermute | solution.py:487
  14.4 0.0 collective-permute-start.7
  14.4 1.7 %collective-permute-done.6.y_got = f32[8,512]{1,0:T(8,128)S(1)} collective-permute-done((f32[8,512]{1,0:T(8,128)S(1)}, f32[8,512]{1,0:T(8,128)S(1)}, u32[]{:S(2)}, u32[]{:S(2)}) %collective-permute-start.6) | collective-permute-done | bytes 16416 | tf_op jit(solution)/shard_map/ppermute | solution.py:487
  16.1 0.0 collective-permute-done.7.y_got_too
  16.1 0.0 collective-permute-done.4.below_z
  16.1 0.0 collective-permute-done.5.above_z
  16.1 0.4 shard_map.124
  16.5 0.1 collective-permute-start.8
  16.6 1.7 %collective-permute-start.9 = (f32[32,512]{1,0:T(8,128)S(1)}, f32[32,512]{1,0:T(8,128)S(1)}, u32[]{:S(2)}, u32[]{:S(2)}) collective-permute-start(f32[32,512]{1,0:T(8,128)S(1)} %get-tuple-element.75), channel_id=1, source_target_pairs={{0,24},{8,0},{16,8},{24,16},{1,25},{9,1},{17,9},{25,17},{2,26},{10... | collective-permute-start | bytes 196616 | tf_op jit(solution)/shard_map/ppermute | solution.py:487
  18.3 3.4 %collective-permute-start.10 = (f32[8,512]{1,0:T(8,128)S(1)}, f32[8,512]{1,0:T(8,128)S(1)}, u32[]{:S(2)}, u32[]{:S(2)}) collective-permute-start(f32[8,512]{1,0:T(8,128)S(1)} %get-tuple-element.76), channel_id=1, source_target_pairs={{0,1},{1,0},{2,3},{3,2},{4,5},{5,4},{6,7},{7,6},{8,9},{9,8},{10,11... | collective-permute-start | bytes 49160 | tf_op jit(solution)/shard_map/ppermute | solution.py:487
  21.8 0.0 collective-permute-start.11
  21.8 1.7 %collective-permute-done.10.y_got = f32[8,512]{1,0:T(8,128)S(1)} collective-permute-done((f32[8,512]{1,0:T(8,128)S(1)}, f32[8,512]{1,0:T(8,128)S(1)}, u32[]{:S(2)}, u32[]{:S(2)}) %collective-permute-start.10) | collective-permute-done | bytes 16416 | tf_op jit(solution)/shard_map/ppermute | solution.py:487
  23.5 0.0 collective-permute-done.11.y_got_too
  23.5 0.0 collective-permute-done.8.below_z
  23.5 0.0 collective-permute-done.9.above_z
  23.5 0.4 shard_map.125
  23.9 0.1 collective-permute-start.12
  24.0 1.7 %collective-permute-start.13 = (f32[32,512]{1,0:T(8,128)S(1)}, f32[32,512]{1,0:T(8,128)S(1)}, u32[]{:S(2)}, u32[]{:S(2)}) collective-permute-start(f32[32,512]{1,0:T(8,128)S(1)} %get-tuple-element.83), channel_id=1, source_target_pairs={{0,24},{8,0},{16,8},{24,16},{1,25},{9,1},{17,9},{25,17},{2,26},{10... | collective-permute-start | bytes 196616 | tf_op jit(solution)/shard_map/ppermute | solution.py:487
  25.7 4.4 %collective-permute-start.14 = (f32[8,512]{1,0:T(8,128)S(1)}, f32[8,512]{1,0:T(8,128)S(1)}, u32[]{:S(2)}, u32[]{:S(2)}) collective-permute-start(f32[8,512]{1,0:T(8,128)S(1)} %get-tuple-element.84), channel_id=1, source_target_pairs={{0,1},{1,0},{2,3},{3,2},{4,5},{5,4},{6,7},{7,6},{8,9},{9,8},{10,11... | collective-permute-start | bytes 49160 | tf_op jit(solution)/shard_map/ppermute | solution.py:487
  30.1 0.0 collective-permute-start.15
  30.1 0.4 shard_map.126.early
  30.5 0.4 shard_map.127.middle
  30.9 0.9 %collective-permute-done.14.y_got = f32[8,512]{1,0:T(8,128)S(1)} collective-permute-done((f32[8,512]{1,0:T(8,128)S(1)}, f32[8,512]{1,0:T(8,128)S(1)}, u32[]{:S(2)}, u32[]{:S(2)}) %collective-permute-start.14) | collective-permute-done | bytes 16416 | tf_op jit(solution)/shard_map/ppermute | solution.py:487
  31.9 0.0 collective-permute-done.15.y_got_too
  31.9 0.0 collective-permute-done.12.below_z
  31.9 0.0 collective-permute-done.13.above_z
  31.9 0.7 %shard_map.128 = f32[32,128]{1,0:T(8,128)S(1)} custom-call(f32[8,32,512]{2,1,0:T(8,128)S(1)} %get-tuple-element.78.refs_5_.q2_ref.q2, f32[6,8,32,512]{3,2,1,0:T(8,128)S(1)} %get-tuple-element.65.faces, f32[2,32,512]{2,1,0:T(8,128)S(1)} %get-tuple-element.66.face_z, f32[2,8,512]{2,1,0:T(8,128)S(1)} %get-tuple-element.67.face_y, ...), custom_call_target="tpu_custom_call" | custom-call | tf_op jit(solution)/shard_map/pallas_call | solution.py:498
  32.5 15.1 %all_to_all.11 = f32[32,1,128]{2,1,0:T(1,128)S(1)} all-to-all(f32[32,1,128]{2,1,0:T(1,128)S(1)} %bitcast.5), channel_id=1, replica_groups=mesh['gz'=4,'gy'=8] {'gz','gy'}, dimensions={0} | all-to-all | bytes 32768 | tf_op jit(solution)/shard_map/all_to_all | solution.py:559
  47.6 1.3 %shard_map.129 = (f32[8,32,512]{2,1,0:T(8,128)}, f32[8,32,512]{2,1,0:T(8,128)}, f32[1,2]{1,0:T(1,128)}) custom-call(f32[32,128]{1,0:T(8,128)S(1)} %bitcast.6, f32[8,32,512]{2,1,0:T(8,128)S(1)} %get-tuple-element.64.q_ref.refs_2_.refs_3_.q0, f32[8,32,512]{2,1,0:T(8,128)S(1)} %get-tuple-element.73.q_ref.refs_3_.refs_4_.q1, ...), custom_call_target="tpu_custom_call" | custom-call | tf_op jit(solution)/shard_map/pallas_call | solution.py:498
Async XLA Ops:
  2.6 6.7 %collective-permute-start = (f32[2,32,512]{2,1,0:T(8,128)S(1)}, f32[2,32,512]{2,1,0:T(8,128)S(1)}, u32[]{:S(2)}, u32[]{:S(2)}) collective-permute-start(f32[2,32,512]{2,1,0:T(8,128)S(1)} %get-tuple-element.60), channel_id=1, source_target_pairs={{0,8},{8,16},{16,24},{24,0},{1,9},{9,17},{17,25},{25,1},{2,10},{10... | collective-permute-start | bytes 393224 | tf_op jit(solution)/shard_map/ppermute | solution.py:487
  3.1 6.2 %collective-permute-start.1 = (f32[2,32,512]{2,1,0:T(8,128)S(1)}, f32[2,32,512]{2,1,0:T(8,128)S(1)}, u32[]{:S(2)}, u32[]{:S(2)}) collective-permute-start(f32[2,32,512]{2,1,0:T(8,128)S(1)} %get-tuple-element.61), channel_id=1, source_target_pairs={{0,24},{8,0},{16,8},{24,16},{1,25},{9,1},{17,9},{25,17},{2,26},{10... | collective-permute-start | bytes 393224 | tf_op jit(solution)/shard_map/ppermute | solution.py:487
  5.1 4.2 %collective-permute-start.2 = (f32[2,8,512]{2,1,0:T(8,128)S(1)}, f32[2,8,512]{2,1,0:T(8,128)S(1)}, u32[]{:S(2)}, u32[]{:S(2)}) collective-permute-start(f32[2,8,512]{2,1,0:T(8,128)S(1)} %get-tuple-element.62), channel_id=1, source_target_pairs={{0,1},{1,0},{2,3},{3,2},{4,5},{5,4},{6,7},{7,6},{8,9},{9,8},{10,11... | collective-permute-start | bytes 98312 | tf_op jit(solution)/shard_map/ppermute | solution.py:487
  7.4 1.9 %collective-permute-start.3 = (f32[2,8,512]{2,1,0:T(8,128)S(1)}, f32[2,8,512]{2,1,0:T(8,128)S(1)}, u32[]{:S(2)}, u32[]{:S(2)}) collective-permute-start(f32[2,8,512]{2,1,0:T(8,128)S(1)} %get-tuple-element.63), channel_id=1, source_target_pairs={{0,8},{1,2},{2,1},{3,4},{4,3},{5,6},{6,5},{7,15},{8,0},{9,10},{10,... | collective-permute-start | bytes 98312 | tf_op jit(solution)/shard_map/ppermute | solution.py:487
  9.6 6.5 %collective-permute-start.4 = (f32[32,512]{1,0:T(8,128)S(1)}, f32[32,512]{1,0:T(8,128)S(1)}, u32[]{:S(2)}, u32[]{:S(2)}) collective-permute-start(f32[32,512]{1,0:T(8,128)S(1)} %get-tuple-element.69), channel_id=1, source_target_pairs={{0,8},{8,16},{16,24},{24,0},{1,9},{9,17},{17,25},{25,1},{2,10},{10... | collective-permute-start | bytes 196616 | tf_op jit(solution)/shard_map/ppermute | solution.py:487
  10.4 5.7 %collective-permute-start.5 = (f32[32,512]{1,0:T(8,128)S(1)}, f32[32,512]{1,0:T(8,128)S(1)}, u32[]{:S(2)}, u32[]{:S(2)}) collective-permute-start(f32[32,512]{1,0:T(8,128)S(1)} %get-tuple-element.70), channel_id=1, source_target_pairs={{0,24},{8,0},{16,8},{24,16},{1,25},{9,1},{17,9},{25,17},{2,26},{10... | collective-permute-start | bytes 196616 | tf_op jit(solution)/shard_map/ppermute | solution.py:487
  11.4 4.7 %collective-permute-start.6 = (f32[8,512]{1,0:T(8,128)S(1)}, f32[8,512]{1,0:T(8,128)S(1)}, u32[]{:S(2)}, u32[]{:S(2)}) collective-permute-start(f32[8,512]{1,0:T(8,128)S(1)} %get-tuple-element.71), channel_id=1, source_target_pairs={{0,1},{1,0},{2,3},{3,2},{4,5},{5,4},{6,7},{7,6},{8,9},{9,8},{10,11... | collective-permute-start | bytes 49160 | tf_op jit(solution)/shard_map/ppermute | solution.py:487
  14.4 1.7 %collective-permute-start.7 = (f32[8,512]{1,0:T(8,128)S(1)}, f32[8,512]{1,0:T(8,128)S(1)}, u32[]{:S(2)}, u32[]{:S(2)}) collective-permute-start(f32[8,512]{1,0:T(8,128)S(1)} %get-tuple-element.72), channel_id=1, source_target_pairs={{0,8},{1,2},{2,1},{3,4},{4,3},{5,6},{6,5},{7,15},{8,0},{9,10},{10,... | collective-permute-start | bytes 49160 | tf_op jit(solution)/shard_map/ppermute | solution.py:487
  16.5 6.9 %collective-permute-start.8 = (f32[32,512]{1,0:T(8,128)S(1)}, f32[32,512]{1,0:T(8,128)S(1)}, u32[]{:S(2)}, u32[]{:S(2)}) collective-permute-start(f32[32,512]{1,0:T(8,128)S(1)} %get-tuple-element.74), channel_id=1, source_target_pairs={{0,8},{8,16},{16,24},{24,0},{1,9},{9,17},{17,25},{25,1},{2,10},{10... | collective-permute-start | bytes 196616 | tf_op jit(solution)/shard_map/ppermute | solution.py:487
  16.6 6.9 %collective-permute-start.9 = (f32[32,512]{1,0:T(8,128)S(1)}, f32[32,512]{1,0:T(8,128)S(1)}, u32[]{:S(2)}, u32[]{:S(2)}) collective-permute-start(f32[32,512]{1,0:T(8,128)S(1)} %get-tuple-element.75), channel_id=1, source_target_pairs={{0,24},{8,0},{16,8},{24,16},{1,25},{9,1},{17,9},{25,17},{2,26},{10... | collective-permute-start | bytes 196616 | tf_op jit(solution)/shard_map/ppermute | solution.py:487
  18.3 5.1 %collective-permute-start.10 = (f32[8,512]{1,0:T(8,128)S(1)}, f32[8,512]{1,0:T(8,128)S(1)}, u32[]{:S(2)}, u32[]{:S(2)}) collective-permute-start(f32[8,512]{1,0:T(8,128)S(1)} %get-tuple-element.76), channel_id=1, source_target_pairs={{0,1},{1,0},{2,3},{3,2},{4,5},{5,4},{6,7},{7,6},{8,9},{9,8},{10,11... | collective-permute-start | bytes 49160 | tf_op jit(solution)/shard_map/ppermute | solution.py:487
  21.8 1.7 %collective-permute-start.11 = (f32[8,512]{1,0:T(8,128)S(1)}, f32[8,512]{1,0:T(8,128)S(1)}, u32[]{:S(2)}, u32[]{:S(2)}) collective-permute-start(f32[8,512]{1,0:T(8,128)S(1)} %get-tuple-element.77), channel_id=1, source_target_pairs={{0,8},{1,2},{2,1},{3,4},{4,3},{5,6},{6,5},{7,15},{8,0},{9,10},{10,... | collective-permute-start | bytes 49160 | tf_op jit(solution)/shard_map/ppermute | solution.py:487
  23.9 8.0 %collective-permute-start.12 = (f32[32,512]{1,0:T(8,128)S(1)}, f32[32,512]{1,0:T(8,128)S(1)}, u32[]{:S(2)}, u32[]{:S(2)}) collective-permute-start(f32[32,512]{1,0:T(8,128)S(1)} %get-tuple-element.82), channel_id=1, source_target_pairs={{0,8},{8,16},{16,24},{24,0},{1,9},{9,17},{17,25},{25,1},{2,10},{10... | collective-permute-start | bytes 196616 | tf_op jit(solution)/shard_map/ppermute | solution.py:487
  24.0 7.9 %collective-permute-start.13 = (f32[32,512]{1,0:T(8,128)S(1)}, f32[32,512]{1,0:T(8,128)S(1)}, u32[]{:S(2)}, u32[]{:S(2)}) collective-permute-start(f32[32,512]{1,0:T(8,128)S(1)} %get-tuple-element.83), channel_id=1, source_target_pairs={{0,24},{8,0},{16,8},{24,16},{1,25},{9,1},{17,9},{25,17},{2,26},{10... | collective-permute-start | bytes 196616 | tf_op jit(solution)/shard_map/ppermute | solution.py:487
  25.7 6.1 %collective-permute-start.14 = (f32[8,512]{1,0:T(8,128)S(1)}, f32[8,512]{1,0:T(8,128)S(1)}, u32[]{:S(2)}, u32[]{:S(2)}) collective-permute-start(f32[8,512]{1,0:T(8,128)S(1)} %get-tuple-element.84), channel_id=1, source_target_pairs={{0,1},{1,0},{2,3},{3,2},{4,5},{5,4},{6,7},{7,6},{8,9},{9,8},{10,11... | collective-permute-start | bytes 49160 | tf_op jit(solution)/shard_map/ppermute | solution.py:487
  30.1 1.7 %collective-permute-start.15 = (f32[8,512]{1,0:T(8,128)S(1)}, f32[8,512]{1,0:T(8,128)S(1)}, u32[]{:S(2)}, u32[]{:S(2)}) collective-permute-start(f32[8,512]{1,0:T(8,128)S(1)} %get-tuple-element.85), channel_id=1, source_target_pairs={{0,8},{1,2},{2,1},{3,4},{4,3},{5,6},{6,5},{7,15},{8,0},{9,10},{10,... | collective-permute-start | bytes 49160 | tf_op jit(solution)/shard_map/ppermute | solution.py:487
